TPU v7x, 32 devices: a whole 2x2x4 slice. The times are simulated.
32 devices in a mesh: dp: 8 (over y, x, core), mp: 4 (over z).
Axes of the slice: x: 2, y: 2, z: 4, core: 2. Of those that a mesh axis runs over, the one named last changes fastest.
Arguments:
- candidates: bfloat16 [64, 256, 768], P('dp', 'mp'), may hold values from -6 to 6
- owner_row: int32 [64], replicated, may hold values from 0 to 63, as said below
- selected: int32 [16], replicated, may hold values from 0 to 63, as said below
- dest_slot: int32 [16], replicated, may hold values from 0 to 15, as said below
- patch_weight: bfloat16 [768, 768], P(None, 'mp'), may hold values from -0.21875 to 0.21875
- positions: bfloat16 [256, 768], P(None, 'mp'), may hold values from -3 to 3
- qkv_weight: bfloat16 [768, 3, 768], P(None, None, 'mp'), may hold values from -1 to 1
- out_weight: bfloat16 [768, 768], P('mp'), may hold values from -0.21875 to 0.21875
- attn_gain: bfloat16 [768], replicated, may hold values from 0.099609375 to 1.8984375
- mlp_gain: bfloat16 [768], replicated, may hold values from 0.099609375 to 1.8984375
- up_weight: bfloat16 [768, 3072], P(None, 'mp'), may hold values from -0.21875 to 0.21875
- down_weight: bfloat16 [3072, 768], P('mp'), may hold values from -0.109375 to 0.109375
Outputs:
- layer_out: bfloat16 [16, 256, 768], P('dp', 'mp')
Inputs may be any that keep to these rules, and one draw needn't show every extreme that they name: `owner_row`: a permutation; storage row r sits on index r // 8 of dp. `selected`: distinct candidates; no index of dp stores more than 4 of them, and some index stores exactly 4. `dest_slot`: a permutation; the 2 slots s with equal s // 2 get candidates stored on different indices of dp.
All inputs are finite; a program needn't handle non-finite values.
Results may differ from a plain program's by a relative error of at most 0.012.
Values may be sent and summed in bfloat16 or wider, within the bound.
No kernel may reach another device: no remote copies, remote signals or barrier semaphores. Data moves between devices by JAX's collectives and lax.ppermute only.
A program may use at most 128 MiB of HBM per device.

v0:
```python
import jax
import jax.numpy as jnp
from jax import lax
from jax.sharding import PartitionSpec as P

PATCHES = 256
CAND_DEV = 8
SEL_DEV = 2
HEAD_DIM = 64


def norm_rows(values, gain):
    average = jnp.mean(values, axis=-1, keepdims=True)
    centred = values - average
    variance = jnp.mean(centred * centred, axis=-1, keepdims=True)
    return centred * lax.rsqrt(variance + 1e-06) * gain.astype(jnp.float32)


def local(
    candidates,
    owner_row,
    selected,
    dest_slot,
    patch_weight,
    positions,
    qkv_weight,
    out_weight,
    attn_gain,
    mlp_gain,
    up_weight,
    down_weight,
):
    learners = lax.axis_size("dp")
    own_index = lax.axis_index("dp")
    quarter = candidates.shape[1]
    pixel_width = candidates.shape[2]
    chosen_rows = jnp.take(owner_row, selected)
    slot_rows = jnp.zeros(dest_slot.shape, jnp.int32).at[dest_slot].set(chosen_rows)
    source_owner = slot_rows // CAND_DEV
    local_row = slot_rows % CAND_DEV
    stored = candidates.reshape(CAND_DEV, quarter * pixel_width)
    mine = (source_owner == own_index).reshape(learners, SEL_DEV)
    picked = jnp.sum(jnp.where(mine, local_row.reshape(learners, SEL_DEV), 0), axis=1)
    outgoing = jnp.take(stored, picked, axis=0)
    incoming = lax.all_to_all(outgoing, "dp", split_axis=0, concat_axis=0, tiled=True)
    senders = lax.dynamic_slice_in_dim(source_owner, own_index * SEL_DEV, SEL_DEV)
    arrived = jnp.take(incoming, senders, axis=0)
    own_pixels = arrived.reshape(SEL_DEV, quarter, pixel_width)
    product = jnp.einsum(
        "brp,pe->bre",
        lax.all_gather(own_pixels, "mp", axis=1, tiled=True),
        patch_weight,
        preferred_element_type=jnp.float32,
    )
    embedded = (product + positions.astype(jnp.float32)[None]).astype(jnp.bfloat16)
    activations = lax.all_gather(embedded, "mp", axis=2, tiled=True).astype(jnp.float32)
    normed = norm_rows(activations, attn_gain).astype(jnp.bfloat16)
    projected = jnp.einsum(
        "btd,dce->btce", normed, qkv_weight, preferred_element_type=jnp.float32
    ).astype(jnp.bfloat16)
    local_heads = qkv_weight.shape[2] // HEAD_DIM
    head_split = projected.reshape(SEL_DEV, PATCHES, 3, local_heads, HEAD_DIM)
    queries = head_split[:, :, 0]
    attn_keys = head_split[:, :, 1]
    attn_values = head_split[:, :, 2]
    scores = jnp.einsum(
        "bqhd,bkhd->bhqk", queries, attn_keys, preferred_element_type=jnp.float32
    ) * HEAD_DIM ** (-0.5)
    attn_probs = jax.nn.softmax(scores, axis=-1).astype(jnp.bfloat16)
    context = jnp.einsum(
        "bhqk,bkhd->bqhd", attn_probs, attn_values, preferred_element_type=jnp.float32
    ).astype(jnp.bfloat16)
    context = context.reshape(SEL_DEV, PATCHES, local_heads * HEAD_DIM)
    partial_out = jnp.einsum("bte,ed->btd", context, out_weight, preferred_element_type=jnp.float32)
    attended = lax.psum(partial_out.astype(jnp.bfloat16), "mp").astype(jnp.float32)
    after_attn = activations + attended
    normed2 = norm_rows(after_attn, mlp_gain).astype(jnp.bfloat16)
    hidden = jax.nn.gelu(
        jnp.einsum("btd,df->btf", normed2, up_weight, preferred_element_type=jnp.float32),
        approximate=False,
    ).astype(jnp.bfloat16)
    down_terms = jnp.einsum("btf,fd->btd", hidden, down_weight, preferred_element_type=jnp.float32)
    summed = lax.psum_scatter(
        down_terms.astype(jnp.bfloat16), "mp", scatter_dimension=1, tiled=True
    ).astype(jnp.float32)
    residual = lax.dynamic_slice_in_dim(after_attn, lax.axis_index("mp") * quarter, quarter, 1)
    return (residual + summed).astype(jnp.bfloat16)


def solution(mesh):
    return jax.shard_map(
        local,
        mesh=mesh,
        in_specs=(
            P("dp", "mp", None),
            P(),
            P(),
            P(),
            P(None, "mp"),
            P(None, "mp"),
            P(None, None, "mp"),
            P("mp", None),
            P(),
            P(),
            P(None, "mp"),
            P("mp", None),
        ),
        out_specs=P("dp", "mp", None),
        check_vma=False,
    )
```

profile of v0, /device:TPU:0, one launch (start us, length us, event | category | flops | bytes accessed | tf_op | source)
XLA Modules:
  0.0 183.8 jit_solution(13271876456663978697)
XLA Ops:
  6.5 0.0 copy-start
  6.5 0.8 compare_select_fusion.3
  7.3 1.3 gather_fusion
  8.6 0.7 compare_select_fusion.4
  9.3 0.6 scatter_custom_fusion
  9.9 0.1 select_n.81
  10.0 0.1 reduce_sum.56
  10.2 1.6 copy.77
  11.8 1.1 gather_fusion.1
  12.8 0.1 bitcast_select_fusion
  13.0 0.5 broadcast.218
  13.5 1.2 reduce.4
  14.7 0.0 copy-start.5
  14.7 0.0 copy-start.6
  14.7 1.5 reshape.149
  16.2 5.2 %all-to-all-start = ((bf16[8,2,24576]{2,1,0:T(2,128)(2,1)}), bf16[8,2,24576]{2,1,0:T(2,128)(2,1)S(1)}, u32[]{:S(2)}, u32[]{:S(2)}) async-start(bf16[8,2,24576]{2,1,0:T(2,128)(2,1)} %reshape.149), calls=%async_computation | async-start | bytes 1572864 | tf_op jit(solution)/shard_map/all_to_all | solution.py:45
  21.4 0.0 all-reduce.4.cloned.1.call-start
  21.5 0.0 copy-done.5
  21.5 0.7 convert_element_type.51
  22.2 0.0 copy-done.6
  22.2 0.1 compare_and_fusion.1
  22.3 11.7 %all-to-all-done = bf16[8,2,24576]{2,1,0:T(2,128)(2,1)S(1)} async-done(((bf16[8,2,24576]{2,1,0:T(2,128)(2,1)}), bf16[8,2,24576]{2,1,0:T(2,128)(2,1)S(1)}, u32[]{:S(2)}, u32[]{:S(2)}) %all-to-all-start) | async-done | bytes 786464 | tf_op jit(solution)/shard_map/all_to_all | solution.py:45
  34.0 0.8 reshape.150
  34.8 0.9 copy.82
  35.7 0.0 copy-start.2
  35.7 0.0 copy-start.4
  35.7 0.8 gather_fusion.2
  36.5 0.1 bitcast_select_fusion.1
  36.6 18.1 %all_gather.6 = bf16[2,256,768]{2,1,0:T(8,128)(2,1)S(1)} all-gather(bf16[2,64,768]{2,1,0:T(8,128)(2,1)S(1)} %bitcast_select_fusion.1), channel_id=1, replica_groups=mesh['dp'=8,'mp'=4] {'mp'}, dimensions={1}, use_global_device_ids=true | all-gather | bytes 983040 | tf_op jit(solution)/shard_map/all_gather | solution.py:51
  54.7 0.0 copy-done.2
  54.7 0.0 copy-done.4
  54.7 0.4 fusion.20
  55.1 0.2 copy.63
  55.3 17.4 %all_gather.7 = bf16[2,256,768]{1,0,2:T(2,128)(2,1)S(1)} all-gather(bf16[2,256,192]{1,0,2:T(2,128)(2,1)S(1)} %copy.63), channel_id=1, replica_groups=mesh['dp'=8,'mp'=4] {'mp'}, dimensions={2}, use_global_device_ids=true | all-gather | bytes 983040 | tf_op jit(solution)/shard_map/all_gather | solution.py:56
  72.7 0.6 copy.64
  73.3 0.0 copy-start.9
  73.3 0.2 convert_reduce_fusion
  73.5 0.4 fusion.4
  73.9 0.6 copy-done.9
  74.5 0.8 convolution_convert_fusion.2
  75.3 0.7 fusion.108
  76.0 0.9 convolution_convert_fusion.3
  76.9 0.1 copy-done.3
  76.9 1.3 convolution_convert_fusion.1
  78.3 0.0 all-reduce.4.cloned.1.call-update
  78.3 0.2 all-reduce.6.cloned.1.call-start
  78.5 0.0 copy-done.7
  78.5 44.0 %all-reduce.4.cloned.1.call-done = bf16[2,256,768]{2,1,0:T(8,128)(2,1)} async-done(((bf16[2,256,768]{2,1,0:T(8,128)(2,1)}), bf16[2,256,768]{2,1,0:T(8,128)(2,1)}) %all-reduce.4.cloned.1.call-update) | async-done | bytes 786448 | tf_op jit(solution)/shard_map/psum | solution.py:75
  122.5 1.5 fusion.107
  124.0 0.0 copy-done.1
  124.0 0.4 multiply_reduce_fusion
  124.4 0.0 copy-done
  124.4 0.0 copy-start.8
  124.5 1.3 fusion.63
  125.7 0.0 copy-done.8
  125.7 4.4 %convolution_convert_fusion = bf16[2,256,768]{2,1,0:T(8,128)(2,1)S(1)} fusion(bf16[768,768]{1,0:T(8,128)(2,1)S(1)} %copy-done.8, f32[2,256,768]{2,1,0:T(8,128)S(1)} %get-tuple-element.13, u8[256,768]{1,0:T(8,128)(4,1)S(1)} %get-tuple-element.6, u8[256,768]{1,0:T(8,128)(4,1)S(1)} %get-tuple-element.5), kind=kOutput, calls=%fused_computation.41 | convolution fusion | flops 631898112 | bytes 3932160 | tf_op jit(solution)/shard_map/btf,fd->btd/dot_general | solution.py:82
  130.2 0.0 copy-start.10
  130.2 1.7 copy.69
  131.9 0.0 all-reduce.6.cloned.1.call-update
  131.9 0.0 copy-done.10
  131.9 0.6 dynamic-slice
  133.2 42.0 %all-reduce.6.cloned.1.call-done = bf16[2,256,768]{2,0,1:T(2,128)(2,1)} async-done(((bf16[2,256,768]{2,0,1:T(2,128)(2,1)}), bf16[2,256,768]{2,0,1:T(2,128)(2,1)}) %all-reduce.6.cloned.1.call-update) | async-done | bytes 786448
  175.2 1.1 constant_dynamic-slice_fusion
  176.3 0.7 add_convert_fusion
  (15 shorter events, 0.1 us)
Async XLA Ops:
  6.5 117.9 %copy-start = (bf16[768,768]{1,0:T(8,128)(2,1)S(1)}, bf16[768,768]{1,0:T(8,128)(2,1)}, u32[]{:S(2)}) copy-start(bf16[768,768]{1,0:T(8,128)(2,1)} %param.22) | copy-start | bytes 3538948
  14.7 6.8 %copy-start.5 = (bf16[256,192]{0,1:T(8,128)(2,1)S(1)}, bf16[256,192]{0,1:T(8,128)(2,1)}, u32[]{:S(2)}) copy-start(bf16[256,192]{0,1:T(8,128)(2,1)} %param.17) | copy-start | bytes 294916
  14.7 7.5 %copy-start.6 = (bf16[768]{0:T(1024)(128)(2,1)S(1)}, bf16[768]{0:T(1024)(128)(2,1)}, u32[]{:S(2)}) copy-start(bf16[768]{0:T(1024)(128)(2,1)} %param.20) | copy-start | bytes 4612
  16.2 17.8 %all-to-all-start = ((bf16[8,2,24576]{2,1,0:T(2,128)(2,1)}), bf16[8,2,24576]{2,1,0:T(2,128)(2,1)S(1)}, u32[]{:S(2)}, u32[]{:S(2)}) async-start(bf16[8,2,24576]{2,1,0:T(2,128)(2,1)} %reshape.149), calls=%async_computation | async-start | bytes 1572864 | tf_op jit(solution)/shard_map/all_to_all | solution.py:45
  21.4 101.1 %all-reduce.4.cloned.1.call-start = ((), (), s32[]{:S(2)}) async-start(), calls=%async_computation.1 | async-start | bytes 1572864 | tf_op jit(solution)/shard_map/psum | solution.py:75
  35.7 19.0 %copy-start.2 = (f32[256,192]{0,1:T(8,128)S(1)}, f32[256,192]{0,1:T(8,128)}, u32[]{:S(2)}) copy-start(f32[256,192]{0,1:T(8,128)} %convert_element_type.51) | copy-start | bytes 589828
  35.7 19.0 %copy-start.4 = (bf16[768,192]{0,1:T(8,128)(2,1)S(1)}, bf16[768,192]{0,1:T(8,128)(2,1)}, u32[]{:S(2)}) copy-start(bf16[768,192]{0,1:T(8,128)(2,1)} %param.16) | copy-start | bytes 884740
  73.3 1.2 copy-start.9
  76.0 1.0 copy-start.3
  76.9 1.6 copy-start.7
  78.3 96.9 %all-reduce.6.cloned.1.call-start = ((), (), s32[]{:S(2)}) async-start(), calls=%async_computation.2 | async-start | bytes 1572864
  122.5 1.5 copy-start.1
  124.4 1.3 copy-start.8
  130.2 1.8 copy-start.10
Sparse Core Ops, SparseCore 0:
  78.4 44.0 all-reduce.3
  132.0 43.1 all-reduce.5
where the time goes:
time: 184 us
  waiting for transfers between devices  97.8 us (53%)
  blocking collectives  35.5 us (19%)
  between operations  14.3 us (8%)
  local copies, waits for them, and re-layouts  14 us (8%)
  matrix products  9.79 us (5%)
  other arithmetic  7.02 us (4%)
  starting transfers between devices  5.46 us (3%)
    psum x1, waiting for transfers between devices, local(): lax.psum(partial_out.astype(jnp.bfloat16), 'mp').astype(jnp.float32)  44 us
    unnamed x3, waiting for transfers between devices  42.1 us
    all_gather x1, blocking collectives, local(): lax.all_gather(own_pixels, 'mp', axis=1, tiled=True)  18.1 us
    all_gather x1, blocking collectives, local(): lax.all_gather(embedded, 'mp', axis=2, tiled=True).astype(jnp.float32)  17.4 us
    all_to_all x1, waiting for transfers between devices, local(): lax.all_to_all(outgoing, 'dp', split_axis=0, concat_axis=0, tiled=True)  11.7 us
    unnamed x28, local copies, waits for them, and re-layouts  7.11 us
    all_to_all x1, starting transfers between devices, local(): lax.all_to_all(outgoing, 'dp', split_axis=0, concat_axis=0, tiled=True)  5.2 us
    dot_general x1, matrix products, local(): jnp.einsum('btf,fd->btd', hidden, down_weight, preferred_element_type=jnp...  4.43 us
  transfers between devices with their start and end apart: 3, of which 3 were waited for; matrix products, arithmetic and copies ran while one was open for 1% of the time, Pallas kernels for 0%

commit v1 on v0

v1 whole, which is shorter than its diff:
```python
import jax
import jax.numpy as jnp
from jax import lax
from jax.sharding import PartitionSpec as P

CAND_DEV = 8
SEL_DEV = 2
HEAD_DIM = 64


def norm_rows(values, gain):
    average = jnp.mean(values, axis=-1, keepdims=True)
    centred = values - average
    variance = jnp.mean(centred * centred, axis=-1, keepdims=True)
    return centred * lax.rsqrt(variance + 1e-06) * gain.astype(jnp.float32)


def shift(value, step):
    count = lax.axis_size("mp")
    return lax.ppermute(value, "mp", [(i, (i + step) % count) for i in range(count)])


def spread(value):
    return [value] + [shift(value, s) for s in range(1, lax.axis_size("mp"))]


def collect(parts):
    return [parts[0]] + [shift(parts[s], -s) for s in range(1, lax.axis_size("mp"))]


def total(parts):
    result = parts[0].astype(jnp.float32)
    for part in parts[1:]:
        result = result + part.astype(jnp.float32)
    return result


def local(
    candidates,
    owner_row,
    selected,
    dest_slot,
    patch_weight,
    positions,
    qkv_weight,
    out_weight,
    attn_gain,
    mlp_gain,
    up_weight,
    down_weight,
):
    learners = lax.axis_size("dp")
    own_index = lax.axis_index("dp")
    groups = lax.axis_size("mp")
    own_group = lax.axis_index("mp")
    quarter = candidates.shape[1]
    pixel_width = candidates.shape[2]
    chosen_rows = jnp.take(owner_row, selected)
    slot_rows = jnp.zeros(dest_slot.shape, jnp.int32).at[dest_slot].set(chosen_rows)
    source_owner = slot_rows // CAND_DEV
    local_row = slot_rows % CAND_DEV
    mine = (source_owner == own_index).reshape(learners, SEL_DEV)
    picked = jnp.sum(jnp.where(mine, local_row.reshape(learners, SEL_DEV), 0), axis=1)
    outgoing = jnp.take(candidates, picked, axis=0)
    incoming = lax.all_to_all(outgoing, "dp", split_axis=0, concat_axis=0, tiled=True)
    senders = lax.dynamic_slice_in_dim(source_owner, own_index * SEL_DEV, SEL_DEV)
    own_pixels = jnp.take(incoming, senders, axis=0)

    weight_parts = [patch_weight]
    position_parts = [lax.dynamic_slice_in_dim(positions, own_group * quarter, quarter, 0)]
    for s in range(1, groups):
        rows = lax.dynamic_slice_in_dim(positions, ((own_group + s) % groups) * quarter, quarter, 0)
        both = shift(jnp.concatenate([patch_weight, rows], axis=0), s)
        weight_parts.append(both[:pixel_width])
        position_parts.append(both[pixel_width:])
    stack = jnp.stack(
        [jnp.concatenate([w, p], axis=0) for w, p in zip(weight_parts, position_parts)]
    )
    whole = jnp.concatenate(
        [
            lax.dynamic_index_in_dim(stack, (own_group - j) % groups, 0, keepdims=False)
            for j in range(groups)
        ],
        axis=1,
    )
    product = jnp.einsum(
        "brp,pe->bre", own_pixels, whole[:pixel_width], preferred_element_type=jnp.float32
    )
    embedded = (product + whole[pixel_width:].astype(jnp.float32)[None]).astype(jnp.bfloat16)
    activations = embedded.astype(jnp.float32)
    normed = norm_rows(activations, attn_gain).astype(jnp.bfloat16)
    tokens = jnp.concatenate(spread(normed), axis=1)
    projected = jnp.einsum(
        "btd,dce->btce", tokens, qkv_weight, preferred_element_type=jnp.float32
    ).astype(jnp.bfloat16)
    local_heads = qkv_weight.shape[2] // HEAD_DIM
    head_split = projected.reshape(SEL_DEV, groups * quarter, 3, local_heads, HEAD_DIM)
    queries = head_split[:, :, 0]
    attn_keys = head_split[:, :, 1]
    attn_values = head_split[:, :, 2]
    scores = jnp.einsum(
        "bqhd,bkhd->bhqk", queries, attn_keys, preferred_element_type=jnp.float32
    ) * HEAD_DIM ** (-0.5)
    attn_probs = jax.nn.softmax(scores, axis=-1).astype(jnp.bfloat16)
    context = jnp.einsum(
        "bhqk,bkhd->bqhd", attn_probs, attn_values, preferred_element_type=jnp.float32
    ).astype(jnp.bfloat16)
    context = context.reshape(SEL_DEV, groups * quarter, local_heads * HEAD_DIM)
    partial_out = jnp.einsum(
        "bte,ed->btd", context, out_weight, preferred_element_type=jnp.float32
    ).astype(jnp.bfloat16)
    attended = total(
        collect([partial_out[:, s * quarter : (s + 1) * quarter] for s in range(groups)])
    )
    after_attn = activations + attended
    normed2 = norm_rows(after_attn, mlp_gain).astype(jnp.bfloat16)
    down_terms = []
    for part in spread(normed2):
        hidden = jax.nn.gelu(
            jnp.einsum("btd,df->btf", part, up_weight, preferred_element_type=jnp.float32),
            approximate=False,
        ).astype(jnp.bfloat16)
        down_terms.append(
            jnp.einsum(
                "btf,fd->btd", hidden, down_weight, preferred_element_type=jnp.float32
            ).astype(jnp.bfloat16)
        )
    return (after_attn + total(collect(down_terms))).astype(jnp.bfloat16)


def solution(mesh):
    return jax.shard_map(
        local,
        mesh=mesh,
        in_specs=(
            P("dp", "mp", None),
            P(),
            P(),
            P(),
            P(None, "mp"),
            P(None, "mp"),
            P(None, None, "mp"),
            P("mp", None),
            P(),
            P(),
            P(None, "mp"),
            P("mp", None),
        ),
        out_specs=P("dp", "mp", None),
        check_vma=False,
    )
```

time: 184 us -> 130 us (0.71)
  starting transfers between devices: 5.46 us -> 45.8 us
  waiting for transfers between devices: 97.8 us -> 59.5 us
  blocking collectives: 35.5 us -> 0 us
  between operations: 14.3 us -> 0.45 us
  local copies, waits for them, and re-layouts: 14 us -> 5.84 us
    ppermute x0 -> x15, waiting for transfers between devices: none -> 59.5 us  [shift(): lax.ppermute(value, 'mp', [(i, (i + step) % count) for i in range(count)])]
    psum x1 -> x0, waiting for transfers between devices: 44 us -> none  [local(): lax.psum(partial_out.astype(jnp.bfloat16), 'mp').astype(jnp.float32)]
    unnamed x3 -> x0, waiting for transfers between devices: 42.1 us -> none
    ppermute x0 -> x15, starting transfers between devices: none -> 41.6 us  [shift(): lax.ppermute(value, 'mp', [(i, (i + step) % count) for i in range(count)])]
    all_gather x2 -> x0, blocking collectives: 35.5 us -> none  [the longest x1 18.1 us: local(): lax.all_gather(own_pixels, 'mp', axis=1, tiled=True)]
    all_to_all x1, waiting for transfers between devices: 11.7 us -> 0.01 us  [local(): lax.all_to_all(outgoing, 'dp', split_axis=0, concat_axis=0, tiled=True)]
    unnamed x28 -> x20, local copies, waits for them, and re-layouts: 7.11 us -> 0.12 us
    another operation x0 -> x2, other arithmetic: none -> 3.38 us  [local(): jnp.stack([jnp.concatenate([w, p], axis=0) for w, p in zip(weight_parts,...]
  transfers between devices with their start and end apart: 3 -> 16, of which waited for: 3 -> 8; matrix products, arithmetic and copies ran while one was open for 1% -> 9% of each run, Pallas kernels for 0% -> 0%
where the time goes in v1:
time: 130 us
  waiting for transfers between devices  59.5 us (46%)
  starting transfers between devices  45.8 us (35%)
  matrix products  11.2 us (9%)
  other arithmetic  7.26 us (6%)
  local copies, waits for them, and re-layouts  5.84 us (4%)
    ppermute x15, waiting for transfers between devices, shift(): lax.ppermute(value, 'mp', [(i, (i + step) % count) for i in range(count)])  59.5 us
    ppermute x15, starting transfers between devices, shift(): lax.ppermute(value, 'mp', [(i, (i + step) % count) for i in range(count)])  41.6 us
    dot_general x4, matrix products, local(): jnp.einsum('btf,fd->btd', hidden, down_weight, preferred_element_type=jnp...  5.27 us
    all_to_all x1, starting transfers between devices, local(): lax.all_to_all(outgoing, 'dp', split_axis=0, concat_axis=0, tiled=True)  4.2 us
    another operation x2, other arithmetic, local(): jnp.stack([jnp.concatenate([w, p], axis=0) for w, p in zip(weight_parts,...  3.38 us
  transfers between devices with their start and end apart: 16, of which 8 were waited for; matrix products, arithmetic and copies ran while one was open for 9% of the time, Pallas kernels for 0%

profile of v1, /device:TPU:0, one launch (start us, length us, event | category | flops | bytes accessed | tf_op | source)
XLA Modules:
  0.0 130.0 jit_solution(10563297743808347183)
XLA Ops:
  0.1 1.1 constant_dynamic-slice_fusion.7
  1.2 1.9 %maximum_bitcast_fusion.2 = (bf16[1,832,192]{1,2,0:T(8,128)(2,1)S(1)}, bf16[832,192]{0,1:T(8,128)(2,1)}, bf16[832,192]{0,1:T(8,128)(2,1)}, bf16[832,192]{0,1:T(8,128)(2,1)S(1)}) fusion(bf16[64,192]{0,1:T(8,128)(2,1)S(1)} %get-tuple-element.30, bf16[768,192]{0,1:T(8,128)(2,1)} %param.16, bf16[64,192]{0,1:T(8,128)(2,1)S(1)} %get-tuple-element.31, ...), kind=kLoop, calls=%fused_computation.139 | loop fusion | flops 2076672 | bytes 1671168 | tf_op jit(solution)/shard_map/stack | solution.py:76
  3.1 3.1 %collective-permute-start = (bf16[832,192]{0,1:T(8,128)(2,1)}, bf16[832,192]{0,1:T(8,128)(2,1)}, u32[]{:S(2)}, u32[]{:S(2)}) collective-permute-start(bf16[832,192]{0,1:T(8,128)(2,1)} %get-tuple-element.27), channel_id=1, source_target_pairs={{0,1},{1,2},{2,3},{3,0},{4,5},{5,6},{6,7},{7,4},{8,9},{9,10},{10,1... | collective-permute-start | bytes 958472 | tf_op jit(solution)/shard_map/ppermute | solution.py:20
  6.2 2.6 %collective-permute-start.1 = (bf16[832,192]{0,1:T(8,128)(2,1)}, bf16[832,192]{0,1:T(8,128)(2,1)}, u32[]{:S(2)}, u32[]{:S(2)}) collective-permute-start(bf16[832,192]{0,1:T(8,128)(2,1)} %get-tuple-element.28), channel_id=1, source_target_pairs={{0,2},{1,3},{2,0},{3,1},{4,6},{5,7},{6,4},{7,5},{8,10},{9,11},{10,... | collective-permute-start | bytes 958472 | tf_op jit(solution)/shard_map/ppermute | solution.py:20
  8.8 1.3 %collective-permute-start.2 = (bf16[832,192]{0,1:T(8,128)(2,1)S(1)}, bf16[832,192]{0,1:T(8,128)(2,1)}, u32[]{:S(2)}, u32[]{:S(2)}) collective-permute-start(bf16[832,192]{0,1:T(8,128)(2,1)S(1)} %get-tuple-element.29), channel_id=1, source_target_pairs={{0,3},{1,0},{2,1},{3,2},{4,7},{5,4},{6,5},{7,6},{8,11},{9,8},{10,9... | collective-permute-start | bytes 958472 | tf_op jit(solution)/shard_map/ppermute | solution.py:20
  10.2 0.7 gather_fusion
  10.8 0.6 scatter_custom_fusion
  11.5 0.1 select_n.125
  11.6 0.1 reduce_sum.56
  11.7 0.6 gather_fusion.1
  12.4 0.0 copy-start.4
  12.4 1.0 broadcast_select_fusion
  13.4 4.2 %all-to-all-start = ((bf16[8,64,768]{2,1,0:T(8,128)(2,1)}), bf16[8,64,768]{2,1,0:T(8,128)(2,1)}, u32[]{:S(2)}, u32[]{:S(2)}) async-start(bf16[8,64,768]{2,1,0:T(8,128)(2,1)} %broadcast_select_fusion), calls=%async_computation | async-start | bytes 1572864 | tf_op jit(solution)/shard_map/all_to_all | solution.py:65
  17.6 0.1 compare_and_fusion.1
  17.8 13.7 %collective-permute-done.1 = bf16[832,192]{0,1:T(8,128)(2,1)} collective-permute-done((bf16[832,192]{0,1:T(8,128)(2,1)}, bf16[832,192]{0,1:T(8,128)(2,1)}, u32[]{:S(2)}, u32[]{:S(2)}) %collective-permute-start.1) | collective-permute-done | bytes 319520 | tf_op jit(solution)/shard_map/ppermute | solution.py:20
  31.5 1.4 %pad_maximum_fusion = bf16[4,832,192]{1,2,0:T(8,128)(2,1)S(1)} fusion(bf16[1,832,192]{1,2,0:T(8,128)(2,1)} %bitcast.5, bf16[1,832,192]{1,2,0:T(8,128)(2,1)} %bitcast.4, bf16[1,832,192]{1,2,0:T(8,128)(2,1)} %bitcast.3, bf16[1,832,192]{1,2,0:T(8,128)(2,1)S(1)} %get-tuple-element.26), kind=kLoop, calls=%fused_computation.10 | loop fusion | flops 1916928 | bytes 2555904 | tf_op jit(solution)/shard_map/stack | solution.py:76
  32.9 0.1 constant_dynamic-slice_fusion.3
  33.1 0.2 copy.21
  33.3 0.2 copy.22
  33.5 0.2 copy.23
  33.7 0.2 copy.24
  33.9 0.1 maximum_convert_fusion
  33.9 1.6 %pad_maximum_fusion.1 = bf16[832,768]{1,0:T(8,128)(2,1)} fusion(bf16[832,192]{1,0:T(8,128)(2,1)S(1)} %bitcast.122, bf16[832,192]{1,0:T(8,128)(2,1)S(1)} %bitcast.120, bf16[832,192]{1,0:T(8,128)(2,1)S(1)} %bitcast.118, bf16[832,192]{1,0:T(8,128)(2,1)S(1)} %bitcast.116), kind=kLoop, calls=%fused_computation.12 | loop fusion | flops 5111808 | bytes 2555904 | tf_op jit(solution)/shard_map/concatenate | solution.py:79
  35.6 1.7 %gather_fusion.2 = bf16[2,64,768]{2,1,0:T(8,128)(2,1)S(1)} fusion(bf16[8,64,768]{2,1,0:T(8,128)(2,1)} %all-to-all-done, s32[1024]{0:T(1024)S(1)} %pad_clamp_fusion), kind=kCustom, calls=%fused_computation.2 | custom fusion | bytes 393224 | tf_op jit(solution)/shard_map/jit(_take)/gather | solution.py:67
  37.3 0.0 copy-start.9
  37.3 1.8 %fusion.367 = (f32[2,64]{1,0:T(2,128)S(1)}, f32[2,64,768]{2,1,0:T(8,128)S(1)}) fusion(f32[64,768]{1,0:T(8,128)S(1)} %maximum_convert_fusion, bf16[832,768]{1,0:T(8,128)(2,1)} %pad_maximum_fusion.1, bf16[2,64,768]{2,1,0:T(8,128)(2,1)S(1)} %gather_fusion.2, pred[2]{0:T(512)(128)(4,1)S(1)} %get-tuple-element.15), kind=kOutput, calls=%fused_computation.455 | convolution fusion | flops 151486336 | bytes 1966594 | tf_op jit(solution)/shard_map/brp,pe->bre/dot_general | solution.py:86
  39.1 0.2 multiply_reduce_fusion.1
  39.3 0.1 multiply_convert_fusion.1
  39.4 7.9 %collective-permute-start.3 = (bf16[2,64,768]{2,1,0:T(8,128)(2,1)S(1)}, bf16[2,64,768]{2,1,0:T(8,128)(2,1)S(1)}, u32[]{:S(2)}, u32[]{:S(2)}) collective-permute-start(bf16[2,64,768]{2,1,0:T(8,128)(2,1)S(1)} %multiply_convert_fusion.1), channel_id=1, source_target_pairs={{0,1},{1,2},{2,3},{3,0},{4,5},{5,6},{6,7},{7,4},{8,9},{9,10},{10,1... | collective-permute-start | bytes 589832 | tf_op jit(solution)/shard_map/ppermute | solution.py:20
  47.3 1.6 %collective-permute-start.4 = (bf16[2,64,768]{2,1,0:T(8,128)(2,1)S(1)}, bf16[2,64,768]{2,1,0:T(8,128)(2,1)S(1)}, u32[]{:S(2)}, u32[]{:S(2)}) collective-permute-start(bf16[2,64,768]{2,1,0:T(8,128)(2,1)S(1)} %multiply_convert_fusion.1), channel_id=1, source_target_pairs={{0,2},{1,3},{2,0},{3,1},{4,6},{5,7},{6,4},{7,5},{8,10},{9,11},{10,... | collective-permute-start | bytes 589832 | tf_op jit(solution)/shard_map/ppermute | solution.py:20
  48.9 0.8 collective-permute-start.5
  49.8 4.4 %collective-permute-done.3 = bf16[2,64,768]{2,1,0:T(8,128)(2,1)S(1)} collective-permute-done((bf16[2,64,768]{2,1,0:T(8,128)(2,1)S(1)}, bf16[2,64,768]{2,1,0:T(8,128)(2,1)S(1)}, u32[]{:S(2)}, u32[]{:S(2)}) %collective-permute-start.3) | collective-permute-done | bytes 196640 | tf_op jit(solution)/shard_map/ppermute | solution.py:20
  54.2 6.7 %collective-permute-done.4 = bf16[2,64,768]{2,1,0:T(8,128)(2,1)S(1)} collective-permute-done((bf16[2,64,768]{2,1,0:T(8,128)(2,1)S(1)}, bf16[2,64,768]{2,1,0:T(8,128)(2,1)S(1)}, u32[]{:S(2)}, u32[]{:S(2)}) %collective-permute-start.4) | collective-permute-done | bytes 196640 | tf_op jit(solution)/shard_map/ppermute | solution.py:20
  60.9 0.7 convolution_convert_fusion.1
  61.6 0.7 fusion.368
  62.3 0.9 convolution_convert_fusion.2
  63.1 0.0 copy-start.5
  63.2 0.1 copy-done.3
  63.2 0.4 convolution_convert_fusion
  63.7 6.5 %collective-permute-start.6 = (bf16[2,64,768]{2,1,0:T(8,128)(2,1)S(1)}, bf16[2,64,768]{2,1,0:T(8,128)(2,1)S(1)}, u32[]{:S(2)}, u32[]{:S(2)}) collective-permute-start(bf16[2,64,768]{2,1,0:T(8,128)(2,1)S(1)} %get-tuple-element.23), channel_id=1, source_target_pairs={{0,3},{1,0},{2,1},{3,2},{4,7},{5,4},{6,5},{7,6},{8,11},{9,8},{10,9... | collective-permute-start | bytes 589832 | tf_op jit(solution)/shard_map/ppermute | solution.py:20
  70.2 0.6 collective-permute-start.8
  70.9 4.7 %collective-permute-done.6 = bf16[2,64,768]{2,1,0:T(8,128)(2,1)S(1)} collective-permute-done((bf16[2,64,768]{2,1,0:T(8,128)(2,1)S(1)}, bf16[2,64,768]{2,1,0:T(8,128)(2,1)S(1)}, u32[]{:S(2)}, u32[]{:S(2)}) %collective-permute-start.6) | collective-permute-done | bytes 196640 | tf_op jit(solution)/shard_map/ppermute | solution.py:20
  75.6 11.8 %collective-permute-done.7 = bf16[2,64,768]{2,1,0:T(8,128)(2,1)S(1)} collective-permute-done((bf16[2,64,768]{2,1,0:T(8,128)(2,1)S(1)}, bf16[2,64,768]{2,1,0:T(8,128)(2,1)S(1)}, u32[]{:S(2)}, u32[]{:S(2)}) %collective-permute-start.7) | collective-permute-done | bytes 196640 | tf_op jit(solution)/shard_map/ppermute | solution.py:20
  87.3 0.2 fusion.365
  87.5 0.2 multiply_reduce_fusion
  87.7 0.0 copy-start.8
  87.8 0.1 multiply_convert_fusion
  87.9 0.1 collective-permute-start.9
  87.9 2.0 %collective-permute-start.11 = (bf16[2,64,768]{2,1,0:T(8,128)(2,1)S(1)}, bf16[2,64,768]{2,1,0:T(8,128)(2,1)S(1)}, u32[]{:S(2)}, u32[]{:S(2)}) collective-permute-start(bf16[2,64,768]{2,1,0:T(8,128)(2,1)S(1)} %multiply_convert_fusion), channel_id=1, source_target_pairs={{0,2},{1,3},{2,0},{3,1},{4,6},{5,7},{6,4},{7,5},{8,10},{9,11},{10,... | collective-permute-start | bytes 589832 | tf_op jit(solution)/shard_map/ppermute | solution.py:20
  89.9 2.8 %collective-permute-start.13 = (bf16[2,64,768]{2,1,0:T(8,128)(2,1)S(1)}, bf16[2,64,768]{2,1,0:T(8,128)(2,1)S(1)}, u32[]{:S(2)}, u32[]{:S(2)}) collective-permute-start(bf16[2,64,768]{2,1,0:T(8,128)(2,1)S(1)} %multiply_convert_fusion), channel_id=1, source_target_pairs={{0,3},{1,0},{2,1},{3,2},{4,7},{5,4},{6,5},{7,6},{8,11},{9,8},{10,9... | collective-permute-start | bytes 589832 | tf_op jit(solution)/shard_map/ppermute | solution.py:20
  92.8 4.8 %collective-permute-done.9 = bf16[2,64,768]{2,1,0:T(8,128)(2,1)S(1)} collective-permute-done((bf16[2,64,768]{2,1,0:T(8,128)(2,1)S(1)}, bf16[2,64,768]{2,1,0:T(8,128)(2,1)S(1)}, u32[]{:S(2)}, u32[]{:S(2)}) %collective-permute-start.9) | collective-permute-done | bytes 196640 | tf_op jit(solution)/shard_map/ppermute | solution.py:20
  97.6 0.4 fusion.220
  98.0 1.1 fusion.25
  99.2 0.1 collective-permute-start.10
  99.2 5.0 %collective-permute-done.11 = bf16[2,64,768]{2,1,0:T(8,128)(2,1)S(1)} collective-permute-done((bf16[2,64,768]{2,1,0:T(8,128)(2,1)S(1)}, bf16[2,64,768]{2,1,0:T(8,128)(2,1)S(1)}, u32[]{:S(2)}, u32[]{:S(2)}) %collective-permute-start.11) | collective-permute-done | bytes 196640 | tf_op jit(solution)/shard_map/ppermute | solution.py:20
  104.3 0.4 fusion.221
  104.6 1.1 fusion.28
  105.8 9.8 %collective-permute-start.12 = (bf16[2,64,768]{2,1,0:T(8,128)(2,1)S(1)}, bf16[2,64,768]{2,1,0:T(8,128)(2,1)S(1)}, u32[]{:S(2)}, u32[]{:S(2)}) collective-permute-start(bf16[2,64,768]{2,1,0:T(8,128)(2,1)S(1)} %fusion.28), channel_id=1, source_target_pairs={{0,2},{1,3},{2,0},{3,1},{4,6},{5,7},{6,4},{7,5},{8,10},{9,11},{10,... | collective-permute-start | bytes 589832 | tf_op jit(solution)/shard_map/ppermute | solution.py:20
  115.6 0.4 fusion.222
  116.0 1.1 fusion.31
  117.1 2.3 %collective-permute-start.14 = (bf16[2,64,768]{2,1,0:T(8,128)(2,1)S(1)}, bf16[2,64,768]{2,1,0:T(8,128)(2,1)S(1)}, u32[]{:S(2)}, u32[]{:S(2)}) collective-permute-start(bf16[2,64,768]{2,1,0:T(8,128)(2,1)S(1)} %fusion.31), channel_id=1, source_target_pairs={{0,1},{1,2},{2,3},{3,0},{4,5},{5,6},{6,7},{7,4},{8,9},{9,10},{10,1... | collective-permute-start | bytes 589832 | tf_op jit(solution)/shard_map/ppermute | solution.py:20
  119.5 0.4 fusion.219
  119.9 8.3 %collective-permute-done.12 = bf16[2,64,768]{2,1,0:T(8,128)(2,1)S(1)} collective-permute-done((bf16[2,64,768]{2,1,0:T(8,128)(2,1)S(1)}, bf16[2,64,768]{2,1,0:T(8,128)(2,1)S(1)}, u32[]{:S(2)}, u32[]{:S(2)}) %collective-permute-start.12) | collective-permute-done | bytes 196640 | tf_op jit(solution)/shard_map/ppermute | solution.py:20
  128.2 1.8 %add_convert_fusion = bf16[2,64,768]{2,1,0:T(8,128)(2,1)} fusion(f32[2,64,768]{2,1,0:T(8,128)S(1)} %get-tuple-element.14, bf16[2,64,768]{2,1,0:T(8,128)(2,1)S(1)} %collective-permute-done.14, bf16[2,64,768]{2,1,0:T(8,128)(2,1)S(1)} %collective-permute-done.12, bf16[2,64,768]{2,1,0:T(8,128)(2,1)S(1)} %collective-permute-done.10, ...), kind=kOutput, calls=%fused_computation.81 | convolution fusion | flops 158859264 | bytes 2850816 | tf_op jit(solution)/shard_map/btf,fd->btd/dot_general | solution.py:124
  (39 shorter events, 0.2 us)
Async XLA Ops:
  0.0 97.6 %copy-start = (bf16[768,768]{1,0:T(8,128)(2,1)S(1)}, bf16[768,768]{1,0:T(8,128)(2,1)}, u32[]{:S(2)}) copy-start(bf16[768,768]{1,0:T(8,128)(2,1)} %param.22) | copy-start | bytes 3538948
  0.0 10.1 %copy-start.7 = (s32[16]{0:T(128)S(1)}, s32[16]{0:T(128)}, u32[]{:S(2)}) copy-start(s32[16]{0:T(128)} %param.14) | copy-start | bytes 196
  0.0 10.1 %copy-start.6 = (s32[16]{0:T(128)S(1)}, s32[16]{0:T(128)}, u32[]{:S(2)}) copy-start(s32[16]{0:T(128)} %param.15) | copy-start | bytes 196
  0.0 10.2 %copy-start.1 = (s32[64]{0:T(128)S(1)}, s32[64]{0:T(128)}, u32[]{:S(2)}) copy-start(s32[64]{0:T(128)} %param.13) | copy-start | bytes 772
  0.1 11.7 %copy-start.2 = (bf16[8,64,768]{2,1,0:T(8,128)(2,1)S(1)}, bf16[8,64,768]{2,1,0:T(8,128)(2,1)}, u32[]{:S(2)}) copy-start(bf16[8,64,768]{2,1,0:T(8,128)(2,1)} %param.12) | copy-start | bytes 2359300
  3.1 14.6 %collective-permute-start = (bf16[832,192]{0,1:T(8,128)(2,1)}, bf16[832,192]{0,1:T(8,128)(2,1)}, u32[]{:S(2)}, u32[]{:S(2)}) collective-permute-start(bf16[832,192]{0,1:T(8,128)(2,1)} %get-tuple-element.27), channel_id=1, source_target_pairs={{0,1},{1,2},{2,3},{3,0},{4,5},{5,6},{6,7},{7,4},{8,9},{9,10},{10,1... | collective-permute-start | bytes 958472 | tf_op jit(solution)/shard_map/ppermute | solution.py:20
  6.2 25.3 %collective-permute-start.1 = (bf16[832,192]{0,1:T(8,128)(2,1)}, bf16[832,192]{0,1:T(8,128)(2,1)}, u32[]{:S(2)}, u32[]{:S(2)}) collective-permute-start(bf16[832,192]{0,1:T(8,128)(2,1)} %get-tuple-element.28), channel_id=1, source_target_pairs={{0,2},{1,3},{2,0},{3,1},{4,6},{5,7},{6,4},{7,5},{8,10},{9,11},{10,... | collective-permute-start | bytes 958472 | tf_op jit(solution)/shard_map/ppermute | solution.py:20
  8.8 22.7 %collective-permute-start.2 = (bf16[832,192]{0,1:T(8,128)(2,1)S(1)}, bf16[832,192]{0,1:T(8,128)(2,1)}, u32[]{:S(2)}, u32[]{:S(2)}) collective-permute-start(bf16[832,192]{0,1:T(8,128)(2,1)S(1)} %get-tuple-element.29), channel_id=1, source_target_pairs={{0,3},{1,0},{2,1},{3,2},{4,7},{5,4},{6,5},{7,6},{8,11},{9,8},{10,9... | collective-permute-start | bytes 958472 | tf_op jit(solution)/shard_map/ppermute | solution.py:20
  12.4 5.4 %copy-start.4 = (bf16[768]{0:T(1024)(128)(2,1)S(1)}, bf16[768]{0:T(1024)(128)(2,1)}, u32[]{:S(2)}) copy-start(bf16[768]{0:T(1024)(128)(2,1)} %param.20) | copy-start | bytes 4612
  13.4 22.2 %all-to-all-start = ((bf16[8,64,768]{2,1,0:T(8,128)(2,1)}), bf16[8,64,768]{2,1,0:T(8,128)(2,1)}, u32[]{:S(2)}, u32[]{:S(2)}) async-start(bf16[8,64,768]{2,1,0:T(8,128)(2,1)} %broadcast_select_fusion), calls=%async_computation | async-start | bytes 1572864 | tf_op jit(solution)/shard_map/all_to_all | solution.py:65
  37.3 23.7 %copy-start.9 = (bf16[768,3,192]{0,2,1:T(8,128)(2,1)S(1)}, bf16[768,3,192]{0,2,1:T(8,128)(2,1)}, u32[]{:S(2)}) copy-start(bf16[768,3,192]{0,2,1:T(8,128)(2,1)} %param.18) | copy-start | bytes 2654212
  39.4 14.8 %collective-permute-start.3 = (bf16[2,64,768]{2,1,0:T(8,128)(2,1)S(1)}, bf16[2,64,768]{2,1,0:T(8,128)(2,1)S(1)}, u32[]{:S(2)}, u32[]{:S(2)}) collective-permute-start(bf16[2,64,768]{2,1,0:T(8,128)(2,1)S(1)} %multiply_convert_fusion.1), channel_id=1, source_target_pairs={{0,1},{1,2},{2,3},{3,0},{4,5},{5,6},{6,7},{7,4},{8,9},{9,10},{10,1... | collective-permute-start | bytes 589832 | tf_op jit(solution)/shard_map/ppermute | solution.py:20
  47.3 13.6 %collective-permute-start.4 = (bf16[2,64,768]{2,1,0:T(8,128)(2,1)S(1)}, bf16[2,64,768]{2,1,0:T(8,128)(2,1)S(1)}, u32[]{:S(2)}, u32[]{:S(2)}) collective-permute-start(bf16[2,64,768]{2,1,0:T(8,128)(2,1)S(1)} %multiply_convert_fusion.1), channel_id=1, source_target_pairs={{0,2},{1,3},{2,0},{3,1},{4,6},{5,7},{6,4},{7,5},{8,10},{9,11},{10,... | collective-permute-start | bytes 589832 | tf_op jit(solution)/shard_map/ppermute | solution.py:20
  48.9 12.0 %collective-permute-start.5 = (bf16[2,64,768]{2,1,0:T(8,128)(2,1)S(1)}, bf16[2,64,768]{2,1,0:T(8,128)(2,1)S(1)}, u32[]{:S(2)}, u32[]{:S(2)}) collective-permute-start(bf16[2,64,768]{2,1,0:T(8,128)(2,1)S(1)} %multiply_convert_fusion.1), channel_id=1, source_target_pairs={{0,3},{1,0},{2,1},{3,2},{4,7},{5,4},{6,5},{7,6},{8,11},{9,8},{10,9... | collective-permute-start | bytes 589832 | tf_op jit(solution)/shard_map/ppermute | solution.py:20
  62.3 1.0 copy-start.3
  63.1 7.7 %copy-start.5 = (bf16[768]{0:T(1024)(128)(2,1)S(1)}, bf16[768]{0:T(1024)(128)(2,1)}, u32[]{:S(2)}) copy-start(bf16[768]{0:T(1024)(128)(2,1)} %param.21) | copy-start | bytes 4612
  63.7 11.9 %collective-permute-start.6 = (bf16[2,64,768]{2,1,0:T(8,128)(2,1)S(1)}, bf16[2,64,768]{2,1,0:T(8,128)(2,1)S(1)}, u32[]{:S(2)}, u32[]{:S(2)}) collective-permute-start(bf16[2,64,768]{2,1,0:T(8,128)(2,1)S(1)} %get-tuple-element.23), channel_id=1, source_target_pairs={{0,3},{1,0},{2,1},{3,2},{4,7},{5,4},{6,5},{7,6},{8,11},{9,8},{10,9... | collective-permute-start | bytes 589832 | tf_op jit(solution)/shard_map/ppermute | solution.py:20
  70.2 17.1 %collective-permute-start.7 = (bf16[2,64,768]{2,1,0:T(8,128)(2,1)S(1)}, bf16[2,64,768]{2,1,0:T(8,128)(2,1)S(1)}, u32[]{:S(2)}, u32[]{:S(2)}) collective-permute-start(bf16[2,64,768]{2,1,0:T(8,128)(2,1)S(1)} %get-tuple-element.25), channel_id=1, source_target_pairs={{0,2},{1,3},{2,0},{3,1},{4,6},{5,7},{6,4},{7,5},{8,10},{9,11},{10,... | collective-permute-start | bytes 589832 | tf_op jit(solution)/shard_map/ppermute | solution.py:20
  70.2 17.1 %collective-permute-start.8 = (bf16[2,64,768]{2,1,0:T(8,128)(2,1)S(1)}, bf16[2,64,768]{2,1,0:T(8,128)(2,1)S(1)}, u32[]{:S(2)}, u32[]{:S(2)}) collective-permute-start(bf16[2,64,768]{2,1,0:T(8,128)(2,1)S(1)} %get-tuple-element.24), channel_id=1, source_target_pairs={{0,1},{1,2},{2,3},{3,0},{4,5},{5,6},{6,7},{7,4},{8,9},{9,10},{10,1... | collective-permute-start | bytes 589832 | tf_op jit(solution)/shard_map/ppermute | solution.py:20
  87.7 10.3 %copy-start.8 = (bf16[768,768]{1,0:T(8,128)(2,1)S(1)}, bf16[768,768]{1,0:T(8,128)(2,1)}, u32[]{:S(2)}) copy-start(bf16[768,768]{1,0:T(8,128)(2,1)} %param.23) | copy-start | bytes 3538948
  87.9 9.7 %collective-permute-start.9 = (bf16[2,64,768]{2,1,0:T(8,128)(2,1)S(1)}, bf16[2,64,768]{2,1,0:T(8,128)(2,1)S(1)}, u32[]{:S(2)}, u32[]{:S(2)}) collective-permute-start(bf16[2,64,768]{2,1,0:T(8,128)(2,1)S(1)} %multiply_convert_fusion), channel_id=1, source_target_pairs={{0,1},{1,2},{2,3},{3,0},{4,5},{5,6},{6,7},{7,4},{8,9},{9,10},{10,1... | collective-permute-start | bytes 589832 | tf_op jit(solution)/shard_map/ppermute | solution.py:20
  87.9 16.3 %collective-permute-start.11 = (bf16[2,64,768]{2,1,0:T(8,128)(2,1)S(1)}, bf16[2,64,768]{2,1,0:T(8,128)(2,1)S(1)}, u32[]{:S(2)}, u32[]{:S(2)}) collective-permute-start(bf16[2,64,768]{2,1,0:T(8,128)(2,1)S(1)} %multiply_convert_fusion), channel_id=1, source_target_pairs={{0,2},{1,3},{2,0},{3,1},{4,6},{5,7},{6,4},{7,5},{8,10},{9,11},{10,... | collective-permute-start | bytes 589832 | tf_op jit(solution)/shard_map/ppermute | solution.py:20
  89.9 25.7 %collective-permute-start.13 = (bf16[2,64,768]{2,1,0:T(8,128)(2,1)S(1)}, bf16[2,64,768]{2,1,0:T(8,128)(2,1)S(1)}, u32[]{:S(2)}, u32[]{:S(2)}) collective-permute-start(bf16[2,64,768]{2,1,0:T(8,128)(2,1)S(1)} %multiply_convert_fusion), channel_id=1, source_target_pairs={{0,3},{1,0},{2,1},{3,2},{4,7},{5,4},{6,5},{7,6},{8,11},{9,8},{10,9... | collective-permute-start | bytes 589832 | tf_op jit(solution)/shard_map/ppermute | solution.py:20
  99.2 20.7 %collective-permute-start.10 = (bf16[2,64,768]{2,1,0:T(8,128)(2,1)S(1)}, bf16[2,64,768]{2,1,0:T(8,128)(2,1)S(1)}, u32[]{:S(2)}, u32[]{:S(2)}) collective-permute-start(bf16[2,64,768]{2,1,0:T(8,128)(2,1)S(1)} %fusion.25), channel_id=1, source_target_pairs={{0,3},{1,0},{2,1},{3,2},{4,7},{5,4},{6,5},{7,6},{8,11},{9,8},{10,9... | collective-permute-start | bytes 589832 | tf_op jit(solution)/shard_map/ppermute | solution.py:20
  105.8 22.4 %collective-permute-start.12 = (bf16[2,64,768]{2,1,0:T(8,128)(2,1)S(1)}, bf16[2,64,768]{2,1,0:T(8,128)(2,1)S(1)}, u32[]{:S(2)}, u32[]{:S(2)}) collective-permute-start(bf16[2,64,768]{2,1,0:T(8,128)(2,1)S(1)} %fusion.28), channel_id=1, source_target_pairs={{0,2},{1,3},{2,0},{3,1},{4,6},{5,7},{6,4},{7,5},{8,10},{9,11},{10,... | collective-permute-start | bytes 589832 | tf_op jit(solution)/shard_map/ppermute | solution.py:20
  117.1 11.0 %collective-permute-start.14 = (bf16[2,64,768]{2,1,0:T(8,128)(2,1)S(1)}, bf16[2,64,768]{2,1,0:T(8,128)(2,1)S(1)}, u32[]{:S(2)}, u32[]{:S(2)}) collective-permute-start(bf16[2,64,768]{2,1,0:T(8,128)(2,1)S(1)} %fusion.31), channel_id=1, source_target_pairs={{0,1},{1,2},{2,3},{3,0},{4,5},{5,6},{6,7},{7,4},{8,9},{9,10},{10,1... | collective-permute-start | bytes 589832 | tf_op jit(solution)/shard_map/ppermute | solution.py:20

commit v2 on v1

--- a/solution.py
+++ b/solution.py
@@ -20,12 +20,24 @@
     return lax.ppermute(value, "mp", [(i, (i + step) % count) for i in range(count)])
 
 
+def far_first(count):
+    return sorted(range(1, count), key=lambda s: (-min(s, count - s), -s))
+
+
+def exchange(parts, sign):
+    count = lax.axis_size("mp")
+    results = [parts[0]] + [None] * (count - 1)
+    for s in far_first(count):
+        results[s] = shift(parts[s], s * sign)
+    return results
+
+
 def spread(value):
-    return [value] + [shift(value, s) for s in range(1, lax.axis_size("mp"))]
+    return exchange([value] * lax.axis_size("mp"), 1)
 
 
 def collect(parts):
-    return [parts[0]] + [shift(parts[s], -s) for s in range(1, lax.axis_size("mp"))]
+    return exchange(parts, -1)
 
 
 def total(parts):
@@ -35,7 +47,7 @@
     return result
 
 
-def local(
+def layer(
     candidates,
     owner_row,
     selected,
@@ -66,16 +78,11 @@
     senders = lax.dynamic_slice_in_dim(source_owner, own_index * SEL_DEV, SEL_DEV)
     own_pixels = jnp.take(incoming, senders, axis=0)
 
-    weight_parts = [patch_weight]
-    position_parts = [lax.dynamic_slice_in_dim(positions, own_group * quarter, quarter, 0)]
-    for s in range(1, groups):
+    bundles = []
+    for s in range(groups):
         rows = lax.dynamic_slice_in_dim(positions, ((own_group + s) % groups) * quarter, quarter, 0)
-        both = shift(jnp.concatenate([patch_weight, rows], axis=0), s)
-        weight_parts.append(both[:pixel_width])
-        position_parts.append(both[pixel_width:])
-    stack = jnp.stack(
-        [jnp.concatenate([w, p], axis=0) for w, p in zip(weight_parts, position_parts)]
-    )
+        bundles.append(jnp.concatenate([patch_weight, rows], axis=0))
+    stack = jnp.stack(exchange(bundles, 1))
     whole = jnp.concatenate(
         [
             lax.dynamic_index_in_dim(stack, (own_group - j) % groups, 0, keepdims=False)
@@ -114,23 +121,21 @@
     )
     after_attn = activations + attended
     normed2 = norm_rows(after_attn, mlp_gain).astype(jnp.bfloat16)
-    down_terms = []
-    for part in spread(normed2):
-        hidden = jax.nn.gelu(
-            jnp.einsum("btd,df->btf", part, up_weight, preferred_element_type=jnp.float32),
-            approximate=False,
-        ).astype(jnp.bfloat16)
-        down_terms.append(
-            jnp.einsum(
-                "btf,fd->btd", hidden, down_weight, preferred_element_type=jnp.float32
-            ).astype(jnp.bfloat16)
-        )
-    return (after_attn + total(collect(down_terms))).astype(jnp.bfloat16)
+    tokens2 = jnp.concatenate(spread(normed2), axis=1)
+    hidden = jax.nn.gelu(
+        jnp.einsum("btd,df->btf", tokens2, up_weight, preferred_element_type=jnp.float32),
+        approximate=False,
+    ).astype(jnp.bfloat16)
+    down_terms = jnp.einsum(
+        "btf,fd->btd", hidden, down_weight, preferred_element_type=jnp.float32
+    ).astype(jnp.bfloat16)
+    feed = total(collect([down_terms[:, s * quarter : (s + 1) * quarter] for s in range(groups)]))
+    return (after_attn + feed).astype(jnp.bfloat16)
 
 
 def solution(mesh):
     return jax.shard_map(
-        local,
+        layer,
         mesh=mesh,
         in_specs=(
             P("dp", "mp", None),

time: 130 us -> 133 us (1.023)
  waiting for transfers between devices: 59.5 us -> 70.8 us
  starting transfers between devices: 45.8 us -> 37.9 us
    ppermute x15, waiting for transfers between devices: 59.5 us -> 70.8 us  [shift(): lax.ppermute(value, 'mp', [(i, (i + step) % count) for i in range(count)])]
    ppermute x15, starting transfers between devices: 41.6 us -> 33.6 us  [shift(): lax.ppermute(value, 'mp', [(i, (i + step) % count) for i in range(count)])]
    dot_general x12 -> x6, matrix products: 10.5 us -> 9.22 us  [the longest x1 4.42 us: layer(): jnp.einsum('btf,fd->btd', hidden, down_weight, preferred_element_type=jnp...]
  transfers between devices with their start and end apart: 16 -> 16, of which waited for: 8 -> 9; matrix products, arithmetic and copies ran while one was open for 9% -> 5% of each run, Pallas kernels for 0% -> 0%
where the time goes in v2:
time: 133 us
  waiting for transfers between devices  70.8 us (53%)
  starting transfers between devices  37.9 us (28%)
  matrix products  9.89 us (7%)
  other arithmetic  8.08 us (6%)
  local copies, waits for them, and re-layouts  5.88 us (4%)
    ppermute x15, waiting for transfers between devices, shift(): lax.ppermute(value, 'mp', [(i, (i + step) % count) for i in range(count)])  70.8 us
    ppermute x15, starting transfers between devices, shift(): lax.ppermute(value, 'mp', [(i, (i + step) % count) for i in range(count)])  33.6 us
    dot_general x1, matrix products, layer(): jnp.einsum('btf,fd->btd', hidden, down_weight, preferred_element_type=jnp...  4.42 us
    all_to_all x1, starting transfers between devices, layer(): lax.all_to_all(outgoing, 'dp', split_axis=0, concat_axis=0, tiled=True)  4.22 us
    another operation x2, other arithmetic, layer(): stack = jnp.stack(exchange(bundles, 1))  3.41 us
  transfers between devices with their start and end apart: 16, of which 9 were waited for; matrix products, arithmetic and copies ran while one was open for 5% of the time, Pallas kernels for 0%

profile of v2, /device:TPU:0, one launch (start us, length us, event | category | flops | bytes accessed | tf_op | source)
XLA Modules:
  0.0 132.9 jit_solution(5020988755827445049)
XLA Ops:
  0.1 1.1 constant_dynamic-slice_fusion.7
  1.2 2.0 %maximum_bitcast_fusion.2 = (bf16[1,832,192]{1,2,0:T(8,128)(2,1)S(1)}, bf16[832,192]{0,1:T(8,128)(2,1)}, bf16[832,192]{0,1:T(8,128)(2,1)}, bf16[832,192]{0,1:T(8,128)(2,1)S(1)}) fusion(bf16[64,192]{0,1:T(8,128)(2,1)S(1)} %get-tuple-element.27, bf16[768,192]{0,1:T(8,128)(2,1)} %param.16, bf16[64,192]{0,1:T(8,128)(2,1)S(1)} %get-tuple-element.28, ...), kind=kLoop, calls=%fused_computation.99 | loop fusion | flops 2076672 | bytes 1671168 | tf_op jit(solution)/shard_map/stack | solution.py:85
  3.2 3.1 %collective-permute-start = (bf16[832,192]{0,1:T(8,128)(2,1)}, bf16[832,192]{0,1:T(8,128)(2,1)}, u32[]{:S(2)}, u32[]{:S(2)}) collective-permute-start(bf16[832,192]{0,1:T(8,128)(2,1)} %get-tuple-element.24), channel_id=1, source_target_pairs={{0,1},{1,2},{2,3},{3,0},{4,5},{5,6},{6,7},{7,4},{8,9},{9,10},{10,1... | collective-permute-start | bytes 958472 | tf_op jit(solution)/shard_map/ppermute | solution.py:20
  6.2 2.6 %collective-permute-start.1 = (bf16[832,192]{0,1:T(8,128)(2,1)}, bf16[832,192]{0,1:T(8,128)(2,1)}, u32[]{:S(2)}, u32[]{:S(2)}) collective-permute-start(bf16[832,192]{0,1:T(8,128)(2,1)} %get-tuple-element.25), channel_id=1, source_target_pairs={{0,2},{1,3},{2,0},{3,1},{4,6},{5,7},{6,4},{7,5},{8,10},{9,11},{10,... | collective-permute-start | bytes 958472 | tf_op jit(solution)/shard_map/ppermute | solution.py:20
  8.8 1.3 %collective-permute-start.2 = (bf16[832,192]{0,1:T(8,128)(2,1)S(1)}, bf16[832,192]{0,1:T(8,128)(2,1)}, u32[]{:S(2)}, u32[]{:S(2)}) collective-permute-start(bf16[832,192]{0,1:T(8,128)(2,1)S(1)} %get-tuple-element.26), channel_id=1, source_target_pairs={{0,3},{1,0},{2,1},{3,2},{4,7},{5,4},{6,5},{7,6},{8,11},{9,8},{10,9... | collective-permute-start | bytes 958472 | tf_op jit(solution)/shard_map/ppermute | solution.py:20
  10.2 0.7 gather_fusion
  10.9 0.6 scatter_custom_fusion
  11.5 0.1 select_n.127
  11.6 0.1 reduce_sum.56
  11.8 0.6 gather_fusion.1
  12.4 0.0 copy-start.4
  12.4 1.0 broadcast_select_fusion
  13.4 4.2 %all-to-all-start = ((bf16[8,64,768]{2,1,0:T(8,128)(2,1)}), bf16[8,64,768]{2,1,0:T(8,128)(2,1)}, u32[]{:S(2)}, u32[]{:S(2)}) async-start(bf16[8,64,768]{2,1,0:T(8,128)(2,1)} %broadcast_select_fusion), calls=%async_computation | async-start | bytes 1572864 | tf_op jit(solution)/shard_map/all_to_all | solution.py:77
  17.7 0.1 compare_and_fusion.1
  17.8 0.0 collective-permute-done
  17.8 13.7 %collective-permute-done.1 = bf16[832,192]{0,1:T(8,128)(2,1)} collective-permute-done((bf16[832,192]{0,1:T(8,128)(2,1)}, bf16[832,192]{0,1:T(8,128)(2,1)}, u32[]{:S(2)}, u32[]{:S(2)}) %collective-permute-start.1) | collective-permute-done | bytes 319520 | tf_op jit(solution)/shard_map/ppermute | solution.py:20
  31.5 1.4 %pad_maximum_fusion = bf16[4,832,192]{1,2,0:T(8,128)(2,1)S(1)} fusion(bf16[1,832,192]{1,2,0:T(8,128)(2,1)} %bitcast.5, bf16[1,832,192]{1,2,0:T(8,128)(2,1)} %bitcast.4, bf16[1,832,192]{1,2,0:T(8,128)(2,1)} %bitcast.3, bf16[1,832,192]{1,2,0:T(8,128)(2,1)S(1)} %get-tuple-element.23), kind=kLoop, calls=%fused_computation.33 | loop fusion | flops 1916928 | bytes 2555904 | tf_op jit(solution)/shard_map/stack | solution.py:85
  33.0 0.1 constant_dynamic-slice_fusion.3
  33.1 0.2 copy.21
  33.3 0.2 copy.22
  33.5 0.2 copy.23
  33.7 0.2 copy.24
  33.9 0.1 maximum_convert_fusion
  34.0 1.6 %pad_maximum_fusion.1 = bf16[832,768]{1,0:T(8,128)(2,1)} fusion(bf16[832,192]{1,0:T(8,128)(2,1)S(1)} %bitcast.88, bf16[832,192]{1,0:T(8,128)(2,1)S(1)} %bitcast.86, bf16[832,192]{1,0:T(8,128)(2,1)S(1)} %bitcast.84, bf16[832,192]{1,0:T(8,128)(2,1)S(1)} %bitcast.82), kind=kLoop, calls=%fused_computation.35 | loop fusion | flops 5111808 | bytes 2555904 | tf_op jit(solution)/shard_map/concatenate | solution.py:86
  35.6 1.7 %gather_fusion.2 = bf16[2,64,768]{2,1,0:T(8,128)(2,1)S(1)} fusion(bf16[8,64,768]{2,1,0:T(8,128)(2,1)} %all-to-all-done, s32[1024]{0:T(1024)S(1)} %pad_clamp_fusion), kind=kCustom, calls=%fused_computation.2 | custom fusion | bytes 393224 | tf_op jit(solution)/shard_map/jit(_take)/gather | solution.py:79
  37.3 0.0 copy-start.9
  37.3 1.8 %fusion.116 = (f32[2,64]{1,0:T(2,128)S(1)}, f32[2,64,768]{2,1,0:T(8,128)S(1)}) fusion(f32[64,768]{1,0:T(8,128)S(1)} %maximum_convert_fusion, bf16[832,768]{1,0:T(8,128)(2,1)} %pad_maximum_fusion.1, bf16[2,64,768]{2,1,0:T(8,128)(2,1)S(1)} %gather_fusion.2, pred[2]{0:T(512)(128)(4,1)S(1)} %get-tuple-element.9), kind=kOutput, calls=%fused_computation.186 | convolution fusion | flops 151486336 | bytes 1966594 | tf_op jit(solution)/shard_map/brp,pe->bre/dot_general | solution.py:93
  39.1 0.2 multiply_reduce_fusion.1
  39.3 0.1 multiply_convert_fusion.1
  39.5 7.9 %collective-permute-start.3 = (bf16[2,64,768]{2,1,0:T(8,128)(2,1)S(1)}, bf16[2,64,768]{2,1,0:T(8,128)(2,1)S(1)}, u32[]{:S(2)}, u32[]{:S(2)}) collective-permute-start(bf16[2,64,768]{2,1,0:T(8,128)(2,1)S(1)} %multiply_convert_fusion.1), channel_id=1, source_target_pairs={{0,1},{1,2},{2,3},{3,0},{4,5},{5,6},{6,7},{7,4},{8,9},{9,10},{10,1... | collective-permute-start | bytes 589832 | tf_op jit(solution)/shard_map/ppermute | solution.py:20
  47.4 1.6 %collective-permute-start.4 = (bf16[2,64,768]{2,1,0:T(8,128)(2,1)S(1)}, bf16[2,64,768]{2,1,0:T(8,128)(2,1)S(1)}, u32[]{:S(2)}, u32[]{:S(2)}) collective-permute-start(bf16[2,64,768]{2,1,0:T(8,128)(2,1)S(1)} %multiply_convert_fusion.1), channel_id=1, source_target_pairs={{0,2},{1,3},{2,0},{3,1},{4,6},{5,7},{6,4},{7,5},{8,10},{9,11},{10,... | collective-permute-start | bytes 589832 | tf_op jit(solution)/shard_map/ppermute | solution.py:20
  49.0 0.8 collective-permute-start.5
  49.8 4.4 %collective-permute-done.3 = bf16[2,64,768]{2,1,0:T(8,128)(2,1)S(1)} collective-permute-done((bf16[2,64,768]{2,1,0:T(8,128)(2,1)S(1)}, bf16[2,64,768]{2,1,0:T(8,128)(2,1)S(1)}, u32[]{:S(2)}, u32[]{:S(2)}) %collective-permute-start.3) | collective-permute-done | bytes 196640 | tf_op jit(solution)/shard_map/ppermute | solution.py:20
  54.3 6.7 %collective-permute-done.4 = bf16[2,64,768]{2,1,0:T(8,128)(2,1)S(1)} collective-permute-done((bf16[2,64,768]{2,1,0:T(8,128)(2,1)S(1)}, bf16[2,64,768]{2,1,0:T(8,128)(2,1)S(1)}, u32[]{:S(2)}, u32[]{:S(2)}) %collective-permute-start.4) | collective-permute-done | bytes 196640 | tf_op jit(solution)/shard_map/ppermute | solution.py:20
  61.0 0.7 convolution_convert_fusion.2
  61.6 0.7 fusion.117
  62.3 0.9 convolution_convert_fusion.3
  63.2 0.0 copy-start.5
  63.2 0.1 copy-done.3
  63.3 0.4 convolution_convert_fusion.1
  63.7 6.6 %collective-permute-start.6 = (bf16[2,64,768]{2,1,0:T(8,128)(2,1)S(1)}, bf16[2,64,768]{2,1,0:T(8,128)(2,1)S(1)}, u32[]{:S(2)}, u32[]{:S(2)}) collective-permute-start(bf16[2,64,768]{2,1,0:T(8,128)(2,1)S(1)} %get-tuple-element.20), channel_id=1, source_target_pairs={{0,3},{1,0},{2,1},{3,2},{4,7},{5,4},{6,5},{7,6},{8,11},{9,8},{10,9... | collective-permute-start | bytes 589832 | tf_op jit(solution)/shard_map/ppermute | solution.py:20
  70.3 0.0 collective-permute-start.7
  70.3 0.6 collective-permute-start.8
  70.9 4.7 %collective-permute-done.6 = bf16[2,64,768]{2,1,0:T(8,128)(2,1)S(1)} collective-permute-done((bf16[2,64,768]{2,1,0:T(8,128)(2,1)S(1)}, bf16[2,64,768]{2,1,0:T(8,128)(2,1)S(1)}, u32[]{:S(2)}, u32[]{:S(2)}) %collective-permute-start.6) | collective-permute-done | bytes 196640 | tf_op jit(solution)/shard_map/ppermute | solution.py:20
  75.6 11.7 %collective-permute-done.7 = bf16[2,64,768]{2,1,0:T(8,128)(2,1)S(1)} collective-permute-done((bf16[2,64,768]{2,1,0:T(8,128)(2,1)S(1)}, bf16[2,64,768]{2,1,0:T(8,128)(2,1)S(1)}, u32[]{:S(2)}, u32[]{:S(2)}) %collective-permute-start.7) | collective-permute-done | bytes 196640 | tf_op jit(solution)/shard_map/ppermute | solution.py:20
  87.4 0.0 collective-permute-done.8
  87.4 0.2 fusion.113
  87.6 0.2 multiply_reduce_fusion
  87.8 0.1 multiply_convert_fusion
  87.9 0.0 copy-start.8
  87.9 2.0 %collective-permute-start.10 = (bf16[2,64,768]{2,1,0:T(8,128)(2,1)S(1)}, bf16[2,64,768]{2,1,0:T(8,128)(2,1)S(1)}, u32[]{:S(2)}, u32[]{:S(2)}) collective-permute-start(bf16[2,64,768]{2,1,0:T(8,128)(2,1)S(1)} %multiply_convert_fusion), channel_id=1, source_target_pairs={{0,2},{1,3},{2,0},{3,1},{4,6},{5,7},{6,4},{7,5},{8,10},{9,11},{10,... | collective-permute-start | bytes 589832 | tf_op jit(solution)/shard_map/ppermute | solution.py:20
  89.9 0.4 collective-permute-start.11
  90.4 1.6 %collective-permute-start.9 = (bf16[2,64,768]{2,1,0:T(8,128)(2,1)S(1)}, bf16[2,64,768]{2,1,0:T(8,128)(2,1)S(1)}, u32[]{:S(2)}, u32[]{:S(2)}) collective-permute-start(bf16[2,64,768]{2,1,0:T(8,128)(2,1)S(1)} %multiply_convert_fusion), channel_id=1, source_target_pairs={{0,1},{1,2},{2,3},{3,0},{4,5},{5,6},{6,7},{7,4},{8,9},{9,10},{10,1... | collective-permute-start | bytes 589832 | tf_op jit(solution)/shard_map/ppermute | solution.py:20
  92.0 11.0 %collective-permute-done.10 = bf16[2,64,768]{2,1,0:T(8,128)(2,1)S(1)} collective-permute-done((bf16[2,64,768]{2,1,0:T(8,128)(2,1)S(1)}, bf16[2,64,768]{2,1,0:T(8,128)(2,1)S(1)}, u32[]{:S(2)}, u32[]{:S(2)}) %collective-permute-start.10) | collective-permute-done | bytes 196640 | tf_op jit(solution)/shard_map/ppermute | solution.py:20
  102.9 1.1 collective-permute-done.11
  104.0 0.0 collective-permute-done.9
  104.0 1.1 fusion.64
  105.1 4.4 %convolution_convert_fusion = bf16[2,256,768]{2,1,0:T(8,128)(2,1)S(1)} fusion(bf16[768,768]{1,0:T(8,128)(2,1)S(1)} %copy-done.8, f32[2,256,768]{2,1,0:T(8,128)S(1)} %get-tuple-element.33, u8[256,768]{1,0:T(8,128)(4,1)S(1)} %get-tuple-element.6, u8[256,768]{1,0:T(8,128)(4,1)S(1)} %get-tuple-element.5), kind=kOutput, calls=%fused_computation.31 | convolution fusion | flops 631898112 | bytes 3932160 | tf_op jit(solution)/shard_map/btf,fd->btd/dot_general | solution.py:129
  109.6 0.1 collective-permute-start.12
  109.7 5.0 %collective-permute-start.13 = (bf16[2,64,768]{2,1,0:T(8,128)(2,1)S(1)}, bf16[2,64,768]{2,1,0:T(8,128)(2,1)S(1)}, u32[]{:S(2)}, u32[]{:S(2)}) collective-permute-start(bf16[2,64,768]{2,1,0:T(8,128)(2,1)S(1)} %get-tuple-element.19), channel_id=1, source_target_pairs={{0,2},{1,3},{2,0},{3,1},{4,6},{5,7},{6,4},{7,5},{8,10},{9,11},{10,... | collective-permute-start | bytes 589832 | tf_op jit(solution)/shard_map/ppermute | solution.py:20
  114.7 3.6 %collective-permute-done.12 = bf16[2,64,768]{2,1,0:T(8,128)(2,1)S(1)} collective-permute-done((bf16[2,64,768]{2,1,0:T(8,128)(2,1)S(1)}, bf16[2,64,768]{2,1,0:T(8,128)(2,1)S(1)}, u32[]{:S(2)}, u32[]{:S(2)}) %collective-permute-start.12) | collective-permute-done | bytes 196640 | tf_op jit(solution)/shard_map/ppermute | solution.py:20
  118.3 13.8 %collective-permute-done.13 = bf16[2,64,768]{2,1,0:T(8,128)(2,1)S(1)} collective-permute-done((bf16[2,64,768]{2,1,0:T(8,128)(2,1)S(1)}, bf16[2,64,768]{2,1,0:T(8,128)(2,1)S(1)}, u32[]{:S(2)}, u32[]{:S(2)}) %collective-permute-start.13) | collective-permute-done | bytes 196640 | tf_op jit(solution)/shard_map/ppermute | solution.py:20
  132.1 0.0 collective-permute-done.14
  132.1 0.8 add_convert_fusion
  (35 shorter events, 0.2 us)
Async XLA Ops:
  0.0 104.0 %copy-start = (bf16[768,768]{1,0:T(8,128)(2,1)S(1)}, bf16[768,768]{1,0:T(8,128)(2,1)}, u32[]{:S(2)}) copy-start(bf16[768,768]{1,0:T(8,128)(2,1)} %param.22) | copy-start | bytes 3538948
  0.0 10.2 %copy-start.7 = (s32[16]{0:T(128)S(1)}, s32[16]{0:T(128)}, u32[]{:S(2)}) copy-start(s32[16]{0:T(128)} %param.14) | copy-start | bytes 196
  0.0 10.2 %copy-start.6 = (s32[16]{0:T(128)S(1)}, s32[16]{0:T(128)}, u32[]{:S(2)}) copy-start(s32[16]{0:T(128)} %param.15) | copy-start | bytes 196
  0.0 10.2 %copy-start.1 = (s32[64]{0:T(128)S(1)}, s32[64]{0:T(128)}, u32[]{:S(2)}) copy-start(s32[64]{0:T(128)} %param.13) | copy-start | bytes 772
  0.0 11.8 %copy-start.2 = (bf16[8,64,768]{2,1,0:T(8,128)(2,1)S(1)}, bf16[8,64,768]{2,1,0:T(8,128)(2,1)}, u32[]{:S(2)}) copy-start(bf16[8,64,768]{2,1,0:T(8,128)(2,1)} %param.12) | copy-start | bytes 2359300
  3.2 14.6 %collective-permute-start = (bf16[832,192]{0,1:T(8,128)(2,1)}, bf16[832,192]{0,1:T(8,128)(2,1)}, u32[]{:S(2)}, u32[]{:S(2)}) collective-permute-start(bf16[832,192]{0,1:T(8,128)(2,1)} %get-tuple-element.24), channel_id=1, source_target_pairs={{0,1},{1,2},{2,3},{3,0},{4,5},{5,6},{6,7},{7,4},{8,9},{9,10},{10,1... | collective-permute-start | bytes 958472 | tf_op jit(solution)/shard_map/ppermute | solution.py:20
  6.2 25.3 %collective-permute-start.1 = (bf16[832,192]{0,1:T(8,128)(2,1)}, bf16[832,192]{0,1:T(8,128)(2,1)}, u32[]{:S(2)}, u32[]{:S(2)}) collective-permute-start(bf16[832,192]{0,1:T(8,128)(2,1)} %get-tuple-element.25), channel_id=1, source_target_pairs={{0,2},{1,3},{2,0},{3,1},{4,6},{5,7},{6,4},{7,5},{8,10},{9,11},{10,... | collective-permute-start | bytes 958472 | tf_op jit(solution)/shard_map/ppermute | solution.py:20
  8.8 22.7 %collective-permute-start.2 = (bf16[832,192]{0,1:T(8,128)(2,1)S(1)}, bf16[832,192]{0,1:T(8,128)(2,1)}, u32[]{:S(2)}, u32[]{:S(2)}) collective-permute-start(bf16[832,192]{0,1:T(8,128)(2,1)S(1)} %get-tuple-element.26), channel_id=1, source_target_pairs={{0,3},{1,0},{2,1},{3,2},{4,7},{5,4},{6,5},{7,6},{8,11},{9,8},{10,9... | collective-permute-start | bytes 958472 | tf_op jit(solution)/shard_map/ppermute | solution.py:20
  12.4 5.4 %copy-start.4 = (bf16[768]{0:T(1024)(128)(2,1)S(1)}, bf16[768]{0:T(1024)(128)(2,1)}, u32[]{:S(2)}) copy-start(bf16[768]{0:T(1024)(128)(2,1)} %param.20) | copy-start | bytes 4612
  13.4 22.2 %all-to-all-start = ((bf16[8,64,768]{2,1,0:T(8,128)(2,1)}), bf16[8,64,768]{2,1,0:T(8,128)(2,1)}, u32[]{:S(2)}, u32[]{:S(2)}) async-start(bf16[8,64,768]{2,1,0:T(8,128)(2,1)} %broadcast_select_fusion), calls=%async_computation | async-start | bytes 1572864 | tf_op jit(solution)/shard_map/all_to_all | solution.py:77
  37.3 23.7 %copy-start.9 = (bf16[768,3,192]{0,2,1:T(8,128)(2,1)S(1)}, bf16[768,3,192]{0,2,1:T(8,128)(2,1)}, u32[]{:S(2)}) copy-start(bf16[768,3,192]{0,2,1:T(8,128)(2,1)} %param.18) | copy-start | bytes 2654212
  39.5 14.8 %collective-permute-start.3 = (bf16[2,64,768]{2,1,0:T(8,128)(2,1)S(1)}, bf16[2,64,768]{2,1,0:T(8,128)(2,1)S(1)}, u32[]{:S(2)}, u32[]{:S(2)}) collective-permute-start(bf16[2,64,768]{2,1,0:T(8,128)(2,1)S(1)} %multiply_convert_fusion.1), channel_id=1, source_target_pairs={{0,1},{1,2},{2,3},{3,0},{4,5},{5,6},{6,7},{7,4},{8,9},{9,10},{10,1... | collective-permute-start | bytes 589832 | tf_op jit(solution)/shard_map/ppermute | solution.py:20
  47.4 13.6 %collective-permute-start.4 = (bf16[2,64,768]{2,1,0:T(8,128)(2,1)S(1)}, bf16[2,64,768]{2,1,0:T(8,128)(2,1)S(1)}, u32[]{:S(2)}, u32[]{:S(2)}) collective-permute-start(bf16[2,64,768]{2,1,0:T(8,128)(2,1)S(1)} %multiply_convert_fusion.1), channel_id=1, source_target_pairs={{0,2},{1,3},{2,0},{3,1},{4,6},{5,7},{6,4},{7,5},{8,10},{9,11},{10,... | collective-permute-start | bytes 589832 | tf_op jit(solution)/shard_map/ppermute | solution.py:20
  49.0 12.0 %collective-permute-start.5 = (bf16[2,64,768]{2,1,0:T(8,128)(2,1)S(1)}, bf16[2,64,768]{2,1,0:T(8,128)(2,1)S(1)}, u32[]{:S(2)}, u32[]{:S(2)}) collective-permute-start(bf16[2,64,768]{2,1,0:T(8,128)(2,1)S(1)} %multiply_convert_fusion.1), channel_id=1, source_target_pairs={{0,3},{1,0},{2,1},{3,2},{4,7},{5,4},{6,5},{7,6},{8,11},{9,8},{10,9... | collective-permute-start | bytes 589832 | tf_op jit(solution)/shard_map/ppermute | solution.py:20
  62.3 1.0 copy-start.3
  63.2 7.7 %copy-start.5 = (bf16[768]{0:T(1024)(128)(2,1)S(1)}, bf16[768]{0:T(1024)(128)(2,1)}, u32[]{:S(2)}) copy-start(bf16[768]{0:T(1024)(128)(2,1)} %param.21) | copy-start | bytes 4612
  63.7 11.9 %collective-permute-start.6 = (bf16[2,64,768]{2,1,0:T(8,128)(2,1)S(1)}, bf16[2,64,768]{2,1,0:T(8,128)(2,1)S(1)}, u32[]{:S(2)}, u32[]{:S(2)}) collective-permute-start(bf16[2,64,768]{2,1,0:T(8,128)(2,1)S(1)} %get-tuple-element.20), channel_id=1, source_target_pairs={{0,3},{1,0},{2,1},{3,2},{4,7},{5,4},{6,5},{7,6},{8,11},{9,8},{10,9... | collective-permute-start | bytes 589832 | tf_op jit(solution)/shard_map/ppermute | solution.py:20
  70.3 17.1 %collective-permute-start.7 = (bf16[2,64,768]{2,1,0:T(8,128)(2,1)S(1)}, bf16[2,64,768]{2,1,0:T(8,128)(2,1)S(1)}, u32[]{:S(2)}, u32[]{:S(2)}) collective-permute-start(bf16[2,64,768]{2,1,0:T(8,128)(2,1)S(1)} %get-tuple-element.22), channel_id=1, source_target_pairs={{0,2},{1,3},{2,0},{3,1},{4,6},{5,7},{6,4},{7,5},{8,10},{9,11},{10,... | collective-permute-start | bytes 589832 | tf_op jit(solution)/shard_map/ppermute | solution.py:20
  70.3 17.1 %collective-permute-start.8 = (bf16[2,64,768]{2,1,0:T(8,128)(2,1)S(1)}, bf16[2,64,768]{2,1,0:T(8,128)(2,1)S(1)}, u32[]{:S(2)}, u32[]{:S(2)}) collective-permute-start(bf16[2,64,768]{2,1,0:T(8,128)(2,1)S(1)} %get-tuple-element.21), channel_id=1, source_target_pairs={{0,1},{1,2},{2,3},{3,0},{4,5},{5,6},{6,7},{7,4},{8,9},{9,10},{10,1... | collective-permute-start | bytes 589832 | tf_op jit(solution)/shard_map/ppermute | solution.py:20
  87.9 17.1 %copy-start.8 = (bf16[768,768]{1,0:T(8,128)(2,1)S(1)}, bf16[768,768]{1,0:T(8,128)(2,1)}, u32[]{:S(2)}) copy-start(bf16[768,768]{1,0:T(8,128)(2,1)} %param.23) | copy-start | bytes 3538948
  87.9 15.0 %collective-permute-start.10 = (bf16[2,64,768]{2,1,0:T(8,128)(2,1)S(1)}, bf16[2,64,768]{2,1,0:T(8,128)(2,1)S(1)}, u32[]{:S(2)}, u32[]{:S(2)}) collective-permute-start(bf16[2,64,768]{2,1,0:T(8,128)(2,1)S(1)} %multiply_convert_fusion), channel_id=1, source_target_pairs={{0,2},{1,3},{2,0},{3,1},{4,6},{5,7},{6,4},{7,5},{8,10},{9,11},{10,... | collective-permute-start | bytes 589832 | tf_op jit(solution)/shard_map/ppermute | solution.py:20
  89.9 14.1 %collective-permute-start.11 = (bf16[2,64,768]{2,1,0:T(8,128)(2,1)S(1)}, bf16[2,64,768]{2,1,0:T(8,128)(2,1)S(1)}, u32[]{:S(2)}, u32[]{:S(2)}) collective-permute-start(bf16[2,64,768]{2,1,0:T(8,128)(2,1)S(1)} %multiply_convert_fusion), channel_id=1, source_target_pairs={{0,3},{1,0},{2,1},{3,2},{4,7},{5,4},{6,5},{7,6},{8,11},{9,8},{10,9... | collective-permute-start | bytes 589832 | tf_op jit(solution)/shard_map/ppermute | solution.py:20
  90.4 13.6 %collective-permute-start.9 = (bf16[2,64,768]{2,1,0:T(8,128)(2,1)S(1)}, bf16[2,64,768]{2,1,0:T(8,128)(2,1)S(1)}, u32[]{:S(2)}, u32[]{:S(2)}) collective-permute-start(bf16[2,64,768]{2,1,0:T(8,128)(2,1)S(1)} %multiply_convert_fusion), channel_id=1, source_target_pairs={{0,1},{1,2},{2,3},{3,0},{4,5},{5,6},{6,7},{7,4},{8,9},{9,10},{10,1... | collective-permute-start | bytes 589832 | tf_op jit(solution)/shard_map/ppermute | solution.py:20
  109.6 8.7 %collective-permute-start.12 = (bf16[2,64,768]{2,1,0:T(8,128)(2,1)S(1)}, bf16[2,64,768]{2,1,0:T(8,128)(2,1)S(1)}, u32[]{:S(2)}, u32[]{:S(2)}) collective-permute-start(bf16[2,64,768]{2,1,0:T(8,128)(2,1)S(1)} %get-tuple-element.17), channel_id=1, source_target_pairs={{0,3},{1,0},{2,1},{3,2},{4,7},{5,4},{6,5},{7,6},{8,11},{9,8},{10,9... | collective-permute-start | bytes 589832 | tf_op jit(solution)/shard_map/ppermute | solution.py:20
  109.7 22.4 %collective-permute-start.13 = (bf16[2,64,768]{2,1,0:T(8,128)(2,1)S(1)}, bf16[2,64,768]{2,1,0:T(8,128)(2,1)S(1)}, u32[]{:S(2)}, u32[]{:S(2)}) collective-permute-start(bf16[2,64,768]{2,1,0:T(8,128)(2,1)S(1)} %get-tuple-element.19), channel_id=1, source_target_pairs={{0,2},{1,3},{2,0},{3,1},{4,6},{5,7},{6,4},{7,5},{8,10},{9,11},{10,... | collective-permute-start | bytes 589832 | tf_op jit(solution)/shard_map/ppermute | solution.py:20
  114.7 17.4 %collective-permute-start.14 = (bf16[2,64,768]{2,1,0:T(8,128)(2,1)S(1)}, bf16[2,64,768]{2,1,0:T(8,128)(2,1)S(1)}, u32[]{:S(2)}, u32[]{:S(2)}) collective-permute-start(bf16[2,64,768]{2,1,0:T(8,128)(2,1)S(1)} %get-tuple-element.18), channel_id=1, source_target_pairs={{0,1},{1,2},{2,3},{3,0},{4,5},{5,6},{6,7},{7,4},{8,9},{9,10},{10,1... | collective-permute-start | bytes 589832 | tf_op jit(solution)/shard_map/ppermute | solution.py:20

commit v3 on v0

v3 whole, which is shorter than its diff:
```python
import jax
import jax.numpy as jnp
from jax import lax
from jax.experimental import pallas as pl
from jax.experimental.pallas import tpu as pltpu
from jax.sharding import PartitionSpec as P

CAND_DEV = 8
SEL_DEV = 2
HEAD_DIM = 64
SPREAD = 8
BF16 = jnp.bfloat16
F32 = jnp.float32


def norm_rows(values, gain):
    average = jnp.mean(values, axis=-1, keepdims=True)
    centred = values - average
    variance = jnp.mean(centred * centred, axis=-1, keepdims=True)
    return centred * lax.rsqrt(variance + 1e-06) * gain.astype(F32)


def swap(value, axis, bits):
    return lax.ppermute(value, axis, [(i, i ^ bits) for i in range(lax.axis_size(axis))])


def dot(left, right):
    return jnp.dot(left, right, preferred_element_type=F32)


ANY = pl.BlockSpec(memory_space=pl.ANY)
SCALARS = pl.BlockSpec(memory_space=pltpu.SMEM)
FAST = pl.BlockSpec(memory_space=pltpu.VMEM)
UNIT = 128
SMALL = pltpu.CompilerParams(vmem_limit_bytes=4 * 1024 * 1024)


def copier(body, outs, where, *operands):
    return pl.pallas_call(
        body,
        in_specs=[SCALARS] + [FAST] * len(operands),
        out_specs=tuple(FAST for _ in outs),
        out_shape=tuple(pltpu.VMEM(shape, BF16) for shape in outs),
        compiler_params=SMALL,
    )(where, *(pltpu.with_memory_space_constraint(x, pltpu.VMEM) for x in operands))


def route_kernel(own, owner_row, selected, dest_slot, candidates, outgoing, senders, sem):
    me = own[0]

    def visit(i, sent):
        row = owner_row[selected[i]]
        owner = row // CAND_DEV
        slot = dest_slot[i]

        @pl.when(slot // SEL_DEV == me)
        def _():
            senders[slot % SEL_DEV] = owner

        @pl.when(owner == me)
        def _():
            pltpu.make_async_copy(
                candidates.at[row % CAND_DEV], outgoing.at[slot // SEL_DEV], sem.at[0]
            ).start()

        return sent + (owner == me).astype(jnp.int32)

    sent = lax.fori_loop(0, selected.shape[0], visit, 0)

    def finish(_, carry):
        pltpu.make_async_copy(candidates.at[0], outgoing.at[0], sem.at[0]).wait()
        return carry

    lax.fori_loop(0, sent, finish, 0)


def route(owner_row, selected, dest_slot, candidates):
    learners = lax.axis_size("dp")
    own = jnp.full((1,), lax.axis_index("dp"), jnp.int32)
    return pl.pallas_call(
        route_kernel,
        in_specs=[SCALARS] * 4 + [ANY],
        out_specs=(FAST, SCALARS),
        out_shape=(
            jax.ShapeDtypeStruct((learners,) + candidates.shape[1:], BF16),
            jax.ShapeDtypeStruct((SEL_DEV,), jnp.int32),
        ),
        scratch_shapes=[pltpu.SemaphoreType.DMA((1,))],
    )(own, owner_row, selected, dest_slot, candidates)


def attn_unit(array, unit):
    columns = array.shape[1] // UNIT
    rows = array.shape[0] // 4
    return (
        pl.ds(pl.multiple_of((unit // columns) * rows, rows), rows),
        pl.ds(pl.multiple_of((unit % columns) * UNIT, UNIT), UNIT),
    )


def lanes(index):
    return pl.ds(pl.multiple_of(index * UNIT, UNIT), UNIT)


def block(index, size):
    return pl.ds(pl.multiple_of(index * size, size), size)


def extract_kernel(where, embed, attn, up, down, embed_piece, both_piece, mlp_piece, sem):
    piece = where[0]
    rows = embed.shape[0]
    size = up.shape[0] // SPREAD
    copies = [
        pltpu.make_async_copy(up.at[block(piece, size)], mlp_piece.at[pl.ds(0, size)], sem.at[0]),
        pltpu.make_async_copy(
            down.at[block(piece, size)], mlp_piece.at[pl.ds(size, size)], sem.at[1]
        ),
    ]
    for copy in copies:
        copy.start()
    unit = embed[:, lanes(piece)]
    embed_piece[...] = unit
    both_piece[:rows] = unit
    for i in range(3):
        both_piece[(1 + i) * rows : (2 + i) * rows] = attn[attn_unit(attn, 3 * piece + i)]
    for copy in copies:
        copy.wait()


def extract(where, embed, attn, up, down):
    rows = embed.shape[0]
    return pl.pallas_call(
        extract_kernel,
        in_specs=[SCALARS, FAST, FAST, ANY, ANY],
        out_specs=(FAST, FAST, FAST),
        out_shape=(
            pltpu.VMEM((rows, UNIT), BF16),
            pltpu.VMEM((4 * rows, UNIT), BF16),
            pltpu.VMEM((2 * up.shape[0] // SPREAD, up.shape[1]), BF16),
        ),
        scratch_shapes=[pltpu.SemaphoreType.DMA((2,))],
        compiler_params=SMALL,
    )(
        where,
        pltpu.with_memory_space_constraint(embed, pltpu.VMEM),
        pltpu.with_memory_space_constraint(attn, pltpu.VMEM),
        up,
        down,
    )


def units_kernel(where, neighbour, opposite, third, target):
    rows = neighbour.shape[0]
    target[:rows] = neighbour[...]
    target[rows : 2 * rows] = opposite[:rows]
    target[2 * rows : 3 * rows] = third[...]
    target[3 * rows :] = opposite[rows:]


def stack_kernel(where, *refs):
    *parts, target = refs
    rows = parts[0].shape[0]
    for n, part in enumerate(parts):
        target[n * rows : (n + 1) * rows] = part[...]


def place_attn_kernel(where, embed, mine, others, embed_whole, attn_far):
    piece, group = where[0], where[1]
    rows = embed.shape[0]
    size = 6 * rows
    embed_whole[block(group, rows)] = embed[...]
    for source, core in ((mine, 0), (others, 1)):
        for n in range(SPREAD // 2):
            p = piece ^ (2 * n + core)
            for k in range(3):
                at = n * size + k * rows
                embed_whole[block(group ^ (k + 1), rows), lanes(p)] = source[at : at + rows]
                at += 3 * rows
                attn_far[attn_unit(attn_far, 3 * p + k)] = source[at : at + rows]


def place_mlp_kernel(where, mine, others, up_far, down_far):
    piece = where[0]
    size = up_far.shape[0] // SPREAD
    for source, core in ((mine, 0), (others, 1)):
        for n in range(SPREAD // 2):
            p = piece ^ (2 * n + core)
            at = n * 2 * size
            up_far[block(p, size)] = source[at : at + size]
            down_far[block(p, size)] = source[at + size : at + 2 * size]


def neighbours_of(where, piece):
    parts = [piece]
    for bits in range(2, SPREAD, 2):
        parts.append(swap(piece, "dp", bits))
    rows = len(parts) * piece.shape[0]
    mine = copier(stack_kernel, ((rows,) + piece.shape[1:],), where, *parts)[0]
    return mine, swap(mine, "dp", 1)


def heads(projected, local_heads):
    return projected.reshape(projected.shape[0], local_heads, HEAD_DIM)


def attend(normed, shard):
    width = shard.shape[0] // 4
    qkv = shard[: 3 * width].reshape(3, width, -1)
    local_heads = width // HEAD_DIM
    projected = jnp.einsum("td,ced->cte", normed, qkv, preferred_element_type=F32).astype(BF16)
    queries, attn_keys, attn_values = (heads(projected[c], local_heads) for c in range(3))
    scores = jnp.einsum("qhd,khd->hqk", queries, attn_keys, preferred_element_type=F32)
    probs = jax.nn.softmax(scores * HEAD_DIM ** (-0.5), axis=-1).astype(BF16)
    context = jnp.einsum("hqk,khd->qhd", probs, attn_values, preferred_element_type=F32)
    return dot(context.astype(BF16).reshape(normed.shape[0], -1), shard[3 * width :])


def feed_forward(normed, up, down):
    hidden = jax.nn.gelu(dot(normed, up), approximate=False).astype(BF16)
    return dot(hidden, down)


def layer(
    candidates,
    owner_row,
    selected,
    dest_slot,
    patch_weight,
    positions,
    qkv_weight,
    out_weight,
    attn_gain,
    mlp_gain,
    up_weight,
    down_weight,
):
    groups = lax.axis_size("mp")
    group = lax.axis_index("mp")
    pair = group // 2
    quarter = candidates.shape[1]
    where = jnp.stack([lax.axis_index("dp") % SPREAD, group]).astype(jnp.int32)

    outgoing, senders = route(owner_row, selected, dest_slot, candidates)
    incoming = lax.all_to_all(outgoing, "dp", split_axis=0, concat_axis=0, tiled=True)

    patch_weight, positions, qkv_weight, out_weight, _ = lax.optimization_barrier(
        (patch_weight, positions, qkv_weight, out_weight, senders)
    )
    pixel_width, width = patch_weight.shape
    model = out_weight.shape[1]
    embed_own = jnp.concatenate([patch_weight.T, positions.T], axis=1)
    attn_own = jnp.concatenate([qkv_weight.transpose(1, 2, 0).reshape(-1, model), out_weight])
    embed_piece, both_piece, mlp_piece = extract(where, embed_own, attn_own, up_weight, down_weight)
    third = swap(embed_piece, "mp", 3)
    opposite = swap(both_piece, "mp", 2)
    neighbour = swap(embed_piece, "mp", 1)
    units = copier(units_kernel, ((6 * width, UNIT),), where, neighbour, opposite, third)[0]
    embed_whole, attn_far = copier(
        place_attn_kernel,
        ((groups * width, pixel_width + positions.shape[0]), attn_own.shape),
        where,
        embed_own,
        *neighbours_of(where, units),
    )
    mlp_piece = swap(mlp_piece, "mp", 2)
    up_far, down_far = copier(
        place_mlp_kernel,
        (up_weight.shape, down_weight.shape),
        where,
        *neighbours_of(where, mlp_piece),
    )

    kept = lax.dynamic_index_in_dim(incoming, senders[pair], 0, keepdims=False)
    given = lax.dynamic_index_in_dim(incoming, senders[1 - pair], 0, keepdims=False)
    third = swap(given, "mp", 3)
    opposite = swap(given, "mp", 2)
    neighbour = swap(kept, "mp", 1)
    pixels = jnp.concatenate([kept, opposite, neighbour, third])
    tokens = jnp.arange(groups * quarter, dtype=jnp.int32)
    block_of = tokens // quarter
    turned = (block_of >> 1) + 2 * (block_of & 1)
    spot = (group ^ turned) * quarter + tokens % quarter
    picks = (spot[:, None] == tokens[None, :]).astype(BF16)
    embedded = jnp.einsum(
        "tp,ep->te",
        jnp.concatenate([pixels, picks], axis=1),
        embed_whole,
        preferred_element_type=F32,
    ).astype(BF16)
    half = 2 * quarter
    normed = norm_rows(embedded.astype(F32), attn_gain).astype(BF16)
    attended = attend(normed, attn_own) + attend(normed, attn_far)
    other = swap(attended[half:].astype(BF16), "mp", 1)
    after_attn = embedded[:half].astype(F32) + (attended[:half] + other.astype(F32))
    normed2 = norm_rows(after_attn, mlp_gain).astype(BF16)
    tokens2 = jnp.concatenate([normed2, swap(normed2, "mp", 1)])
    feed = feed_forward(tokens2, up_weight, down_weight) + feed_forward(tokens2, up_far, down_far)
    blocks = [feed[i * quarter : (i + 1) * quarter] for i in range(4)]
    from_third = swap(blocks[3].astype(BF16), "mp", 3)
    from_opposite = swap((after_attn[quarter:] + blocks[1]).astype(BF16), "mp", 2)
    from_neighbour = swap(blocks[2].astype(BF16), "mp", 1)
    kept_out = (after_attn[:quarter] + (blocks[0] + from_neighbour.astype(F32))).astype(BF16)
    given_out = (from_opposite.astype(F32) + from_third.astype(F32)).astype(BF16)
    swapped = pair == 1
    return jnp.stack(
        [jnp.where(swapped, given_out, kept_out), jnp.where(swapped, kept_out, given_out)]
    )


def solution(mesh):
    return jax.shard_map(
        layer,
        mesh=mesh,
        in_specs=(
            P("dp", "mp", None),
            P(),
            P(),
            P(),
            P(None, "mp"),
            P(None, "mp"),
            P(None, None, "mp"),
            P("mp", None),
            P(),
            P(),
            P(None, "mp"),
            P("mp", None),
        ),
        out_specs=P("dp", "mp", None),
        check_vma=False,
    )
```

time: 184 us -> 112 us (0.61)
  waiting for transfers between devices: 97.8 us -> 40.7 us
  blocking collectives: 35.5 us -> 0 us
  starting transfers between devices: 5.46 us -> 31.4 us
  between operations: 14.3 us -> 4.36 us
  matrix products: 9.79 us -> 17.8 us
  local copies, waits for them, and re-layouts: 14 us -> 6.78 us
  Pallas kernels: 0 us -> 7.21 us
  other arithmetic: 7.02 us -> 2.87 us
    psum x1 -> x0, waiting for transfers between devices: 44 us -> none  [local(): lax.psum(partial_out.astype(jnp.bfloat16), 'mp').astype(jnp.float32)]
    unnamed x3 -> x0, waiting for transfers between devices: 42.1 us -> none
    ppermute x0 -> x20, waiting for transfers between devices: none -> 36.6 us  [swap(): lax.ppermute(value, axis, [(i, i ^ bits) for i in range(lax.axis_size(axi...]
    all_gather x2 -> x0, blocking collectives: 35.5 us -> none  [the longest x1 18.1 us: local(): lax.all_gather(own_pixels, 'mp', axis=1, tiled=True)]
    ppermute x0 -> x20, starting transfers between devices: none -> 27.2 us  [swap(): lax.ppermute(value, axis, [(i, i ^ bits) for i in range(lax.axis_size(axi...]
    dot_general x6 -> x11, matrix products: 9.12 us -> 16.9 us  [the longest x4 9.31 us: dot(): return jnp.dot(left, right, preferred_element_type=F32)]
    all_to_all x1, waiting for transfers between devices: 11.7 us -> 4.07 us  [layer(): lax.all_to_all(outgoing, 'dp', split_axis=0, concat_axis=0, tiled=True)]
    pallas_call x0 -> x7, Pallas kernels: none -> 7.21 us  [the longest x5 4.14 us: copier(): pl.pallas_call(body, in_specs=[SCALARS] + [FAST] * len(operands), out_spe...]
  transfers between devices with their start and end apart: 3 -> 21, of which waited for: 3 -> 14; matrix products, arithmetic and copies ran while one was open for 1% -> 11% of each run, Pallas kernels for 0% -> 3%
where the time goes in v3:
time: 112 us; the launch traced here: 111 us
  waiting for transfers between devices  40.7 us (36%)
  starting transfers between devices  31.4 us (28%)
  matrix products  17.8 us (16%)
  Pallas kernels  7.21 us (6%)
  local copies, waits for them, and re-layouts  6.78 us (6%)
  between operations  4.36 us (4%)
  other arithmetic  2.87 us (3%)
    ppermute x20, waiting for transfers between devices, swap(): lax.ppermute(value, axis, [(i, i ^ bits) for i in range(lax.axis_size(axi...  36.6 us
    ppermute x20, starting transfers between devices, swap(): lax.ppermute(value, axis, [(i, i ^ bits) for i in range(lax.axis_size(axi...  27.2 us
    dot_general x4, matrix products, dot(): return jnp.dot(left, right, preferred_element_type=F32)  9.31 us
    unnamed x42, local copies, waits for them, and re-layouts  5.04 us
    all_to_all x1, starting transfers between devices, layer(): lax.all_to_all(outgoing, 'dp', split_axis=0, concat_axis=0, tiled=True)  4.24 us
    pallas_call x5, Pallas kernels, copier(): pl.pallas_call(body, in_specs=[SCALARS] + [FAST] * len(operands), out_spe...  4.14 us
    all_to_all x1, waiting for transfers between devices, layer(): lax.all_to_all(outgoing, 'dp', split_axis=0, concat_axis=0, tiled=True)  4.07 us
    dot_general x2, matrix products, attend(): jnp.einsum('hqk,khd->qhd', probs, attn_values, preferred_element_type=F32)  3.44 us
  transfers between devices with their start and end apart: 21, of which 14 were waited for; matrix products, arithmetic and copies ran while one was open for 11% of the time, Pallas kernels for 3%

profile of v3, /device:TPU:0, one launch (start us, length us, event | category | flops | bytes accessed | tf_op | source)
XLA Modules:
  0.0 111.1 jit_solution(12210795560345317487)
XLA Ops:
  0.0 2.1 %shard_map.118 = (bf16[8,64,768]{2,1,0:T(8,128)(2,1)}, s32[2]{0:T(128)}) custom-call(s32[1]{0:T(128)} %bitcast.own, s32[64]{0:T(128)} %owner_row.1, s32[16]{0:T(128)} %selected.1, s32[16]{0:T(128)} %dest_slot.1, bf16[8,64,768]{2,1,0:T(8,128)(2,1)} %candidates.1), custom_call_target="tpu_custom_call" | custom-call | tf_op jit(solution)/shard_map/pallas_call | solution.py:80
  2.2 1.1 pad_maximum_fusion.1.embed
  3.4 1.2 %copy-done.2 = bf16[768,768]{1,0:T(8,128)(2,1)S(1)} copy-done((bf16[768,768]{1,0:T(8,128)(2,1)S(1)}, bf16[768,768]{1,0:T(8,128)(2,1)}, u32[]{:S(2)}) %copy-start.2) | copy-done | bytes 1179672
  4.5 0.4 copy-done.4
  4.9 1.0 shard_map.119
  5.9 4.1 %collective-permute-start.4 = (bf16[768,128]{1,0:T(8,128)(2,1)S(1)}, bf16[768,128]{1,0:T(8,128)(2,1)S(1)}, u32[]{:S(2)}, u32[]{:S(2)}) collective-permute-start(bf16[768,128]{1,0:T(8,128)(2,1)S(1)} %get-tuple-element.25), channel_id=1, source_target_pairs={{0,2},{1,3},{2,0},{3,1},{4,6},{5,7},{6,4},{7,5},{8,10},{9,11},{10,... | collective-permute-start | bytes 589832 | tf_op jit(solution)/shard_map/ppermute | solution.py:24
  10.0 1.6 %collective-permute-start.3 = (bf16[192,128]{1,0:T(8,128)(2,1)S(1)}, bf16[192,128]{1,0:T(8,128)(2,1)S(1)}, u32[]{:S(2)}, u32[]{:S(2)}) collective-permute-start(bf16[192,128]{1,0:T(8,128)(2,1)S(1)} %get-tuple-element.24), channel_id=1, source_target_pairs={{0,1},{1,0},{2,3},{3,2},{4,5},{5,4},{6,7},{7,6},{8,9},{9,8},{10,11... | collective-permute-start | bytes 147464 | tf_op jit(solution)/shard_map/ppermute | solution.py:24
  11.6 4.8 %collective-permute-done.3.neighbour = bf16[192,128]{1,0:T(8,128)(2,1)S(1)} collective-permute-done((bf16[192,128]{1,0:T(8,128)(2,1)S(1)}, bf16[192,128]{1,0:T(8,128)(2,1)S(1)}, u32[]{:S(2)}, u32[]{:S(2)}) %collective-permute-start.3) | collective-permute-done | bytes 49184 | tf_op jit(solution)/shard_map/ppermute | solution.py:24
  16.4 2.5 %collective-permute-done.5.third = bf16[192,128]{1,0:T(8,128)(2,1)S(1)} collective-permute-done((bf16[192,128]{1,0:T(8,128)(2,1)S(1)}, bf16[192,128]{1,0:T(8,128)(2,1)S(1)}, u32[]{:S(2)}, u32[]{:S(2)}) %collective-permute-start.5) | collective-permute-done | bytes 49184 | tf_op jit(solution)/shard_map/ppermute | solution.py:24
  18.9 2.2 %collective-permute-done.4.opposite = bf16[768,128]{1,0:T(8,128)(2,1)S(1)} collective-permute-done((bf16[768,128]{1,0:T(8,128)(2,1)S(1)}, bf16[768,128]{1,0:T(8,128)(2,1)S(1)}, u32[]{:S(2)}, u32[]{:S(2)}) %collective-permute-start.4) | collective-permute-done | bytes 196640 | tf_op jit(solution)/shard_map/ppermute | solution.py:24
  21.0 0.6 shard_map.120.refs_0_
  21.6 2.0 %collective-permute-start.6 = (bf16[1152,128]{1,0:T(8,128)(2,1)S(1)}, bf16[1152,128]{1,0:T(8,128)(2,1)S(1)}, u32[]{:S(2)}, u32[]{:S(2)}) collective-permute-start(bf16[1152,128]{1,0:T(8,128)(2,1)S(1)} %shard_map.120.refs_0_), channel_id=1, source_target_pairs={{0,8},{4,12},{8,0},{12,4},{16,24},{20,28},{24,16},{28,20},{1,9},{5... | collective-permute-start | bytes 884744 | tf_op jit(solution)/shard_map/ppermute | solution.py:24
  23.6 1.6 %collective-permute-start.7 = (bf16[1152,128]{1,0:T(8,128)(2,1)S(1)}, bf16[1152,128]{1,0:T(8,128)(2,1)S(1)}, u32[]{:S(2)}, u32[]{:S(2)}) collective-permute-start(bf16[1152,128]{1,0:T(8,128)(2,1)S(1)} %shard_map.120.refs_0_), channel_id=1, source_target_pairs={{0,16},{4,20},{8,24},{12,28},{16,0},{20,4},{24,8},{28,12},{1,17},{... | collective-permute-start | bytes 884744 | tf_op jit(solution)/shard_map/ppermute | solution.py:24
  25.3 6.3 %collective-permute-done.6.refs_1_ = bf16[1152,128]{1,0:T(8,128)(2,1)S(1)} collective-permute-done((bf16[1152,128]{1,0:T(8,128)(2,1)S(1)}, bf16[1152,128]{1,0:T(8,128)(2,1)S(1)}, u32[]{:S(2)}, u32[]{:S(2)}) %collective-permute-start.6) | collective-permute-done | bytes 294944 | tf_op jit(solution)/shard_map/ppermute | solution.py:24
  31.6 4.8 %collective-permute-done.7.refs_2_ = bf16[1152,128]{1,0:T(8,128)(2,1)S(1)} collective-permute-done((bf16[1152,128]{1,0:T(8,128)(2,1)S(1)}, bf16[1152,128]{1,0:T(8,128)(2,1)S(1)}, u32[]{:S(2)}, u32[]{:S(2)}) %collective-permute-start.7) | collective-permute-done | bytes 294944 | tf_op jit(solution)/shard_map/ppermute | solution.py:24
  36.4 1.5 %collective-permute-done.8.refs_3_ = bf16[1152,128]{1,0:T(8,128)(2,1)S(1)} collective-permute-done((bf16[1152,128]{1,0:T(8,128)(2,1)S(1)}, bf16[1152,128]{1,0:T(8,128)(2,1)S(1)}, u32[]{:S(2)}, u32[]{:S(2)}) %collective-permute-start.8) | collective-permute-done | bytes 294944 | tf_op jit(solution)/shard_map/ppermute | solution.py:24
  37.9 0.6 shard_map.121.mine
  38.6 4.2 %all-to-all-start = ((bf16[8,64,768]{2,1,0:T(8,128)(2,1)}), bf16[8,64,768]{2,1,0:T(8,128)(2,1)}, u32[]{:S(2)}, u32[]{:S(2)}) async-start(bf16[8,64,768]{2,1,0:T(8,128)(2,1)} %get-tuple-element.18), calls=%async_computation | async-start | bytes 1572864 | tf_op jit(solution)/shard_map/all_to_all | solution.py:244
  42.8 3.9 %collective-permute-start.12 = (bf16[192,768]{1,0:T(8,128)(2,1)S(1)}, bf16[192,768]{1,0:T(8,128)(2,1)S(1)}, u32[]{:S(2)}, u32[]{:S(2)}) collective-permute-start(bf16[192,768]{1,0:T(8,128)(2,1)S(1)} %get-tuple-element.28), channel_id=1, source_target_pairs={{0,2},{1,3},{2,0},{3,1},{4,6},{5,7},{6,4},{7,5},{8,10},{9,11},{10,... | collective-permute-start | bytes 884744 | tf_op jit(solution)/shard_map/ppermute | solution.py:24
  46.8 0.7 fusion.195
  51.4 4.1 %all-to-all-done = bf16[8,64,768]{2,1,0:T(8,128)(2,1)} async-done(((bf16[8,64,768]{2,1,0:T(8,128)(2,1)}), bf16[8,64,768]{2,1,0:T(8,128)(2,1)}, u32[]{:S(2)}, u32[]{:S(2)}) %all-to-all-start) | async-done | bytes 786464 | tf_op jit(solution)/shard_map/all_to_all | solution.py:244
  55.4 1.0 dynamic-slice_bitcast_fusion.1
  56.4 3.8 %collective-permute-start.2 = (bf16[64,768]{1,0:T(8,128)(2,1)S(1)}, bf16[64,768]{1,0:T(8,128)(2,1)S(1)}, u32[]{:S(2)}, u32[]{:S(2)}) collective-permute-start(bf16[64,768]{1,0:T(8,128)(2,1)S(1)} %get-tuple-element.36), channel_id=1, source_target_pairs={{0,3},{1,2},{2,1},{3,0},{4,7},{5,6},{6,5},{7,4},{8,11},{9,10},{10,... | collective-permute-start | bytes 294920 | tf_op jit(solution)/shard_map/ppermute | solution.py:24
  60.2 0.2 collective-permute-start
  60.4 0.5 collective-permute-start.1
  61.0 3.1 %collective-permute-done.12.refs_0_ = bf16[192,768]{1,0:T(8,128)(2,1)S(1)} collective-permute-done((bf16[192,768]{1,0:T(8,128)(2,1)S(1)}, bf16[192,768]{1,0:T(8,128)(2,1)S(1)}, u32[]{:S(2)}, u32[]{:S(2)}) %collective-permute-start.12) | collective-permute-done | bytes 294944 | tf_op jit(solution)/shard_map/ppermute | solution.py:24
  64.1 1.9 %collective-permute-start.13 = (bf16[192,768]{1,0:T(8,128)(2,1)S(1)}, bf16[192,768]{1,0:T(8,128)(2,1)S(1)}, u32[]{:S(2)}, u32[]{:S(2)}) collective-permute-start(bf16[192,768]{1,0:T(8,128)(2,1)S(1)} %collective-permute-done.12.refs_0_), channel_id=1, source_target_pairs={{0,8},{4,12},{8,0},{12,4},{16,24},{20,28},{24,16},{28,20},{1,9},{5... | collective-permute-start | bytes 884744 | tf_op jit(solution)/shard_map/ppermute | solution.py:24
  66.0 2.2 %collective-permute-start.14 = (bf16[192,768]{1,0:T(8,128)(2,1)S(1)}, bf16[192,768]{1,0:T(8,128)(2,1)}, u32[]{:S(2)}, u32[]{:S(2)}) collective-permute-start(bf16[192,768]{1,0:T(8,128)(2,1)S(1)} %collective-permute-done.12.refs_0_), channel_id=1, source_target_pairs={{0,16},{4,20},{8,24},{12,28},{16,0},{20,4},{24,8},{28,12},{1,17},{... | collective-permute-start | bytes 884744 | tf_op jit(solution)/shard_map/ppermute | solution.py:24
  68.2 1.2 %shard_map.122 = (bf16[768,1024]{1,0:T(8,128)(2,1)S(1)}, bf16[768,768]{1,0:T(8,128)(2,1)S(1)}) custom-call(s32[2]{0:T(128)S(1)} %pad_add_fusion.where, bf16[192,1024]{1,0:T(8,128)(2,1)S(1)} %pad_maximum_fusion.1.embed, bf16[4608,128]{1,0:T(8,128)(2,1)S(1)} %shard_map.121.mine, bf16[4608,128]{1,0:T(8,128)(2,1)S(1)} %collective-permute-done.9.others), custom_call_target="tpu_custom_call" | custom-call | tf_op jit(solution)/shard_map/pallas_call | solution.py:39
  69.4 1.0 copy-done
  70.6 0.7 convert_reduce_fusion
  71.3 0.2 fusion.11
  71.6 0.2 copy-done.14
  71.8 0.5 fusion.6
  72.3 0.4 fusion.196
  72.8 1.2 %convolution_multiply_fusion.1 = f32[3,256,256]{1,2,0:T(8,128)} fusion(bf16[256,3,64]{0,2,1:T(8,128)(2,1)S(1)} %bitcast.67, bf16[256,3,64]{0,2,1:T(8,128)(2,1)S(1)} %bitcast.65), kind=kOutput, calls=%fused_computation.9 | convolution fusion | flops 25362432 | bytes 983040 | tf_op jit(solution)/shard_map/qhd,khd->hqk/dot_general | solution.py:212
  74.0 0.5 fusion.7
  74.6 0.4 fusion.197
  75.1 1.2 %convolution_multiply_fusion = f32[3,256,256]{1,2,0:T(8,128)} fusion(bf16[256,3,64]{0,2,1:T(8,128)(2,1)S(1)} %bitcast.71, bf16[256,3,64]{0,2,1:T(8,128)(2,1)S(1)} %bitcast.69), kind=kOutput, calls=%fused_computation.8 | convolution fusion | flops 25362432 | bytes 983040 | tf_op jit(solution)/shard_map/qhd,khd->hqk/dot_general | solution.py:212
  76.3 1.7 %convolution_convert_fusion.4 = bf16[3,64,256]{2,1,0:T(8,128)(2,1)S(1)} fusion(bf16[256,3,64]{0,2,1:T(8,128)(2,1)S(1)} %bitcast.74, f32[3,256]{1,0:T(4,128)S(1)} %fusion.196, f32[3,256,256]{1,2,0:T(8,128)} %convolution_multiply_fusion.1), kind=kOutput, calls=%fused_computation.19 | convolution fusion | flops 25805824 | bytes 986112 | tf_op jit(solution)/shard_map/hqk,khd->qhd/dot_general | solution.py:214
  78.0 0.3 fusion.199
  78.3 1.7 %convolution_convert_fusion.3 = bf16[3,64,256]{2,1,0:T(8,128)(2,1)S(1)} fusion(bf16[256,3,64]{0,2,1:T(8,128)(2,1)S(1)} %bitcast.75, f32[3,256]{1,0:T(4,128)S(1)} %fusion.197, f32[3,256,256]{1,2,0:T(8,128)} %convolution_multiply_fusion), kind=kOutput, calls=%fused_computation.18 | convolution fusion | flops 25805824 | bytes 986112 | tf_op jit(solution)/shard_map/hqk,khd->qhd/dot_general | solution.py:214
  80.0 0.3 convolution_add_fusion.1
  80.4 0.2 collective-permute-start.10
  80.6 0.1 copy-done.19
  80.7 0.4 collective-permute-done.14.refs_2_
  81.1 1.0 shard_map.123.mine
  82.2 3.9 %collective-permute-done.10 = bf16[128,768]{1,0:T(8,128)(2,1)S(1)} collective-permute-done((bf16[128,768]{1,0:T(8,128)(2,1)S(1)}, bf16[128,768]{1,0:T(8,128)(2,1)S(1)}, u32[]{:S(2)}, u32[]{:S(2)}) %collective-permute-start.10) | collective-permute-done | bytes 196640 | tf_op jit(solution)/shard_map/ppermute | solution.py:24
  86.2 0.1 fusion.190
  86.3 0.2 multiply_reduce_fusion
  86.5 0.1 multiply_convert_fusion
  86.7 0.4 collective-permute-start.11
  87.1 0.7 shard_map.124
  87.8 1.0 copy-done.6
  88.8 1.1 copy-done.8
  89.9 2.7 %collective-permute-done.11 = bf16[128,768]{1,0:T(8,128)(2,1)} collective-permute-done((bf16[128,768]{1,0:T(8,128)(2,1)S(1)}, bf16[128,768]{1,0:T(8,128)(2,1)}, u32[]{:S(2)}, u32[]{:S(2)}) %collective-permute-start.11) | collective-permute-done | bytes 196640 | tf_op jit(solution)/shard_map/ppermute | solution.py:24
  92.6 4.5 %fusion.44 = f32[256,768]{1,0:T(8,128)} fusion(bf16[768,768]{1,0:T(8,128)(2,1)S(1)} %copy-done.3, bf16[768,768]{1,0:T(8,128)(2,1)S(1)} %copy-done.5, bf16[128,768]{1,0:T(8,128)(2,1)} %collective-permute-done.11, bf16[128,768]{1,0:T(8,128)(2,1)} %copy-done.17), kind=kOutput, calls=%fused_computation.75 | convolution fusion | flops 617545728 | bytes 3538944 | tf_op jit(solution)/shard_map/dot_general | solution.py:28
  97.1 4.2 %fusion.198 = (bf16[256,768]{1,0:T(8,128)(2,1)S(1)}, f32[256,768]{1,0:T(8,128)S(1)}) fusion(f32[256,768]{1,0:T(8,128)} %fusion.44, bf16[768,768]{1,0:T(8,128)(2,1)} %copy-done.8, bf16[768,768]{1,0:T(8,128)(2,1)S(1)} %copy-done.7, bf16[128,768]{1,0:T(8,128)(2,1)} %collective-permute-done.11, bf16[128,768]{1,0:T(8,128)(2,1)} %copy-done.17), kind=kOutput, calls=%fused_computation.247 | convolution fusion | flops 617938944 | bytes 4718592 | tf_op jit(solution)/shard_map/dot_general | solution.py:28
  101.3 3.2 %collective-permute-start.18 = (bf16[64,768]{1,0:T(8,128)(2,1)S(1)}, bf16[64,768]{1,0:T(8,128)(2,1)S(1)}, u32[]{:S(2)}, u32[]{:S(2)}) collective-permute-start(bf16[64,768]{1,0:T(8,128)(2,1)S(1)} %get-tuple-element.38), channel_id=1, source_target_pairs={{0,3},{1,2},{2,1},{3,0},{4,7},{5,6},{6,5},{7,4},{8,11},{9,10},{10,... | collective-permute-start | bytes 294920 | tf_op jit(solution)/shard_map/ppermute | solution.py:24
  104.6 1.3 %collective-permute-start.19 = (bf16[64,768]{1,0:T(8,128)(2,1)S(1)}, bf16[64,768]{1,0:T(8,128)(2,1)S(1)}, u32[]{:S(2)}, u32[]{:S(2)}) collective-permute-start(bf16[64,768]{1,0:T(8,128)(2,1)S(1)} %get-tuple-element.37), channel_id=1, source_target_pairs={{0,1},{1,0},{2,3},{3,2},{4,5},{5,4},{6,7},{7,6},{8,9},{9,8},{10,11... | collective-permute-start | bytes 294920 | tf_op jit(solution)/shard_map/ppermute | solution.py:24
  105.9 2.0 %collective-permute-done.18 = bf16[64,768]{1,0:T(8,128)(2,1)S(1)} collective-permute-done((bf16[64,768]{1,0:T(8,128)(2,1)S(1)}, bf16[64,768]{1,0:T(8,128)(2,1)S(1)}, u32[]{:S(2)}, u32[]{:S(2)}) %collective-permute-start.18) | collective-permute-done | bytes 98336 | tf_op jit(solution)/shard_map/ppermute | solution.py:24
  107.9 2.3 %collective-permute-done.17 = bf16[64,768]{1,0:T(8,128)(2,1)S(1)} collective-permute-done((bf16[64,768]{1,0:T(8,128)(2,1)S(1)}, bf16[64,768]{1,0:T(8,128)(2,1)S(1)}, u32[]{:S(2)}, u32[]{:S(2)}) %collective-permute-start.17) | collective-permute-done | bytes 98336 | tf_op jit(solution)/shard_map/ppermute | solution.py:24
  110.2 0.1 collective-permute-done.19
  110.4 0.7 pad_maximum_fusion.13
  (66 shorter events, 1.0 us)
Async XLA Ops:
  0.0 3.2 %copy-start.13 = (bf16[768,3,192]{0,2,1:T(8,128)(2,1)S(1)}, bf16[768,3,192]{0,2,1:T(8,128)(2,1)}, u32[]{:S(2)}) copy-start(bf16[768,3,192]{0,2,1:T(8,128)(2,1)} %param.18) | copy-start | bytes 2654212
  0.0 3.2 %copy-start.11 = (bf16[192,768]{1,0:T(8,128)(2,1)S(1)}, bf16[192,768]{1,0:T(8,128)(2,1)}, u32[]{:S(2)}) copy-start(bf16[192,768]{1,0:T(8,128)(2,1)} %param.19) | copy-start | bytes 884740
  3.2 1.3 %copy-start.2 = (bf16[768,768]{1,0:T(8,128)(2,1)S(1)}, bf16[768,768]{1,0:T(8,128)(2,1)}, u32[]{:S(2)}) copy-start(bf16[768,768]{1,0:T(8,128)(2,1)} %down.1) | copy-start | bytes 3538948
  3.3 1.6 %copy-start.4 = (bf16[768,768]{1,0:T(8,128)(2,1)S(1)}, bf16[768,768]{1,0:T(8,128)(2,1)}, u32[]{:S(2)}) copy-start(bf16[768,768]{1,0:T(8,128)(2,1)} %up.1) | copy-start | bytes 3538948
  5.9 15.2 %collective-permute-start.4 = (bf16[768,128]{1,0:T(8,128)(2,1)S(1)}, bf16[768,128]{1,0:T(8,128)(2,1)S(1)}, u32[]{:S(2)}, u32[]{:S(2)}) collective-permute-start(bf16[768,128]{1,0:T(8,128)(2,1)S(1)} %get-tuple-element.25), channel_id=1, source_target_pairs={{0,2},{1,3},{2,0},{3,1},{4,6},{5,7},{6,4},{7,5},{8,10},{9,11},{10,... | collective-permute-start | bytes 589832 | tf_op jit(solution)/shard_map/ppermute | solution.py:24
  10.0 6.4 %collective-permute-start.3 = (bf16[192,128]{1,0:T(8,128)(2,1)S(1)}, bf16[192,128]{1,0:T(8,128)(2,1)S(1)}, u32[]{:S(2)}, u32[]{:S(2)}) collective-permute-start(bf16[192,128]{1,0:T(8,128)(2,1)S(1)} %get-tuple-element.24), channel_id=1, source_target_pairs={{0,1},{1,0},{2,3},{3,2},{4,5},{5,4},{6,7},{7,6},{8,9},{9,8},{10,11... | collective-permute-start | bytes 147464 | tf_op jit(solution)/shard_map/ppermute | solution.py:24
  11.6 7.3 %collective-permute-start.5 = (bf16[192,128]{1,0:T(8,128)(2,1)S(1)}, bf16[192,128]{1,0:T(8,128)(2,1)S(1)}, u32[]{:S(2)}, u32[]{:S(2)}) collective-permute-start(bf16[192,128]{1,0:T(8,128)(2,1)S(1)} %get-tuple-element.24), channel_id=1, source_target_pairs={{0,3},{1,2},{2,1},{3,0},{4,7},{5,6},{6,5},{7,4},{8,11},{9,10},{10,... | collective-permute-start | bytes 147464 | tf_op jit(solution)/shard_map/ppermute | solution.py:24
  21.6 9.9 %collective-permute-start.6 = (bf16[1152,128]{1,0:T(8,128)(2,1)S(1)}, bf16[1152,128]{1,0:T(8,128)(2,1)S(1)}, u32[]{:S(2)}, u32[]{:S(2)}) collective-permute-start(bf16[1152,128]{1,0:T(8,128)(2,1)S(1)} %shard_map.120.refs_0_), channel_id=1, source_target_pairs={{0,8},{4,12},{8,0},{12,4},{16,24},{20,28},{24,16},{28,20},{1,9},{5... | collective-permute-start | bytes 884744 | tf_op jit(solution)/shard_map/ppermute | solution.py:24
  23.6 12.7 %collective-permute-start.7 = (bf16[1152,128]{1,0:T(8,128)(2,1)S(1)}, bf16[1152,128]{1,0:T(8,128)(2,1)S(1)}, u32[]{:S(2)}, u32[]{:S(2)}) collective-permute-start(bf16[1152,128]{1,0:T(8,128)(2,1)S(1)} %shard_map.120.refs_0_), channel_id=1, source_target_pairs={{0,16},{4,20},{8,24},{12,28},{16,0},{20,4},{24,8},{28,12},{1,17},{... | collective-permute-start | bytes 884744 | tf_op jit(solution)/shard_map/ppermute | solution.py:24
  25.3 12.6 %collective-permute-start.8 = (bf16[1152,128]{1,0:T(8,128)(2,1)S(1)}, bf16[1152,128]{1,0:T(8,128)(2,1)S(1)}, u32[]{:S(2)}, u32[]{:S(2)}) collective-permute-start(bf16[1152,128]{1,0:T(8,128)(2,1)S(1)} %shard_map.120.refs_0_), channel_id=1, source_target_pairs={{0,24},{4,28},{8,16},{12,20},{16,8},{20,12},{24,0},{28,4},{1,25},{... | collective-permute-start | bytes 884744 | tf_op jit(solution)/shard_map/ppermute | solution.py:24
  38.5 8.3 %copy-start.20 = (s32[2]{0:T(128)S(1)}, s32[2]{0:T(128)}, u32[]{:S(2)}) copy-start(s32[2]{0:T(128)} %get-tuple-element.19) | copy-start | bytes 28
  38.5 22.5 %copy-start.18 = (bf16[768]{0:T(1024)(128)(2,1)S(1)}, bf16[768]{0:T(1024)(128)(2,1)}, u32[]{:S(2)}) copy-start(bf16[768]{0:T(1024)(128)(2,1)} %param.20) | copy-start | bytes 4612
  38.5 27.5 %collective-permute-start.9 = (bf16[4608,128]{1,0:T(8,128)(2,1)S(1)}, bf16[4608,128]{1,0:T(8,128)(2,1)S(1)}, u32[]{:S(2)}, u32[]{:S(2)}) collective-permute-start(bf16[4608,128]{1,0:T(8,128)(2,1)S(1)} %shard_map.121.mine), channel_id=1, source_target_pairs={{0,4},{4,0},{8,12},{12,8},{16,20},{20,16},{24,28},{28,24},{1,5},{5... | collective-permute-start | bytes 3538952 | tf_op jit(solution)/shard_map/ppermute | solution.py:24
  38.6 16.8 %all-to-all-start = ((bf16[8,64,768]{2,1,0:T(8,128)(2,1)}), bf16[8,64,768]{2,1,0:T(8,128)(2,1)}, u32[]{:S(2)}, u32[]{:S(2)}) async-start(bf16[8,64,768]{2,1,0:T(8,128)(2,1)} %get-tuple-element.18), calls=%async_computation | async-start | bytes 1572864 | tf_op jit(solution)/shard_map/all_to_all | solution.py:244
  42.8 21.3 %collective-permute-start.12 = (bf16[192,768]{1,0:T(8,128)(2,1)S(1)}, bf16[192,768]{1,0:T(8,128)(2,1)S(1)}, u32[]{:S(2)}, u32[]{:S(2)}) collective-permute-start(bf16[192,768]{1,0:T(8,128)(2,1)S(1)} %get-tuple-element.28), channel_id=1, source_target_pairs={{0,2},{1,3},{2,0},{3,1},{4,6},{5,7},{6,4},{7,5},{8,10},{9,11},{10,... | collective-permute-start | bytes 884744 | tf_op jit(solution)/shard_map/ppermute | solution.py:24
  56.4 14.1 %collective-permute-start.2 = (bf16[64,768]{1,0:T(8,128)(2,1)S(1)}, bf16[64,768]{1,0:T(8,128)(2,1)S(1)}, u32[]{:S(2)}, u32[]{:S(2)}) collective-permute-start(bf16[64,768]{1,0:T(8,128)(2,1)S(1)} %get-tuple-element.36), channel_id=1, source_target_pairs={{0,3},{1,2},{2,1},{3,0},{4,7},{5,6},{6,5},{7,4},{8,11},{9,10},{10,... | collective-permute-start | bytes 294920 | tf_op jit(solution)/shard_map/ppermute | solution.py:24
  60.2 10.4 %collective-permute-start = (bf16[64,768]{1,0:T(8,128)(2,1)S(1)}, bf16[64,768]{1,0:T(8,128)(2,1)S(1)}, u32[]{:S(2)}, u32[]{:S(2)}) collective-permute-start(bf16[64,768]{1,0:T(8,128)(2,1)S(1)} %get-tuple-element.36), channel_id=1, source_target_pairs={{0,2},{1,3},{2,0},{3,1},{4,6},{5,7},{6,4},{7,5},{8,10},{9,11},{10,... | collective-permute-start | bytes 294920 | tf_op jit(solution)/shard_map/ppermute | solution.py:24
  60.4 10.2 %collective-permute-start.1 = (bf16[64,768]{1,0:T(8,128)(2,1)S(1)}, bf16[64,768]{1,0:T(8,128)(2,1)S(1)}, u32[]{:S(2)}, u32[]{:S(2)}) collective-permute-start(bf16[64,768]{1,0:T(8,128)(2,1)S(1)} %get-tuple-element.35), channel_id=1, source_target_pairs={{0,1},{1,0},{2,3},{3,2},{4,5},{5,4},{6,7},{7,6},{8,9},{9,8},{10,11... | collective-permute-start | bytes 294920 | tf_op jit(solution)/shard_map/ppermute | solution.py:24
  64.1 16.6 %collective-permute-start.13 = (bf16[192,768]{1,0:T(8,128)(2,1)S(1)}, bf16[192,768]{1,0:T(8,128)(2,1)S(1)}, u32[]{:S(2)}, u32[]{:S(2)}) collective-permute-start(bf16[192,768]{1,0:T(8,128)(2,1)S(1)} %collective-permute-done.12.refs_0_), channel_id=1, source_target_pairs={{0,8},{4,12},{8,0},{12,4},{16,24},{20,28},{24,16},{28,20},{1,9},{5... | collective-permute-start | bytes 884744 | tf_op jit(solution)/shard_map/ppermute | solution.py:24
  66.0 15.1 %collective-permute-start.14 = (bf16[192,768]{1,0:T(8,128)(2,1)S(1)}, bf16[192,768]{1,0:T(8,128)(2,1)}, u32[]{:S(2)}, u32[]{:S(2)}) collective-permute-start(bf16[192,768]{1,0:T(8,128)(2,1)S(1)} %collective-permute-done.12.refs_0_), channel_id=1, source_target_pairs={{0,16},{4,20},{8,24},{12,28},{16,0},{20,4},{24,8},{28,12},{1,17},{... | collective-permute-start | bytes 884744 | tf_op jit(solution)/shard_map/ppermute | solution.py:24
  69.4 1.1 copy-start
  70.5 10.6 %collective-permute-start.15 = (bf16[192,768]{1,0:T(8,128)(2,1)S(1)}, bf16[192,768]{1,0:T(8,128)(2,1)S(1)}, u32[]{:S(2)}, u32[]{:S(2)}) collective-permute-start(bf16[192,768]{1,0:T(8,128)(2,1)S(1)} %collective-permute-done.12.refs_0_), channel_id=1, source_target_pairs={{0,24},{4,28},{8,16},{12,20},{16,8},{20,12},{24,0},{28,4},{1,25},{... | collective-permute-start | bytes 884744 | tf_op jit(solution)/shard_map/ppermute | solution.py:24
  70.6 1.2 %copy-start.14 = (bf16[768,3,192]{0,2,1:T(8,128)(2,1)S(1)}, bf16[768,3,192]{0,2,1:T(8,128)(2,1)}, u32[]{:S(2)}) copy-start(bf16[768,3,192]{0,2,1:T(8,128)(2,1)} %param.18) | copy-start | bytes 2654212
  71.3 2.8 %copy-start.15 = (bf16[256,768]{1,0:T(8,128)(2,1)}, bf16[256,768]{1,0:T(8,128)(2,1)S(1)}, u32[]{:S(2)}) copy-start(bf16[256,768]{1,0:T(8,128)(2,1)S(1)} %get-tuple-element.48) | copy-start | bytes 1179652
  72.3 1.7 %copy-start.1 = (bf16[768,768]{1,0:T(8,128)(2,1)S(1)}, bf16[768,768]{1,0:T(8,128)(2,1)}, u32[]{:S(2)}) copy-start(bf16[768,768]{1,0:T(8,128)(2,1)} %copy-done) | copy-start | bytes 3538948
  76.3 1.7 %copy-start.12 = (bf16[192,768]{1,0:T(8,128)(2,1)S(1)}, bf16[192,768]{1,0:T(8,128)(2,1)}, u32[]{:S(2)}) copy-start(bf16[192,768]{1,0:T(8,128)(2,1)} %param.19) | copy-start | bytes 884740
  80.0 0.7 copy-start.19
  80.4 5.8 %collective-permute-start.10 = (bf16[128,768]{1,0:T(8,128)(2,1)S(1)}, bf16[128,768]{1,0:T(8,128)(2,1)S(1)}, u32[]{:S(2)}, u32[]{:S(2)}) collective-permute-start(bf16[128,768]{1,0:T(8,128)(2,1)S(1)} %slice.103), channel_id=1, source_target_pairs={{0,1},{1,0},{2,3},{3,2},{4,5},{5,4},{6,7},{7,6},{8,9},{9,8},{10,11... | collective-permute-start | bytes 589832 | tf_op jit(solution)/shard_map/ppermute | solution.py:24
  80.7 5.5 %copy-start.16 = (bf16[256,768]{1,0:T(8,128)(2,1)S(1)}, bf16[256,768]{1,0:T(8,128)(2,1)}, u32[]{:S(2)}) copy-start(bf16[256,768]{1,0:T(8,128)(2,1)} %copy-done.15) | copy-start | bytes 1179652
  82.2 4.9 %collective-permute-start.16 = (bf16[768,768]{1,0:T(8,128)(2,1)S(1)}, bf16[768,768]{1,0:T(8,128)(2,1)S(1)}, u32[]{:S(2)}, u32[]{:S(2)}) collective-permute-start(bf16[768,768]{1,0:T(8,128)(2,1)S(1)} %shard_map.123.mine), channel_id=1, source_target_pairs={{0,4},{4,0},{8,12},{12,8},{16,20},{20,16},{24,28},{28,24},{1,5},{5... | collective-permute-start | bytes 3538952 | tf_op jit(solution)/shard_map/ppermute | solution.py:24
  86.3 1.5 %copy-start.9 = (f32[128,768]{1,0:T(8,128)}, f32[128,768]{1,0:T(8,128)S(1)}, u32[]{:S(2)}) copy-start(f32[128,768]{1,0:T(8,128)S(1)} %get-tuple-element.34) | copy-start | bytes 1179652
  86.7 1.1 copy-start.17
  86.7 5.9 %copy-start.3 = (bf16[768,768]{1,0:T(8,128)(2,1)S(1)}, bf16[768,768]{1,0:T(8,128)(2,1)}, u32[]{:S(2)}) copy-start(bf16[768,768]{1,0:T(8,128)(2,1)} %down.1) | copy-start | bytes 3538948
  86.7 5.9 %copy-start.5 = (bf16[768,768]{1,0:T(8,128)(2,1)S(1)}, bf16[768,768]{1,0:T(8,128)(2,1)}, u32[]{:S(2)}) copy-start(bf16[768,768]{1,0:T(8,128)(2,1)} %up.1) | copy-start | bytes 3538948
  86.7 5.8 %collective-permute-start.11 = (bf16[128,768]{1,0:T(8,128)(2,1)S(1)}, bf16[128,768]{1,0:T(8,128)(2,1)}, u32[]{:S(2)}, u32[]{:S(2)}) collective-permute-start(bf16[128,768]{1,0:T(8,128)(2,1)S(1)} %multiply_convert_fusion), channel_id=1, source_target_pairs={{0,1},{1,0},{2,3},{3,2},{4,5},{5,4},{6,7},{7,6},{8,9},{9,8},{10,11... | collective-permute-start | bytes 589832 | tf_op jit(solution)/shard_map/ppermute | solution.py:24
  87.8 1.0 copy-start.6
  88.8 1.1 copy-start.8
  92.6 4.5 %copy-start.7 = (bf16[768,768]{1,0:T(8,128)(2,1)S(1)}, bf16[768,768]{1,0:T(8,128)(2,1)}, u32[]{:S(2)}) copy-start(bf16[768,768]{1,0:T(8,128)(2,1)} %copy-done.6) | copy-start | bytes 3538948
  97.1 7.4 %copy-start.10 = (f32[128,768]{1,0:T(8,128)S(1)}, f32[128,768]{1,0:T(8,128)}, u32[]{:S(2)}) copy-start(f32[128,768]{1,0:T(8,128)} %copy-done.9) | copy-start | bytes 1179652
  101.3 6.6 %collective-permute-start.18 = (bf16[64,768]{1,0:T(8,128)(2,1)S(1)}, bf16[64,768]{1,0:T(8,128)(2,1)S(1)}, u32[]{:S(2)}, u32[]{:S(2)}) collective-permute-start(bf16[64,768]{1,0:T(8,128)(2,1)S(1)} %get-tuple-element.38), channel_id=1, source_target_pairs={{0,3},{1,2},{2,1},{3,0},{4,7},{5,6},{6,5},{7,4},{8,11},{9,10},{10,... | collective-permute-start | bytes 294920 | tf_op jit(solution)/shard_map/ppermute | solution.py:24
  104.5 5.7 %collective-permute-start.17 = (bf16[64,768]{1,0:T(8,128)(2,1)S(1)}, bf16[64,768]{1,0:T(8,128)(2,1)S(1)}, u32[]{:S(2)}, u32[]{:S(2)}) collective-permute-start(bf16[64,768]{1,0:T(8,128)(2,1)S(1)} %fusion.114), channel_id=1, source_target_pairs={{0,2},{1,3},{2,0},{3,1},{4,6},{5,7},{6,4},{7,5},{8,10},{9,11},{10,... | collective-permute-start | bytes 294920 | tf_op jit(solution)/shard_map/ppermute | solution.py:24
  104.6 5.7 %collective-permute-start.19 = (bf16[64,768]{1,0:T(8,128)(2,1)S(1)}, bf16[64,768]{1,0:T(8,128)(2,1)S(1)}, u32[]{:S(2)}, u32[]{:S(2)}) collective-permute-start(bf16[64,768]{1,0:T(8,128)(2,1)S(1)} %get-tuple-element.37), channel_id=1, source_target_pairs={{0,1},{1,0},{2,3},{3,2},{4,5},{5,4},{6,7},{7,6},{8,9},{9,8},{10,11... | collective-permute-start | bytes 294920 | tf_op jit(solution)/shard_map/ppermute | solution.py:24

commit v4 on v3

--- a/solution.py
+++ b/solution.py
@@ -199,25 +199,120 @@
     return mine, swap(mine, "dp", 1)
 
 
-def heads(projected, local_heads):
-    return projected.reshape(projected.shape[0], local_heads, HEAD_DIM)
-
-
-def attend(normed, shard):
+def turned_dot(left, right):
+    return lax.dot_general(left, right, (((1,), (1,)), ((), ())), preferred_element_type=F32)
+
+
+def columns_dot(left, right):
+    return lax.dot_general(left, right, (((0,), (0,)), ((), ())), preferred_element_type=F32)
+
+
+def context_of(normed, shard):
     width = shard.shape[0] // 4
-    qkv = shard[: 3 * width].reshape(3, width, -1)
-    local_heads = width // HEAD_DIM
-    projected = jnp.einsum("td,ced->cte", normed, qkv, preferred_element_type=F32).astype(BF16)
-    queries, attn_keys, attn_values = (heads(projected[c], local_heads) for c in range(3))
-    scores = jnp.einsum("qhd,khd->hqk", queries, attn_keys, preferred_element_type=F32)
-    probs = jax.nn.softmax(scores * HEAD_DIM ** (-0.5), axis=-1).astype(BF16)
-    context = jnp.einsum("hqk,khd->qhd", probs, attn_values, preferred_element_type=F32)
-    return dot(context.astype(BF16).reshape(normed.shape[0], -1), shard[3 * width :])
-
-
-def feed_forward(normed, up, down):
-    hidden = jax.nn.gelu(dot(normed, up), approximate=False).astype(BF16)
-    return dot(hidden, down)
+    projected = turned_dot(shard[: 3 * width], normed).astype(BF16)
+    results = []
+    for at in range(0, width, HEAD_DIM):
+        queries, attn_keys, attn_values = (
+            projected[c * width + at : c * width + at + HEAD_DIM] for c in range(3)
+        )
+        scores = columns_dot(attn_keys, queries) * HEAD_DIM ** (-0.5)
+        raised = jnp.exp(scores - jnp.max(scores, axis=0, keepdims=True))
+        probs = (raised / jnp.sum(raised, axis=0, keepdims=True)).astype(BF16)
+        results.append(dot(attn_values, probs).astype(BF16))
+    return results
+
+
+def attend_kernel(where, kept, opposite, neighbour, third, embed, own, far, gain, mine, other):
+    group = where[1]
+    quarter, pixel_width = kept.shape
+    count = embed.shape[1] - pixel_width
+    pixels = jnp.concatenate([kept[...], opposite[...], neighbour[...], third[...]], axis=0)
+    row = lax.broadcasted_iota(jnp.int32, (count, count), 0)
+    column = lax.broadcasted_iota(jnp.int32, (count, count), 1)
+    block_of = row // quarter
+    turned = (block_of >> 1) + 2 * (block_of & 1)
+    spot = (turned ^ group) * quarter + row % quarter
+    picks = jnp.where(spot == column, 1.0, 0.0).astype(BF16)
+    product = turned_dot(pixels, embed[:, :pixel_width]) + turned_dot(picks, embed[:, pixel_width:])
+    activations = product.astype(BF16).astype(F32)
+    normed = norm_rows(activations, gain[...]).astype(BF16)
+    width = own.shape[0] // 4
+    context = jnp.concatenate(context_of(normed, own) + context_of(normed, far), axis=0)
+    out = jnp.concatenate([own[3 * width :], far[3 * width :]], axis=0)
+    attended = columns_dot(context, out)
+    half = 2 * quarter
+    mine[...] = activations[:half] + attended[:half]
+    other[...] = attended[half:].astype(BF16)
+
+
+def attend(where, parts, embed, own, far, gain):
+    half = 2 * parts[0].shape[0]
+    model = own.shape[1]
+    held = [pltpu.with_memory_space_constraint(x, pltpu.VMEM) for x in (*parts, embed, own, far)]
+    return pl.pallas_call(
+        attend_kernel,
+        in_specs=[SCALARS] + [FAST] * 8,
+        out_specs=(FAST, FAST),
+        out_shape=(pltpu.VMEM((half, model), F32), pltpu.VMEM((half, model), BF16)),
+        compiler_params=pltpu.CompilerParams(vmem_limit_bytes=20 * 1024 * 1024),
+    )(where, *held, gain.reshape(1, -1))
+
+
+def gelu(values):
+    return 0.5 * values * (1.0 + lax.erf(values * 0.5 ** 0.5))
+
+
+def feed_through(normed, up, down):
+    return dot(gelu(dot(normed, up)).astype(BF16), down)
+
+
+def first_kernel(normed, up_far, down_far, up, down, feed, up_own, down_own, sem):
+    copies = [
+        pltpu.make_async_copy(up, up_own, sem.at[0]),
+        pltpu.make_async_copy(down, down_own, sem.at[1]),
+    ]
+    for copy in copies:
+        copy.start()
+    part = feed_through(normed[...], up_far[...], down_far[...])
+    for copy in copies:
+        copy.wait()
+    feed[...] = part + feed_through(normed[...], up_own[...], down_own[...])
+
+
+def feed_first(normed, up_far, down_far, up, down):
+    held = [pltpu.with_memory_space_constraint(x, pltpu.VMEM) for x in (normed, up_far, down_far)]
+    return pl.pallas_call(
+        first_kernel,
+        in_specs=[FAST, FAST, FAST, ANY, ANY],
+        out_specs=(FAST, FAST, FAST),
+        out_shape=(
+            pltpu.VMEM((normed.shape[0], down.shape[1]), F32),
+            pltpu.VMEM(up.shape, BF16),
+            pltpu.VMEM(down.shape, BF16),
+        ),
+        scratch_shapes=[pltpu.SemaphoreType.DMA((2,))],
+        compiler_params=pltpu.CompilerParams(vmem_limit_bytes=16 * 1024 * 1024),
+    )(*held, up, down)
+
+
+def second_kernel(normed, up_far, down_far, up_own, down_own, near, third):
+    part = feed_through(normed[...], up_far[...], down_far[...])
+    part = part + feed_through(normed[...], up_own[...], down_own[...])
+    quarter = near.shape[0]
+    near[...] = part[:quarter].astype(BF16)
+    third[...] = part[quarter:].astype(BF16)
+
+
+def feed_second(*operands):
+    half, model = operands[0].shape
+    held = [pltpu.with_memory_space_constraint(x, pltpu.VMEM) for x in operands]
+    return pl.pallas_call(
+        second_kernel,
+        in_specs=[FAST] * 5,
+        out_specs=(FAST, FAST),
+        out_shape=(pltpu.VMEM((half // 2, model), BF16), pltpu.VMEM((half // 2, model), BF16)),
+        compiler_params=pltpu.CompilerParams(vmem_limit_bytes=16 * 1024 * 1024),
+    )(*held)
 
 
 def layer(
@@ -275,31 +370,19 @@
     third = swap(given, "mp", 3)
     opposite = swap(given, "mp", 2)
     neighbour = swap(kept, "mp", 1)
-    pixels = jnp.concatenate([kept, opposite, neighbour, third])
-    tokens = jnp.arange(groups * quarter, dtype=jnp.int32)
-    block_of = tokens // quarter
-    turned = (block_of >> 1) + 2 * (block_of & 1)
-    spot = (group ^ turned) * quarter + tokens % quarter
-    picks = (spot[:, None] == tokens[None, :]).astype(BF16)
-    embedded = jnp.einsum(
-        "tp,ep->te",
-        jnp.concatenate([pixels, picks], axis=1),
-        embed_whole,
-        preferred_element_type=F32,
-    ).astype(BF16)
-    half = 2 * quarter
-    normed = norm_rows(embedded.astype(F32), attn_gain).astype(BF16)
-    attended = attend(normed, attn_own) + attend(normed, attn_far)
-    other = swap(attended[half:].astype(BF16), "mp", 1)
-    after_attn = embedded[:half].astype(F32) + (attended[:half] + other.astype(F32))
+    mine, other = attend(
+        where, (kept, opposite, neighbour, third), embed_whole, attn_own, attn_far, attn_gain
+    )
+    other = swap(other, "mp", 1)
+    after_attn = mine + other.astype(F32)
     normed2 = norm_rows(after_attn, mlp_gain).astype(BF16)
-    tokens2 = jnp.concatenate([normed2, swap(normed2, "mp", 1)])
-    feed = feed_forward(tokens2, up_weight, down_weight) + feed_forward(tokens2, up_far, down_far)
-    blocks = [feed[i * quarter : (i + 1) * quarter] for i in range(4)]
-    from_third = swap(blocks[3].astype(BF16), "mp", 3)
-    from_opposite = swap((after_attn[quarter:] + blocks[1]).astype(BF16), "mp", 2)
-    from_neighbour = swap(blocks[2].astype(BF16), "mp", 1)
-    kept_out = (after_attn[:quarter] + (blocks[0] + from_neighbour.astype(F32))).astype(BF16)
+    neighbour2 = swap(normed2, "mp", 1)
+    feed, up_own, down_own = feed_first(normed2, up_far, down_far, up_weight, down_weight)
+    from_opposite = swap((after_attn + feed)[quarter:].astype(BF16), "mp", 2)
+    for_near, for_third = feed_second(neighbour2, up_far, down_far, up_own, down_own)
+    from_third = swap(for_third, "mp", 3)
+    from_neighbour = swap(for_near, "mp", 1)
+    kept_out = (after_attn[:quarter] + (feed[:quarter] + from_neighbour.astype(F32))).astype(BF16)
     given_out = (from_opposite.astype(F32) + from_third.astype(F32)).astype(BF16)
     swapped = pair == 1
     return jnp.stack(

time: 112 us -> 118 us (1.054)
  matrix products: 17.8 us -> 0 us
  waiting for transfers between devices: 40.7 us -> 54.5 us
  Pallas kernels: 7.21 us -> 16 us
  starting transfers between devices: 31.4 us -> 35.9 us
  local copies, waits for them, and re-layouts: 6.78 us -> 4.3 us
    dot_general x11 -> x0, matrix products: 16.9 us -> none  [the longest x4 9.31 us: dot(): return jnp.dot(left, right, preferred_element_type=F32)]
    ppermute x20, waiting for transfers between devices: 36.6 us -> 46.4 us  [swap(): lax.ppermute(value, axis, [(i, i ^ bits) for i in range(lax.axis_size(axi...]
    pallas_call x0 -> x3, Pallas kernels: none -> 7.6 us  [the longest x1 4.76 us: attend(): pl.pallas_call(attend_kernel, in_specs=[SCALARS] + [FAST] * 8, out_specs=...]
    ppermute x20, starting transfers between devices: 27.2 us -> 31.6 us  [swap(): lax.ppermute(value, axis, [(i, i ^ bits) for i in range(lax.axis_size(axi...]
    all_to_all x1, waiting for transfers between devices: 4.07 us -> 8.05 us  [layer(): lax.all_to_all(outgoing, 'dp', split_axis=0, concat_axis=0, tiled=True)]
    unnamed x42 -> x22, local copies, waits for them, and re-layouts: 5.04 us -> 2.68 us
  transfers between devices with their start and end apart: 21 -> 21, of which waited for: 14 -> 18; matrix products, arithmetic and copies ran while one was open for 11% -> 1% of each run, Pallas kernels for 3% -> 11%
where the time goes in v4:
time: 118 us; the launch traced here: 117 us
  waiting for transfers between devices  54.5 us (46%)
  starting transfers between devices  35.9 us (30%)
  Pallas kernels  16 us (14%)
  local copies, waits for them, and re-layouts  4.3 us (4%)
  between operations  4.15 us (4%)
  other arithmetic  2.49 us (2%)
    ppermute x20, waiting for transfers between devices, swap(): lax.ppermute(value, axis, [(i, i ^ bits) for i in range(lax.axis_size(axi...  46.4 us
    ppermute x20, starting transfers between devices, swap(): lax.ppermute(value, axis, [(i, i ^ bits) for i in range(lax.axis_size(axi...  31.6 us
    all_to_all x1, waiting for transfers between devices, layer(): lax.all_to_all(outgoing, 'dp', split_axis=0, concat_axis=0, tiled=True)  8.05 us
    pallas_call x5, Pallas kernels, copier(): pl.pallas_call(body, in_specs=[SCALARS] + [FAST] * len(operands), out_spe...  5.28 us
    pallas_call x1, Pallas kernels, attend(): pl.pallas_call(attend_kernel, in_specs=[SCALARS] + [FAST] * 8, out_specs=...  4.76 us
    all_to_all x1, starting transfers between devices, layer(): lax.all_to_all(outgoing, 'dp', split_axis=0, concat_axis=0, tiled=True)  4.24 us
    unnamed x22, local copies, waits for them, and re-layouts  2.68 us
  transfers between devices with their start and end apart: 21, of which 18 were waited for; matrix products, arithmetic and copies ran while one was open for 1% of the time, Pallas kernels for 11%

profile of v4, /device:TPU:0, one launch (start us, length us, event | category | flops | bytes accessed | tf_op | source)
XLA Modules:
  0.0 117.2 jit_solution(5555709181845309716)
XLA Ops:
  0.0 2.1 %shard_map.118 = (bf16[8,64,768]{2,1,0:T(8,128)(2,1)}, s32[2]{0:T(128)}) custom-call(s32[1]{0:T(128)} %bitcast.2.own, s32[64]{0:T(128)} %owner_row.1, s32[16]{0:T(128)} %selected.1, s32[16]{0:T(128)} %dest_slot.1, bf16[8,64,768]{2,1,0:T(8,128)(2,1)} %candidates.1), custom_call_target="tpu_custom_call" | custom-call | tf_op jit(solution)/shard_map/pallas_call | solution.py:80
  2.1 0.1 pad_add_fusion.where
  2.2 1.1 pad_maximum_fusion.1.embed
  3.3 0.0 copy-start
  3.3 0.0 copy-start.2
  3.3 0.1 pad_maximum_fusion.attn.own
  3.4 0.6 copy-done.4
  4.0 0.7 copy-done
  4.7 0.4 copy-done.2
  5.0 1.0 shard_map.119
  6.0 4.1 %collective-permute-start.4 = (bf16[768,128]{1,0:T(8,128)(2,1)S(1)}, bf16[768,128]{1,0:T(8,128)(2,1)S(1)}, u32[]{:S(2)}, u32[]{:S(2)}) collective-permute-start(bf16[768,128]{1,0:T(8,128)(2,1)S(1)} %get-tuple-element.32), channel_id=1, source_target_pairs={{0,2},{1,3},{2,0},{3,1},{4,6},{5,7},{6,4},{7,5},{8,10},{9,11},{10,... | collective-permute-start | bytes 589832 | tf_op jit(solution)/shard_map/ppermute | solution.py:24
  10.2 1.6 %collective-permute-start.3 = (bf16[192,128]{1,0:T(8,128)(2,1)S(1)}, bf16[192,128]{1,0:T(8,128)(2,1)S(1)}, u32[]{:S(2)}, u32[]{:S(2)}) collective-permute-start(bf16[192,128]{1,0:T(8,128)(2,1)S(1)} %get-tuple-element.31), channel_id=1, source_target_pairs={{0,1},{1,0},{2,3},{3,2},{4,5},{5,4},{6,7},{7,6},{8,9},{9,8},{10,11... | collective-permute-start | bytes 147464 | tf_op jit(solution)/shard_map/ppermute | solution.py:24
  11.7 1.9 %collective-permute-start.11 = (bf16[192,768]{1,0:T(8,128)(2,1)S(1)}, bf16[192,768]{1,0:T(8,128)(2,1)S(1)}, u32[]{:S(2)}, u32[]{:S(2)}) collective-permute-start(bf16[192,768]{1,0:T(8,128)(2,1)S(1)} %get-tuple-element.37), channel_id=1, source_target_pairs={{0,2},{1,3},{2,0},{3,1},{4,6},{5,7},{6,4},{7,5},{8,10},{9,11},{10,... | collective-permute-start | bytes 884744 | tf_op jit(solution)/shard_map/ppermute | solution.py:24
  13.7 2.9 %collective-permute-done.3.neighbour = bf16[192,128]{1,0:T(8,128)(2,1)S(1)} collective-permute-done((bf16[192,128]{1,0:T(8,128)(2,1)S(1)}, bf16[192,128]{1,0:T(8,128)(2,1)S(1)}, u32[]{:S(2)}, u32[]{:S(2)}) %collective-permute-start.3) | collective-permute-done | bytes 49184 | tf_op jit(solution)/shard_map/ppermute | solution.py:24
  16.6 2.9 %collective-permute-done.5.third = bf16[192,128]{1,0:T(8,128)(2,1)S(1)} collective-permute-done((bf16[192,128]{1,0:T(8,128)(2,1)S(1)}, bf16[192,128]{1,0:T(8,128)(2,1)S(1)}, u32[]{:S(2)}, u32[]{:S(2)}) %collective-permute-start.5) | collective-permute-done | bytes 49184 | tf_op jit(solution)/shard_map/ppermute | solution.py:24
  19.4 8.1 %collective-permute-done.4.opposite = bf16[768,128]{1,0:T(8,128)(2,1)S(1)} collective-permute-done((bf16[768,128]{1,0:T(8,128)(2,1)S(1)}, bf16[768,128]{1,0:T(8,128)(2,1)S(1)}, u32[]{:S(2)}, u32[]{:S(2)}) %collective-permute-start.4) | collective-permute-done | bytes 196640 | tf_op jit(solution)/shard_map/ppermute | solution.py:24
  27.5 0.6 shard_map.120.refs_0_
  28.1 2.6 %collective-permute-start.6 = (bf16[1152,128]{1,0:T(8,128)(2,1)S(1)}, bf16[1152,128]{1,0:T(8,128)(2,1)S(1)}, u32[]{:S(2)}, u32[]{:S(2)}) collective-permute-start(bf16[1152,128]{1,0:T(8,128)(2,1)S(1)} %shard_map.120.refs_0_), channel_id=1, source_target_pairs={{0,8},{4,12},{8,0},{12,4},{16,24},{20,28},{24,16},{28,20},{1,9},{5... | collective-permute-start | bytes 884744 | tf_op jit(solution)/shard_map/ppermute | solution.py:24
  30.7 1.6 %collective-permute-start.7 = (bf16[1152,128]{1,0:T(8,128)(2,1)S(1)}, bf16[1152,128]{1,0:T(8,128)(2,1)S(1)}, u32[]{:S(2)}, u32[]{:S(2)}) collective-permute-start(bf16[1152,128]{1,0:T(8,128)(2,1)S(1)} %shard_map.120.refs_0_), channel_id=1, source_target_pairs={{0,16},{4,20},{8,24},{12,28},{16,0},{20,4},{24,8},{28,12},{1,17},{... | collective-permute-start | bytes 884744 | tf_op jit(solution)/shard_map/ppermute | solution.py:24
  32.2 2.5 %collective-permute-done.11.refs_0_ = bf16[192,768]{1,0:T(8,128)(2,1)S(1)} collective-permute-done((bf16[192,768]{1,0:T(8,128)(2,1)S(1)}, bf16[192,768]{1,0:T(8,128)(2,1)S(1)}, u32[]{:S(2)}, u32[]{:S(2)}) %collective-permute-start.11) | collective-permute-done | bytes 294944 | tf_op jit(solution)/shard_map/ppermute | solution.py:24
  34.7 1.6 %collective-permute-start.12 = (bf16[192,768]{1,0:T(8,128)(2,1)S(1)}, bf16[192,768]{1,0:T(8,128)(2,1)S(1)}, u32[]{:S(2)}, u32[]{:S(2)}) collective-permute-start(bf16[192,768]{1,0:T(8,128)(2,1)S(1)} %collective-permute-done.11.refs_0_), channel_id=1, source_target_pairs={{0,8},{4,12},{8,0},{12,4},{16,24},{20,28},{24,16},{28,20},{1,9},{5... | collective-permute-start | bytes 884744 | tf_op jit(solution)/shard_map/ppermute | solution.py:24
  36.3 1.6 %collective-permute-start.13 = (bf16[192,768]{1,0:T(8,128)(2,1)S(1)}, bf16[192,768]{1,0:T(8,128)(2,1)S(1)}, u32[]{:S(2)}, u32[]{:S(2)}) collective-permute-start(bf16[192,768]{1,0:T(8,128)(2,1)S(1)} %collective-permute-done.11.refs_0_), channel_id=1, source_target_pairs={{0,16},{4,20},{8,24},{12,28},{16,0},{20,4},{24,8},{28,12},{1,17},{... | collective-permute-start | bytes 884744 | tf_op jit(solution)/shard_map/ppermute | solution.py:24
  38.0 0.6 collective-permute-done.6.refs_1_
  38.5 3.0 %collective-permute-start.14 = (bf16[192,768]{1,0:T(8,128)(2,1)S(1)}, bf16[192,768]{1,0:T(8,128)(2,1)S(1)}, u32[]{:S(2)}, u32[]{:S(2)}) collective-permute-start(bf16[192,768]{1,0:T(8,128)(2,1)S(1)} %collective-permute-done.11.refs_0_), channel_id=1, source_target_pairs={{0,24},{4,28},{8,16},{12,20},{16,8},{20,12},{24,0},{28,4},{1,25},{... | collective-permute-start | bytes 884744 | tf_op jit(solution)/shard_map/ppermute | solution.py:24
  41.5 1.5 %collective-permute-done.7.refs_2_ = bf16[1152,128]{1,0:T(8,128)(2,1)S(1)} collective-permute-done((bf16[1152,128]{1,0:T(8,128)(2,1)S(1)}, bf16[1152,128]{1,0:T(8,128)(2,1)S(1)}, u32[]{:S(2)}, u32[]{:S(2)}) %collective-permute-start.7) | collective-permute-done | bytes 294944 | tf_op jit(solution)/shard_map/ppermute | solution.py:24
  43.0 2.9 %collective-permute-done.8.refs_3_ = bf16[1152,128]{1,0:T(8,128)(2,1)S(1)} collective-permute-done((bf16[1152,128]{1,0:T(8,128)(2,1)S(1)}, bf16[1152,128]{1,0:T(8,128)(2,1)S(1)}, u32[]{:S(2)}, u32[]{:S(2)}) %collective-permute-start.8) | collective-permute-done | bytes 294944 | tf_op jit(solution)/shard_map/ppermute | solution.py:24
  45.9 0.6 shard_map.121.mine
  46.5 0.1 collective-permute-start.9
  46.6 4.6 %collective-permute-done.12.refs_1_ = bf16[192,768]{1,0:T(8,128)(2,1)S(1)} collective-permute-done((bf16[192,768]{1,0:T(8,128)(2,1)S(1)}, bf16[192,768]{1,0:T(8,128)(2,1)S(1)}, u32[]{:S(2)}, u32[]{:S(2)}) %collective-permute-start.12) | collective-permute-done | bytes 294944 | tf_op jit(solution)/shard_map/ppermute | solution.py:24
  51.2 4.2 %collective-permute-done.13.refs_2_ = bf16[192,768]{1,0:T(8,128)(2,1)S(1)} collective-permute-done((bf16[192,768]{1,0:T(8,128)(2,1)S(1)}, bf16[192,768]{1,0:T(8,128)(2,1)S(1)}, u32[]{:S(2)}, u32[]{:S(2)}) %collective-permute-start.13) | collective-permute-done | bytes 294944 | tf_op jit(solution)/shard_map/ppermute | solution.py:24
  55.5 1.5 %collective-permute-done.14.refs_3_ = bf16[192,768]{1,0:T(8,128)(2,1)S(1)} collective-permute-done((bf16[192,768]{1,0:T(8,128)(2,1)S(1)}, bf16[192,768]{1,0:T(8,128)(2,1)S(1)}, u32[]{:S(2)}, u32[]{:S(2)}) %collective-permute-start.14) | collective-permute-done | bytes 294944 | tf_op jit(solution)/shard_map/ppermute | solution.py:24
  57.0 0.6 shard_map.124.mine
  57.6 0.0 copy-start.10
  57.7 0.1 collective-permute-start.15
  57.7 4.2 %all-to-all-start = ((bf16[8,64,768]{2,1,0:T(8,128)(2,1)}), bf16[8,64,768]{2,1,0:T(8,128)(2,1)}, u32[]{:S(2)}, u32[]{:S(2)}) async-start(bf16[8,64,768]{2,1,0:T(8,128)(2,1)} %get-tuple-element.25), calls=%async_computation | async-start | bytes 1572864 | tf_op jit(solution)/shard_map/all_to_all | solution.py:339
  62.0 0.7 fusion.4
  66.5 8.0 %all-to-all-done = bf16[8,64,768]{2,1,0:T(8,128)(2,1)} async-done(((bf16[8,64,768]{2,1,0:T(8,128)(2,1)}), bf16[8,64,768]{2,1,0:T(8,128)(2,1)}, u32[]{:S(2)}, u32[]{:S(2)}) %all-to-all-start) | async-done | bytes 786464 | tf_op jit(solution)/shard_map/all_to_all | solution.py:339
  74.6 1.0 dynamic-slice_bitcast_fusion
  75.5 3.9 %collective-permute-start = (bf16[64,768]{1,0:T(8,128)(2,1)S(1)}, bf16[64,768]{1,0:T(8,128)(2,1)S(1)}, u32[]{:S(2)}, u32[]{:S(2)}) collective-permute-start(bf16[64,768]{1,0:T(8,128)(2,1)S(1)} %get-tuple-element.49), channel_id=1, source_target_pairs={{0,2},{1,3},{2,0},{3,1},{4,6},{5,7},{6,4},{7,5},{8,10},{9,11},{10,... | collective-permute-start | bytes 294920 | tf_op jit(solution)/shard_map/ppermute | solution.py:24
  79.4 0.4 collective-permute-start.1
  79.8 1.1 collective-permute-start.2
  81.0 1.0 copy-done.5
  82.0 2.0 %shard_map.122 = (bf16[768,1024]{1,0:T(8,128)(2,1)S(1)}, bf16[768,768]{1,0:T(8,128)(2,1)S(1)}) custom-call(s32[2]{0:T(128)S(1)} %pad_add_fusion.where, bf16[192,1024]{1,0:T(8,128)(2,1)S(1)} %copy-done.5, bf16[4608,128]{1,0:T(8,128)(2,1)S(1)} %shard_map.121.mine, bf16[4608,128]{1,0:T(8,128)(2,1)} %collective-permute-done.9.others), custom_call_target="tpu_custom_call" | custom-call | tf_op jit(solution)/shard_map/pallas_call | solution.py:39
  84.0 0.2 collective-permute-done.opposite
  84.1 0.9 collective-permute-done.1.neighbour
  85.0 1.4 %collective-permute-done.2.third = bf16[64,768]{1,0:T(8,128)(2,1)S(1)} collective-permute-done((bf16[64,768]{1,0:T(8,128)(2,1)S(1)}, bf16[64,768]{1,0:T(8,128)(2,1)S(1)}, u32[]{:S(2)}, u32[]{:S(2)}) %collective-permute-start.2) | collective-permute-done | bytes 98336 | tf_op jit(solution)/shard_map/ppermute | solution.py:24
  86.4 4.8 %shard_map.123 = (f32[128,768]{1,0:T(8,128)S(1)}, bf16[128,768]{1,0:T(8,128)(2,1)S(1)}) custom-call(s32[2]{0:T(128)S(1)} %pad_add_fusion.where, bf16[64,768]{1,0:T(8,128)(2,1)S(1)} %get-tuple-element.50.kept, bf16[64,768]{1,0:T(8,128)(2,1)S(1)} %collective-permute-done.opposite, bf16[64,768]{1,0:T(8,128)(2,1)S(1)} %collective-permute-done.1.neighbour, ...), custom_call_target="tpu_custom_call" | custom-call | tf_op jit(solution)/shard_map/pallas_call | solution.py:252
  91.1 0.8 collective-permute-start.10
  92.0 0.0 copy-start.3
  92.0 1.5 %shard_map.125 = (bf16[768,768]{1,0:T(8,128)(2,1)S(1)}, bf16[768,768]{1,0:T(8,128)(2,1)S(1)}) custom-call(s32[2]{0:T(128)S(1)} %pad_add_fusion.where, bf16[768,768]{1,0:T(8,128)(2,1)S(1)} %shard_map.124.mine, bf16[768,768]{1,0:T(8,128)(2,1)} %collective-permute-done.15.others), custom_call_target="tpu_custom_call" | custom-call | tf_op jit(solution)/shard_map/pallas_call | solution.py:39
  93.5 5.0 %collective-permute-done.10 = bf16[128,768]{1,0:T(8,128)(2,1)S(1)} collective-permute-done((bf16[128,768]{1,0:T(8,128)(2,1)S(1)}, bf16[128,768]{1,0:T(8,128)(2,1)S(1)}, u32[]{:S(2)}, u32[]{:S(2)}) %collective-permute-start.10) | collective-permute-done | bytes 196640 | tf_op jit(solution)/shard_map/ppermute | solution.py:24
  98.5 0.1 fusion.3
  98.7 0.2 multiply_reduce_fusion
  98.9 0.1 multiply_convert_fusion.normed
  99.0 0.8 collective-permute-start.17
  99.8 1.8 %shard_map.126 = (f32[128,768]{1,0:T(8,128)S(1)}, bf16[768,768]{1,0:T(8,128)(2,1)S(1)}, bf16[768,768]{1,0:T(8,128)(2,1)S(1)}) custom-call(bf16[128,768]{1,0:T(8,128)(2,1)S(1)} %multiply_convert_fusion.normed, bf16[768,768]{1,0:T(8,128)(2,1)S(1)} %get-tuple-element.38.up_far, bf16[768,768]{1,0:T(8,128)(2,1)S(1)} %get-tuple-element.39.down_far, ...), custom_call_target="tpu_custom_call" | custom-call | tf_op jit(solution)/shard_map/pallas_call | solution.py:284
  101.6 3.0 %collective-permute-start.16 = (bf16[64,768]{1,0:T(8,128)(2,1)S(1)}, bf16[64,768]{1,0:T(8,128)(2,1)S(1)}, u32[]{:S(2)}, u32[]{:S(2)}) collective-permute-start(bf16[64,768]{1,0:T(8,128)(2,1)S(1)} %fusion.1), channel_id=1, source_target_pairs={{0,2},{1,3},{2,0},{3,1},{4,6},{5,7},{6,4},{7,5},{8,10},{9,11},{10,... | collective-permute-start | bytes 294920 | tf_op jit(solution)/shard_map/ppermute | solution.py:24
  104.6 2.7 %collective-permute-done.17.normed = bf16[128,768]{1,0:T(8,128)(2,1)S(1)} collective-permute-done((bf16[128,768]{1,0:T(8,128)(2,1)S(1)}, bf16[128,768]{1,0:T(8,128)(2,1)S(1)}, u32[]{:S(2)}, u32[]{:S(2)}) %collective-permute-start.17) | collective-permute-done | bytes 196640 | tf_op jit(solution)/shard_map/ppermute | solution.py:24
  107.3 1.0 shard_map.127
  108.3 3.5 %collective-permute-start.18 = (bf16[64,768]{1,0:T(8,128)(2,1)S(1)}, bf16[64,768]{1,0:T(8,128)(2,1)S(1)}, u32[]{:S(2)}, u32[]{:S(2)}) collective-permute-start(bf16[64,768]{1,0:T(8,128)(2,1)S(1)} %get-tuple-element.43), channel_id=1, source_target_pairs={{0,3},{1,2},{2,1},{3,0},{4,7},{5,6},{6,5},{7,4},{8,11},{9,10},{10,... | collective-permute-start | bytes 294920 | tf_op jit(solution)/shard_map/ppermute | solution.py:24
  111.8 3.0 %collective-permute-done.18 = bf16[64,768]{1,0:T(8,128)(2,1)S(1)} collective-permute-done((bf16[64,768]{1,0:T(8,128)(2,1)S(1)}, bf16[64,768]{1,0:T(8,128)(2,1)S(1)}, u32[]{:S(2)}, u32[]{:S(2)}) %collective-permute-start.18) | collective-permute-done | bytes 98336 | tf_op jit(solution)/shard_map/ppermute | solution.py:24
  114.8 1.6 %collective-permute-done.19 = bf16[64,768]{1,0:T(8,128)(2,1)S(1)} collective-permute-done((bf16[64,768]{1,0:T(8,128)(2,1)S(1)}, bf16[64,768]{1,0:T(8,128)(2,1)S(1)}, u32[]{:S(2)}, u32[]{:S(2)}) %collective-permute-start.19) | collective-permute-done | bytes 98336 | tf_op jit(solution)/shard_map/ppermute | solution.py:24
  116.4 0.1 select_bitcast_fusion.1
  116.5 0.7 pad_maximum_fusion.2
  (26 shorter events, 0.1 us)
Async XLA Ops:
  0.0 3.2 %copy-start.6 = (bf16[768,3,192]{0,2,1:T(8,128)(2,1)S(1)}, bf16[768,3,192]{0,2,1:T(8,128)(2,1)}, u32[]{:S(2)}) copy-start(bf16[768,3,192]{0,2,1:T(8,128)(2,1)} %param.18) | copy-start | bytes 2654212
  0.0 3.2 %copy-start.7 = (bf16[192,768]{1,0:T(8,128)(2,1)S(1)}, bf16[192,768]{1,0:T(8,128)(2,1)}, u32[]{:S(2)}) copy-start(bf16[192,768]{1,0:T(8,128)(2,1)} %param.19) | copy-start | bytes 884740
  3.2 0.8 copy-start.4
  3.3 1.4 %copy-start = (bf16[768,768]{1,0:T(8,128)(2,1)S(1)}, bf16[768,768]{1,0:T(8,128)(2,1)}, u32[]{:S(2)}) copy-start(bf16[768,768]{1,0:T(8,128)(2,1)} %up.3) | copy-start | bytes 3538948
  3.3 1.7 %copy-start.2 = (bf16[768,768]{1,0:T(8,128)(2,1)S(1)}, bf16[768,768]{1,0:T(8,128)(2,1)}, u32[]{:S(2)}) copy-start(bf16[768,768]{1,0:T(8,128)(2,1)} %down.3) | copy-start | bytes 3538948
  6.0 21.5 %collective-permute-start.4 = (bf16[768,128]{1,0:T(8,128)(2,1)S(1)}, bf16[768,128]{1,0:T(8,128)(2,1)S(1)}, u32[]{:S(2)}, u32[]{:S(2)}) collective-permute-start(bf16[768,128]{1,0:T(8,128)(2,1)S(1)} %get-tuple-element.32), channel_id=1, source_target_pairs={{0,2},{1,3},{2,0},{3,1},{4,6},{5,7},{6,4},{7,5},{8,10},{9,11},{10,... | collective-permute-start | bytes 589832 | tf_op jit(solution)/shard_map/ppermute | solution.py:24
  10.2 6.4 %collective-permute-start.3 = (bf16[192,128]{1,0:T(8,128)(2,1)S(1)}, bf16[192,128]{1,0:T(8,128)(2,1)S(1)}, u32[]{:S(2)}, u32[]{:S(2)}) collective-permute-start(bf16[192,128]{1,0:T(8,128)(2,1)S(1)} %get-tuple-element.31), channel_id=1, source_target_pairs={{0,1},{1,0},{2,3},{3,2},{4,5},{5,4},{6,7},{7,6},{8,9},{9,8},{10,11... | collective-permute-start | bytes 147464 | tf_op jit(solution)/shard_map/ppermute | solution.py:24
  11.7 7.7 %collective-permute-start.5 = (bf16[192,128]{1,0:T(8,128)(2,1)S(1)}, bf16[192,128]{1,0:T(8,128)(2,1)S(1)}, u32[]{:S(2)}, u32[]{:S(2)}) collective-permute-start(bf16[192,128]{1,0:T(8,128)(2,1)S(1)} %get-tuple-element.31), channel_id=1, source_target_pairs={{0,3},{1,2},{2,1},{3,0},{4,7},{5,6},{6,5},{7,4},{8,11},{9,10},{10,... | collective-permute-start | bytes 147464 | tf_op jit(solution)/shard_map/ppermute | solution.py:24
  11.7 23.0 %collective-permute-start.11 = (bf16[192,768]{1,0:T(8,128)(2,1)S(1)}, bf16[192,768]{1,0:T(8,128)(2,1)S(1)}, u32[]{:S(2)}, u32[]{:S(2)}) collective-permute-start(bf16[192,768]{1,0:T(8,128)(2,1)S(1)} %get-tuple-element.37), channel_id=1, source_target_pairs={{0,2},{1,3},{2,0},{3,1},{4,6},{5,7},{6,4},{7,5},{8,10},{9,11},{10,... | collective-permute-start | bytes 884744 | tf_op jit(solution)/shard_map/ppermute | solution.py:24
  28.1 10.5 %collective-permute-start.6 = (bf16[1152,128]{1,0:T(8,128)(2,1)S(1)}, bf16[1152,128]{1,0:T(8,128)(2,1)S(1)}, u32[]{:S(2)}, u32[]{:S(2)}) collective-permute-start(bf16[1152,128]{1,0:T(8,128)(2,1)S(1)} %shard_map.120.refs_0_), channel_id=1, source_target_pairs={{0,8},{4,12},{8,0},{12,4},{16,24},{20,28},{24,16},{28,20},{1,9},{5... | collective-permute-start | bytes 884744 | tf_op jit(solution)/shard_map/ppermute | solution.py:24
  30.7 12.3 %collective-permute-start.7 = (bf16[1152,128]{1,0:T(8,128)(2,1)S(1)}, bf16[1152,128]{1,0:T(8,128)(2,1)S(1)}, u32[]{:S(2)}, u32[]{:S(2)}) collective-permute-start(bf16[1152,128]{1,0:T(8,128)(2,1)S(1)} %shard_map.120.refs_0_), channel_id=1, source_target_pairs={{0,16},{4,20},{8,24},{12,28},{16,0},{20,4},{24,8},{28,12},{1,17},{... | collective-permute-start | bytes 884744 | tf_op jit(solution)/shard_map/ppermute | solution.py:24
  32.2 13.7 %collective-permute-start.8 = (bf16[1152,128]{1,0:T(8,128)(2,1)S(1)}, bf16[1152,128]{1,0:T(8,128)(2,1)S(1)}, u32[]{:S(2)}, u32[]{:S(2)}) collective-permute-start(bf16[1152,128]{1,0:T(8,128)(2,1)S(1)} %shard_map.120.refs_0_), channel_id=1, source_target_pairs={{0,24},{4,28},{8,16},{12,20},{16,8},{20,12},{24,0},{28,4},{1,25},{... | collective-permute-start | bytes 884744 | tf_op jit(solution)/shard_map/ppermute | solution.py:24
  34.7 16.5 %collective-permute-start.12 = (bf16[192,768]{1,0:T(8,128)(2,1)S(1)}, bf16[192,768]{1,0:T(8,128)(2,1)S(1)}, u32[]{:S(2)}, u32[]{:S(2)}) collective-permute-start(bf16[192,768]{1,0:T(8,128)(2,1)S(1)} %collective-permute-done.11.refs_0_), channel_id=1, source_target_pairs={{0,8},{4,12},{8,0},{12,4},{16,24},{20,28},{24,16},{28,20},{1,9},{5... | collective-permute-start | bytes 884744 | tf_op jit(solution)/shard_map/ppermute | solution.py:24
  36.3 19.2 %collective-permute-start.13 = (bf16[192,768]{1,0:T(8,128)(2,1)S(1)}, bf16[192,768]{1,0:T(8,128)(2,1)S(1)}, u32[]{:S(2)}, u32[]{:S(2)}) collective-permute-start(bf16[192,768]{1,0:T(8,128)(2,1)S(1)} %collective-permute-done.11.refs_0_), channel_id=1, source_target_pairs={{0,16},{4,20},{8,24},{12,28},{16,0},{20,4},{24,8},{28,12},{1,17},{... | collective-permute-start | bytes 884744 | tf_op jit(solution)/shard_map/ppermute | solution.py:24
  38.5 18.5 %collective-permute-start.14 = (bf16[192,768]{1,0:T(8,128)(2,1)S(1)}, bf16[192,768]{1,0:T(8,128)(2,1)S(1)}, u32[]{:S(2)}, u32[]{:S(2)}) collective-permute-start(bf16[192,768]{1,0:T(8,128)(2,1)S(1)} %collective-permute-done.11.refs_0_), channel_id=1, source_target_pairs={{0,24},{4,28},{8,16},{12,20},{16,8},{20,12},{24,0},{28,4},{1,25},{... | collective-permute-start | bytes 884744 | tf_op jit(solution)/shard_map/ppermute | solution.py:24
  46.5 34.5 %collective-permute-start.9 = (bf16[4608,128]{1,0:T(8,128)(2,1)S(1)}, bf16[4608,128]{1,0:T(8,128)(2,1)}, u32[]{:S(2)}, u32[]{:S(2)}) collective-permute-start(bf16[4608,128]{1,0:T(8,128)(2,1)S(1)} %shard_map.121.mine), channel_id=1, source_target_pairs={{0,4},{4,0},{8,12},{12,8},{16,20},{20,16},{24,28},{28,24},{1,5},{5... | collective-permute-start | bytes 3538952 | tf_op jit(solution)/shard_map/ppermute | solution.py:24
  57.6 4.4 %copy-start.9 = (s32[2]{0:T(128)S(1)}, s32[2]{0:T(128)}, u32[]{:S(2)}) copy-start(s32[2]{0:T(128)} %get-tuple-element.26) | copy-start | bytes 28
  57.6 23.3 %copy-start.10 = (bf16[768]{0:T(1024)(128)(2,1)S(1)}, bf16[768]{0:T(1024)(128)(2,1)}, u32[]{:S(2)}) copy-start(bf16[768]{0:T(1024)(128)(2,1)} %param.20) | copy-start | bytes 4612
  57.7 34.3 %collective-permute-start.15 = (bf16[768,768]{1,0:T(8,128)(2,1)S(1)}, bf16[768,768]{1,0:T(8,128)(2,1)}, u32[]{:S(2)}, u32[]{:S(2)}) collective-permute-start(bf16[768,768]{1,0:T(8,128)(2,1)S(1)} %shard_map.124.mine), channel_id=1, source_target_pairs={{0,4},{4,0},{8,12},{12,8},{16,20},{20,16},{24,28},{28,24},{1,5},{5... | collective-permute-start | bytes 3538952 | tf_op jit(solution)/shard_map/ppermute | solution.py:24
  57.7 16.8 %all-to-all-start = ((bf16[8,64,768]{2,1,0:T(8,128)(2,1)}), bf16[8,64,768]{2,1,0:T(8,128)(2,1)}, u32[]{:S(2)}, u32[]{:S(2)}) async-start(bf16[8,64,768]{2,1,0:T(8,128)(2,1)} %get-tuple-element.25), calls=%async_computation | async-start | bytes 1572864 | tf_op jit(solution)/shard_map/all_to_all | solution.py:339
  75.5 8.6 %collective-permute-start = (bf16[64,768]{1,0:T(8,128)(2,1)S(1)}, bf16[64,768]{1,0:T(8,128)(2,1)S(1)}, u32[]{:S(2)}, u32[]{:S(2)}) collective-permute-start(bf16[64,768]{1,0:T(8,128)(2,1)S(1)} %get-tuple-element.49), channel_id=1, source_target_pairs={{0,2},{1,3},{2,0},{3,1},{4,6},{5,7},{6,4},{7,5},{8,10},{9,11},{10,... | collective-permute-start | bytes 294920 | tf_op jit(solution)/shard_map/ppermute | solution.py:24
  79.4 5.5 %collective-permute-start.1 = (bf16[64,768]{1,0:T(8,128)(2,1)S(1)}, bf16[64,768]{1,0:T(8,128)(2,1)S(1)}, u32[]{:S(2)}, u32[]{:S(2)}) collective-permute-start(bf16[64,768]{1,0:T(8,128)(2,1)S(1)} %get-tuple-element.50.kept), channel_id=1, source_target_pairs={{0,1},{1,0},{2,3},{3,2},{4,5},{5,4},{6,7},{7,6},{8,9},{9,8},{10,11... | collective-permute-start | bytes 294920 | tf_op jit(solution)/shard_map/ppermute | solution.py:24
  79.8 6.5 %collective-permute-start.2 = (bf16[64,768]{1,0:T(8,128)(2,1)S(1)}, bf16[64,768]{1,0:T(8,128)(2,1)S(1)}, u32[]{:S(2)}, u32[]{:S(2)}) collective-permute-start(bf16[64,768]{1,0:T(8,128)(2,1)S(1)} %get-tuple-element.49), channel_id=1, source_target_pairs={{0,3},{1,2},{2,1},{3,0},{4,7},{5,6},{6,5},{7,4},{8,11},{9,10},{10,... | collective-permute-start | bytes 294920 | tf_op jit(solution)/shard_map/ppermute | solution.py:24
  81.0 1.0 copy-start.5
  86.4 5.6 %copy-start.8 = (bf16[768]{0:T(1024)(128)(2,1)S(1)}, bf16[768]{0:T(1024)(128)(2,1)}, u32[]{:S(2)}) copy-start(bf16[768]{0:T(1024)(128)(2,1)} %param.21) | copy-start | bytes 4612
  91.1 7.4 %collective-permute-start.10 = (bf16[128,768]{1,0:T(8,128)(2,1)S(1)}, bf16[128,768]{1,0:T(8,128)(2,1)S(1)}, u32[]{:S(2)}, u32[]{:S(2)}) collective-permute-start(bf16[128,768]{1,0:T(8,128)(2,1)S(1)} %get-tuple-element.36), channel_id=1, source_target_pairs={{0,1},{1,0},{2,3},{3,2},{4,5},{5,4},{6,7},{7,6},{8,9},{9,8},{10,11... | collective-permute-start | bytes 589832 | tf_op jit(solution)/shard_map/ppermute | solution.py:24
  92.0 7.8 %copy-start.3 = (bf16[768,768]{1,0:T(8,128)(2,1)S(1)}, bf16[768,768]{1,0:T(8,128)(2,1)}, u32[]{:S(2)}) copy-start(bf16[768,768]{1,0:T(8,128)(2,1)} %down.3) | copy-start | bytes 3538948
  93.5 6.2 %copy-start.1 = (bf16[768,768]{1,0:T(8,128)(2,1)S(1)}, bf16[768,768]{1,0:T(8,128)(2,1)}, u32[]{:S(2)}) copy-start(bf16[768,768]{1,0:T(8,128)(2,1)} %up.3) | copy-start | bytes 3538948
  99.0 8.3 %collective-permute-start.17 = (bf16[128,768]{1,0:T(8,128)(2,1)S(1)}, bf16[128,768]{1,0:T(8,128)(2,1)S(1)}, u32[]{:S(2)}, u32[]{:S(2)}) collective-permute-start(bf16[128,768]{1,0:T(8,128)(2,1)S(1)} %multiply_convert_fusion.normed), channel_id=1, source_target_pairs={{0,1},{1,0},{2,3},{3,2},{4,5},{5,4},{6,7},{7,6},{8,9},{9,8},{10,11... | collective-permute-start | bytes 589832 | tf_op jit(solution)/shard_map/ppermute | solution.py:24
  101.6 10.2 %collective-permute-start.16 = (bf16[64,768]{1,0:T(8,128)(2,1)S(1)}, bf16[64,768]{1,0:T(8,128)(2,1)S(1)}, u32[]{:S(2)}, u32[]{:S(2)}) collective-permute-start(bf16[64,768]{1,0:T(8,128)(2,1)S(1)} %fusion.1), channel_id=1, source_target_pairs={{0,2},{1,3},{2,0},{3,1},{4,6},{5,7},{6,4},{7,5},{8,10},{9,11},{10,... | collective-permute-start | bytes 294920 | tf_op jit(solution)/shard_map/ppermute | solution.py:24
  108.3 6.5 %collective-permute-start.18 = (bf16[64,768]{1,0:T(8,128)(2,1)S(1)}, bf16[64,768]{1,0:T(8,128)(2,1)S(1)}, u32[]{:S(2)}, u32[]{:S(2)}) collective-permute-start(bf16[64,768]{1,0:T(8,128)(2,1)S(1)} %get-tuple-element.43), channel_id=1, source_target_pairs={{0,3},{1,2},{2,1},{3,0},{4,7},{5,6},{6,5},{7,4},{8,11},{9,10},{10,... | collective-permute-start | bytes 294920 | tf_op jit(solution)/shard_map/ppermute | solution.py:24
  111.8 4.6 %collective-permute-start.19 = (bf16[64,768]{1,0:T(8,128)(2,1)S(1)}, bf16[64,768]{1,0:T(8,128)(2,1)S(1)}, u32[]{:S(2)}, u32[]{:S(2)}) collective-permute-start(bf16[64,768]{1,0:T(8,128)(2,1)S(1)} %get-tuple-element.44), channel_id=1, source_target_pairs={{0,1},{1,0},{2,3},{3,2},{4,5},{5,4},{6,7},{7,6},{8,9},{9,8},{10,11... | collective-permute-start | bytes 294920 | tf_op jit(solution)/shard_map/ppermute | solution.py:24

commit v5 on v4

--- a/solution.py
+++ b/solution.py
@@ -31,6 +31,7 @@
 ANY = pl.BlockSpec(memory_space=pl.ANY)
 SCALARS = pl.BlockSpec(memory_space=pltpu.SMEM)
 FAST = pl.BlockSpec(memory_space=pltpu.VMEM)
+SLOW = pl.BlockSpec(memory_space=pltpu.HBM)
 UNIT = 128
 SMALL = pltpu.CompilerParams(vmem_limit_bytes=4 * 1024 * 1024)
 
@@ -86,7 +87,47 @@
             jax.ShapeDtypeStruct((SEL_DEV,), jnp.int32),
         ),
         scratch_shapes=[pltpu.SemaphoreType.DMA((1,))],
+        compiler_params=pltpu.CompilerParams(vmem_limit_bytes=24 * 1024 * 1024),
     )(own, owner_row, selected, dest_slot, candidates)
+
+
+def choose_kernel(where, senders, incoming, kept, given, sem):
+    pair = where[1] // 2
+    copies = [
+        pltpu.make_async_copy(incoming.at[senders[pair]], kept, sem.at[0]),
+        pltpu.make_async_copy(incoming.at[senders[1 - pair]], given, sem.at[1]),
+    ]
+    for copy in copies:
+        copy.start()
+    for copy in copies:
+        copy.wait()
+
+
+def choose(where, senders, incoming):
+    shape = incoming.shape[1:]
+    return pl.pallas_call(
+        choose_kernel,
+        in_specs=[SCALARS, SCALARS, SLOW],
+        out_specs=(FAST, FAST),
+        out_shape=(pltpu.VMEM(shape, BF16), pltpu.VMEM(shape, BF16)),
+        scratch_shapes=[pltpu.SemaphoreType.DMA((2,))],
+        compiler_params=SMALL,
+    )(where, senders, pltpu.with_memory_space_constraint(incoming, pltpu.HBM))
+
+
+def widen_kernel(values, wide):
+    wide[...] = values[...].astype(F32)
+
+
+def widen(values):
+    row = values.reshape(1, -1)
+    return pl.pallas_call(
+        widen_kernel,
+        in_specs=[FAST],
+        out_specs=FAST,
+        out_shape=jax.ShapeDtypeStruct(row.shape, F32),
+        compiler_params=SMALL,
+    )(row)
 
 
 def attn_unit(array, unit):
@@ -131,7 +172,7 @@
     rows = embed.shape[0]
     return pl.pallas_call(
         extract_kernel,
-        in_specs=[SCALARS, FAST, FAST, ANY, ANY],
+        in_specs=[SCALARS, FAST, FAST, SLOW, SLOW],
         out_specs=(FAST, FAST, FAST),
         out_shape=(
             pltpu.VMEM((rows, UNIT), BF16),
@@ -144,8 +185,8 @@
         where,
         pltpu.with_memory_space_constraint(embed, pltpu.VMEM),
         pltpu.with_memory_space_constraint(attn, pltpu.VMEM),
-        up,
-        down,
+        pltpu.with_memory_space_constraint(up, pltpu.HBM),
+        pltpu.with_memory_space_constraint(down, pltpu.HBM),
     )
 
 
@@ -283,7 +324,7 @@
     held = [pltpu.with_memory_space_constraint(x, pltpu.VMEM) for x in (normed, up_far, down_far)]
     return pl.pallas_call(
         first_kernel,
-        in_specs=[FAST, FAST, FAST, ANY, ANY],
+        in_specs=[FAST, FAST, FAST, SLOW, SLOW],
         out_specs=(FAST, FAST, FAST),
         out_shape=(
             pltpu.VMEM((normed.shape[0], down.shape[1]), F32),
@@ -292,7 +333,7 @@
         ),
         scratch_shapes=[pltpu.SemaphoreType.DMA((2,))],
         compiler_params=pltpu.CompilerParams(vmem_limit_bytes=16 * 1024 * 1024),
-    )(*held, up, down)
+    )(*held, *(pltpu.with_memory_space_constraint(x, pltpu.HBM) for x in (up, down)))
 
 
 def second_kernel(normed, up_far, down_far, up_own, down_own, near, third):
@@ -338,9 +379,6 @@
     outgoing, senders = route(owner_row, selected, dest_slot, candidates)
     incoming = lax.all_to_all(outgoing, "dp", split_axis=0, concat_axis=0, tiled=True)
 
-    patch_weight, positions, qkv_weight, out_weight, _ = lax.optimization_barrier(
-        (patch_weight, positions, qkv_weight, out_weight, senders)
-    )
     pixel_width, width = patch_weight.shape
     model = out_weight.shape[1]
     embed_own = jnp.concatenate([patch_weight.T, positions.T], axis=1)
@@ -365,8 +403,7 @@
         *neighbours_of(where, mlp_piece),
     )
 
-    kept = lax.dynamic_index_in_dim(incoming, senders[pair], 0, keepdims=False)
-    given = lax.dynamic_index_in_dim(incoming, senders[1 - pair], 0, keepdims=False)
+    kept, given = choose(where, senders, incoming)
     third = swap(given, "mp", 3)
     opposite = swap(given, "mp", 2)
     neighbour = swap(kept, "mp", 1)
@@ -375,7 +412,8 @@
     )
     other = swap(other, "mp", 1)
     after_attn = mine + other.astype(F32)
-    normed2 = norm_rows(after_attn, mlp_gain).astype(BF16)
+    gain2 = widen(mlp_gain)
+    normed2 = norm_rows(after_attn, gain2).astype(BF16)
     neighbour2 = swap(normed2, "mp", 1)
     feed, up_own, down_own = feed_first(normed2, up_far, down_far, up_weight, down_weight)
     from_opposite = swap((after_attn + feed)[quarter:].astype(BF16), "mp", 2)

time: 118 us -> 113 us (0.958)
  blocking collectives: 0 us -> 15.8 us
  waiting for transfers between devices: 54.5 us -> 45.1 us
  starting transfers between devices: 35.9 us -> 31.1 us
  local copies, waits for them, and re-layouts: 4.3 us -> 0.04 us
  between operations: 4.15 us -> 0.25 us
  other arithmetic: 2.49 us -> 3.77 us
    all_to_all x0 -> x1, blocking collectives: none -> 15.8 us  [layer(): lax.all_to_all(outgoing, 'dp', split_axis=0, concat_axis=0, tiled=True)]
    all_to_all x1 -> x0, waiting for transfers between devices: 8.05 us -> none  [layer(): lax.all_to_all(outgoing, 'dp', split_axis=0, concat_axis=0, tiled=True)]
    all_to_all x1 -> x0, starting transfers between devices: 4.24 us -> none  [layer(): lax.all_to_all(outgoing, 'dp', split_axis=0, concat_axis=0, tiled=True)]
    pallas_call x2 -> x4, Pallas kernels: 2.83 us -> 5.57 us  [the longest x1 2.5 us: feed_first(): pl.pallas_call(first_kernel, in_specs=[FAST, FAST, FAST, SLOW, SLOW], out...]
    unnamed x22 -> x12, local copies, waits for them, and re-layouts: 2.68 us -> 0.04 us
    pallas_call x5, Pallas kernels: 5.28 us -> 3.72 us  [copier(): pl.pallas_call(body, in_specs=[SCALARS] + [FAST] * len(operands), out_spe...]
    ppermute x20, waiting for transfers between devices: 46.4 us -> 45.1 us  [swap(): lax.ppermute(value, axis, [(i, i ^ bits) for i in range(lax.axis_size(axi...]
    concatenate x1, other arithmetic: 0.08 us -> 1.34 us  [layer(): jnp.concatenate([qkv_weight.transpose(1, 2, 0).reshape(-1, model), out_we...]
  transfers between devices with their start and end apart: 21 -> 20, of which waited for: 18 -> 15; matrix products, arithmetic and copies ran while one was open for 1% -> 0% of each run, Pallas kernels for 11% -> 13%
where the time goes in v5:
time: 113 us
  waiting for transfers between devices  45.1 us (40%)
  starting transfers between devices  31.1 us (28%)
  Pallas kernels  16.6 us (15%)
  blocking collectives  15.8 us (14%)
  other arithmetic  3.77 us (3%)
    ppermute x20, waiting for transfers between devices, swap(): lax.ppermute(value, axis, [(i, i ^ bits) for i in range(lax.axis_size(axi...  45.1 us
    ppermute x20, starting transfers between devices, swap(): lax.ppermute(value, axis, [(i, i ^ bits) for i in range(lax.axis_size(axi...  31.1 us
    all_to_all x1, blocking collectives, layer(): lax.all_to_all(outgoing, 'dp', split_axis=0, concat_axis=0, tiled=True)  15.8 us
    pallas_call x1, Pallas kernels, attend(): pl.pallas_call(attend_kernel, in_specs=[SCALARS] + [FAST] * 8, out_specs=...  4.76 us
    pallas_call x5, Pallas kernels, copier(): pl.pallas_call(body, in_specs=[SCALARS] + [FAST] * len(operands), out_spe...  3.72 us
    pallas_call x1, Pallas kernels, feed_first(): pl.pallas_call(first_kernel, in_specs=[FAST, FAST, FAST, SLOW, SLOW], out...  2.5 us
  transfers between devices with their start and end apart: 20, of which 15 were waited for; matrix products, arithmetic and copies ran while one was open for 0% of the time, Pallas kernels for 13%

profile of v5, /device:TPU:0, one launch (start us, length us, event | category | flops | bytes accessed | tf_op | source)
XLA Modules:
  0.0 112.7 jit_solution(17229637810953055561)
XLA Ops:
  0.0 0.1 pad_add_fusion.where
  0.1 1.1 pad_maximum_fusion.1.embed
  1.1 1.3 %pad_maximum_fusion.attn.own = bf16[768,768]{1,0:T(8,128)(2,1)S(1)} fusion(bf16[192,768]{1,0:T(8,128)(2,1)} %param.19, bf16[576,768]{1,0:T(8,128)(2,1)} %bitcast.12), kind=kLoop, calls=%fused_computation | loop fusion | flops 2359296 | bytes 2359296 | tf_op jit(solution)/shard_map/concatenate | solution.py:385
  2.5 1.6 %shard_map.120 = (bf16[192,128]{1,0:T(8,128)(2,1)S(1)}, bf16[768,128]{1,0:T(8,128)(2,1)S(1)}, bf16[192,768]{1,0:T(8,128)(2,1)S(1)}) custom-call(s32[2]{0:T(128)S(1)} %pad_add_fusion.where, bf16[192,1024]{1,0:T(8,128)(2,1)S(1)} %pad_maximum_fusion.1.embed, bf16[768,768]{1,0:T(8,128)(2,1)S(1)} %pad_maximum_fusion.attn.own, bf16[768,768]{1,0:T(8,128)(2,1)} %up.3, ...), custom_call_target="tpu_custom_call" | custom-call | tf_op jit(solution)/shard_map/pallas_call | solution.py:173
  4.1 4.1 %collective-permute-start.4 = (bf16[768,128]{1,0:T(8,128)(2,1)S(1)}, bf16[768,128]{1,0:T(8,128)(2,1)S(1)}, u32[]{:S(2)}, u32[]{:S(2)}) collective-permute-start(bf16[768,128]{1,0:T(8,128)(2,1)S(1)} %get-tuple-element.28), channel_id=1, source_target_pairs={{0,2},{1,3},{2,0},{3,1},{4,6},{5,7},{6,4},{7,5},{8,10},{9,11},{10,... | collective-permute-start | bytes 589832 | tf_op jit(solution)/shard_map/ppermute | solution.py:24
  8.2 1.6 %collective-permute-start.3 = (bf16[192,128]{1,0:T(8,128)(2,1)S(1)}, bf16[192,128]{1,0:T(8,128)(2,1)S(1)}, u32[]{:S(2)}, u32[]{:S(2)}) collective-permute-start(bf16[192,128]{1,0:T(8,128)(2,1)S(1)} %get-tuple-element.27), channel_id=1, source_target_pairs={{0,1},{1,0},{2,3},{3,2},{4,5},{5,4},{6,7},{7,6},{8,9},{9,8},{10,11... | collective-permute-start | bytes 147464 | tf_op jit(solution)/shard_map/ppermute | solution.py:24
  9.8 0.0 collective-permute-start.5
  9.8 1.9 %collective-permute-start.11 = (bf16[192,768]{1,0:T(8,128)(2,1)S(1)}, bf16[192,768]{1,0:T(8,128)(2,1)S(1)}, u32[]{:S(2)}, u32[]{:S(2)}) collective-permute-start(bf16[192,768]{1,0:T(8,128)(2,1)S(1)} %get-tuple-element.33), channel_id=1, source_target_pairs={{0,2},{1,3},{2,0},{3,1},{4,6},{5,7},{6,4},{7,5},{8,10},{9,11},{10,... | collective-permute-start | bytes 884744 | tf_op jit(solution)/shard_map/ppermute | solution.py:24
  11.7 2.9 %collective-permute-done.3.neighbour = bf16[192,128]{1,0:T(8,128)(2,1)S(1)} collective-permute-done((bf16[192,128]{1,0:T(8,128)(2,1)S(1)}, bf16[192,128]{1,0:T(8,128)(2,1)S(1)}, u32[]{:S(2)}, u32[]{:S(2)}) %collective-permute-start.3) | collective-permute-done | bytes 49184 | tf_op jit(solution)/shard_map/ppermute | solution.py:24
  14.6 2.8 %collective-permute-done.5.third = bf16[192,128]{1,0:T(8,128)(2,1)S(1)} collective-permute-done((bf16[192,128]{1,0:T(8,128)(2,1)S(1)}, bf16[192,128]{1,0:T(8,128)(2,1)S(1)}, u32[]{:S(2)}, u32[]{:S(2)}) %collective-permute-start.5) | collective-permute-done | bytes 49184 | tf_op jit(solution)/shard_map/ppermute | solution.py:24
  17.4 8.1 %collective-permute-done.4.opposite = bf16[768,128]{1,0:T(8,128)(2,1)S(1)} collective-permute-done((bf16[768,128]{1,0:T(8,128)(2,1)S(1)}, bf16[768,128]{1,0:T(8,128)(2,1)S(1)}, u32[]{:S(2)}, u32[]{:S(2)}) %collective-permute-start.4) | collective-permute-done | bytes 196640 | tf_op jit(solution)/shard_map/ppermute | solution.py:24
  25.5 0.6 shard_map.121.refs_0_
  26.1 1.9 %collective-permute-start.6 = (bf16[1152,128]{1,0:T(8,128)(2,1)S(1)}, bf16[1152,128]{1,0:T(8,128)(2,1)S(1)}, u32[]{:S(2)}, u32[]{:S(2)}) collective-permute-start(bf16[1152,128]{1,0:T(8,128)(2,1)S(1)} %shard_map.121.refs_0_), channel_id=1, source_target_pairs={{0,8},{4,12},{8,0},{12,4},{16,24},{20,28},{24,16},{28,20},{1,9},{5... | collective-permute-start | bytes 884744 | tf_op jit(solution)/shard_map/ppermute | solution.py:24
  28.0 1.5 %collective-permute-start.7 = (bf16[1152,128]{1,0:T(8,128)(2,1)S(1)}, bf16[1152,128]{1,0:T(8,128)(2,1)S(1)}, u32[]{:S(2)}, u32[]{:S(2)}) collective-permute-start(bf16[1152,128]{1,0:T(8,128)(2,1)S(1)} %shard_map.121.refs_0_), channel_id=1, source_target_pairs={{0,16},{4,20},{8,24},{12,28},{16,0},{20,4},{24,8},{28,12},{1,17},{... | collective-permute-start | bytes 884744 | tf_op jit(solution)/shard_map/ppermute | solution.py:24
  29.5 0.2 collective-permute-start.8
  29.6 2.4 %collective-permute-done.11.refs_0_ = bf16[192,768]{1,0:T(8,128)(2,1)S(1)} collective-permute-done((bf16[192,768]{1,0:T(8,128)(2,1)S(1)}, bf16[192,768]{1,0:T(8,128)(2,1)S(1)}, u32[]{:S(2)}, u32[]{:S(2)}) %collective-permute-start.11) | collective-permute-done | bytes 294944 | tf_op jit(solution)/shard_map/ppermute | solution.py:24
  32.0 1.5 %collective-permute-start.12 = (bf16[192,768]{1,0:T(8,128)(2,1)S(1)}, bf16[192,768]{1,0:T(8,128)(2,1)S(1)}, u32[]{:S(2)}, u32[]{:S(2)}) collective-permute-start(bf16[192,768]{1,0:T(8,128)(2,1)S(1)} %collective-permute-done.11.refs_0_), channel_id=1, source_target_pairs={{0,8},{4,12},{8,0},{12,4},{16,24},{20,28},{24,16},{28,20},{1,9},{5... | collective-permute-start | bytes 884744 | tf_op jit(solution)/shard_map/ppermute | solution.py:24
  33.6 1.5 %collective-permute-start.13 = (bf16[192,768]{1,0:T(8,128)(2,1)S(1)}, bf16[192,768]{1,0:T(8,128)(2,1)S(1)}, u32[]{:S(2)}, u32[]{:S(2)}) collective-permute-start(bf16[192,768]{1,0:T(8,128)(2,1)S(1)} %collective-permute-done.11.refs_0_), channel_id=1, source_target_pairs={{0,16},{4,20},{8,24},{12,28},{16,0},{20,4},{24,8},{28,12},{1,17},{... | collective-permute-start | bytes 884744 | tf_op jit(solution)/shard_map/ppermute | solution.py:24
  35.1 0.9 collective-permute-done.6.refs_1_
  36.0 2.8 %collective-permute-start.14 = (bf16[192,768]{1,0:T(8,128)(2,1)S(1)}, bf16[192,768]{1,0:T(8,128)(2,1)S(1)}, u32[]{:S(2)}, u32[]{:S(2)}) collective-permute-start(bf16[192,768]{1,0:T(8,128)(2,1)S(1)} %collective-permute-done.11.refs_0_), channel_id=1, source_target_pairs={{0,24},{4,28},{8,16},{12,20},{16,8},{20,12},{24,0},{28,4},{1,25},{... | collective-permute-start | bytes 884744 | tf_op jit(solution)/shard_map/ppermute | solution.py:24
  38.8 2.2 %collective-permute-done.7.refs_2_ = bf16[1152,128]{1,0:T(8,128)(2,1)S(1)} collective-permute-done((bf16[1152,128]{1,0:T(8,128)(2,1)S(1)}, bf16[1152,128]{1,0:T(8,128)(2,1)S(1)}, u32[]{:S(2)}, u32[]{:S(2)}) %collective-permute-start.7) | collective-permute-done | bytes 294944 | tf_op jit(solution)/shard_map/ppermute | solution.py:24
  41.0 2.6 %collective-permute-done.8.refs_3_ = bf16[1152,128]{1,0:T(8,128)(2,1)S(1)} collective-permute-done((bf16[1152,128]{1,0:T(8,128)(2,1)S(1)}, bf16[1152,128]{1,0:T(8,128)(2,1)S(1)}, u32[]{:S(2)}, u32[]{:S(2)}) %collective-permute-start.8) | collective-permute-done | bytes 294944 | tf_op jit(solution)/shard_map/ppermute | solution.py:24
  43.6 0.6 shard_map.122.mine
  44.2 0.0 copy-start
  44.3 0.0 copy-start.1
  44.3 0.0 copy-start.2
  44.3 0.0 copy-start.3
  44.3 0.1 collective-permute-start.9
  44.4 4.3 %collective-permute-done.12.refs_1_ = bf16[192,768]{1,0:T(8,128)(2,1)S(1)} collective-permute-done((bf16[192,768]{1,0:T(8,128)(2,1)S(1)}, bf16[192,768]{1,0:T(8,128)(2,1)S(1)}, u32[]{:S(2)}, u32[]{:S(2)}) %collective-permute-start.12) | collective-permute-done | bytes 294944 | tf_op jit(solution)/shard_map/ppermute | solution.py:24
  48.7 4.7 %collective-permute-done.13.refs_2_ = bf16[192,768]{1,0:T(8,128)(2,1)S(1)} collective-permute-done((bf16[192,768]{1,0:T(8,128)(2,1)S(1)}, bf16[192,768]{1,0:T(8,128)(2,1)S(1)}, u32[]{:S(2)}, u32[]{:S(2)}) %collective-permute-start.13) | collective-permute-done | bytes 294944 | tf_op jit(solution)/shard_map/ppermute | solution.py:24
  53.5 0.0 collective-permute-done.14.refs_3_
  53.5 0.6 shard_map.126.mine
  54.1 0.1 collective-permute-start.15
  54.2 1.6 %shard_map.118 = (bf16[8,64,768]{2,1,0:T(8,128)(2,1)S(1)}, s32[2]{0:T(128)S(1)}) custom-call(s32[1]{0:T(128)} %bitcast.2.own, s32[64]{0:T(128)S(1)} %copy-done.1, s32[16]{0:T(128)S(1)} %copy-done.2, s32[16]{0:T(128)S(1)} %copy-done.3, bf16[8,64,768]{2,1,0:T(8,128)(2,1)S(1)} %copy-done), custom_call_target="tpu_custom_call" | custom-call | tf_op jit(solution)/shard_map/pallas_call | solution.py:81
  55.8 0.0 copy-start.4
  55.8 15.8 %all_to_all.5.incoming = bf16[8,64,768]{2,1,0:T(8,128)(2,1)} all-to-all(bf16[8,64,768]{2,1,0:T(8,128)(2,1)S(1)} %get-tuple-element.24), channel_id=1, replica_groups=mesh['dp'=8,'mp'=4] {'dp'}, dimensions={0} | all-to-all | bytes 1572864 | tf_op jit(solution)/shard_map/all_to_all | solution.py:380
  71.6 1.5 %shard_map.119 = (bf16[64,768]{1,0:T(8,128)(2,1)S(1)}, bf16[64,768]{1,0:T(8,128)(2,1)S(1)}) custom-call(s32[2]{0:T(128)S(1)} %pad_add_fusion.where, s32[2]{0:T(128)S(1)} %get-tuple-element.23.senders, bf16[8,64,768]{2,1,0:T(8,128)(2,1)} %all_to_all.5.incoming), custom_call_target="tpu_custom_call" | custom-call | tf_op jit(solution)/shard_map/pallas_call | solution.py:108
  73.1 4.7 %collective-permute-start = (bf16[64,768]{1,0:T(8,128)(2,1)S(1)}, bf16[64,768]{1,0:T(8,128)(2,1)S(1)}, u32[]{:S(2)}, u32[]{:S(2)}) collective-permute-start(bf16[64,768]{1,0:T(8,128)(2,1)S(1)} %get-tuple-element.26), channel_id=1, source_target_pairs={{0,2},{1,3},{2,0},{3,1},{4,6},{5,7},{6,4},{7,5},{8,10},{9,11},{10,... | collective-permute-start | bytes 294920 | tf_op jit(solution)/shard_map/ppermute | solution.py:24
  77.8 0.4 collective-permute-start.1
  78.2 1.1 %collective-permute-start.2 = (bf16[64,768]{1,0:T(8,128)(2,1)S(1)}, bf16[64,768]{1,0:T(8,128)(2,1)S(1)}, u32[]{:S(2)}, u32[]{:S(2)}) collective-permute-start(bf16[64,768]{1,0:T(8,128)(2,1)S(1)} %get-tuple-element.26), channel_id=1, source_target_pairs={{0,3},{1,2},{2,1},{3,0},{4,7},{5,6},{6,5},{7,4},{8,11},{9,10},{10,... | collective-permute-start | bytes 294920 | tf_op jit(solution)/shard_map/ppermute | solution.py:24
  79.4 0.0 collective-permute-done.9.others
  79.4 1.2 %shard_map.123 = (bf16[768,1024]{1,0:T(8,128)(2,1)S(1)}, bf16[768,768]{1,0:T(8,128)(2,1)S(1)}) custom-call(s32[2]{0:T(128)S(1)} %pad_add_fusion.where, bf16[192,1024]{1,0:T(8,128)(2,1)S(1)} %pad_maximum_fusion.1.embed, bf16[4608,128]{1,0:T(8,128)(2,1)S(1)} %shard_map.122.mine, bf16[4608,128]{1,0:T(8,128)(2,1)S(1)} %collective-permute-done.9.others), custom_call_target="tpu_custom_call" | custom-call | tf_op jit(solution)/shard_map/pallas_call | solution.py:40
  80.6 3.0 %collective-permute-done.opposite = bf16[64,768]{1,0:T(8,128)(2,1)S(1)} collective-permute-done((bf16[64,768]{1,0:T(8,128)(2,1)S(1)}, bf16[64,768]{1,0:T(8,128)(2,1)S(1)}, u32[]{:S(2)}, u32[]{:S(2)}) %collective-permute-start) | collective-permute-done | bytes 98336 | tf_op jit(solution)/shard_map/ppermute | solution.py:24
  83.6 1.7 %collective-permute-done.1.neighbour = bf16[64,768]{1,0:T(8,128)(2,1)S(1)} collective-permute-done((bf16[64,768]{1,0:T(8,128)(2,1)S(1)}, bf16[64,768]{1,0:T(8,128)(2,1)S(1)}, u32[]{:S(2)}, u32[]{:S(2)}) %collective-permute-start.1) | collective-permute-done | bytes 98336 | tf_op jit(solution)/shard_map/ppermute | solution.py:24
  85.3 0.0 collective-permute-done.2.third
  85.3 4.8 %shard_map.124 = (f32[128,768]{1,0:T(8,128)S(1)}, bf16[128,768]{1,0:T(8,128)(2,1)S(1)}) custom-call(s32[2]{0:T(128)S(1)} %pad_add_fusion.where, bf16[64,768]{1,0:T(8,128)(2,1)S(1)} %get-tuple-element.25.kept, bf16[64,768]{1,0:T(8,128)(2,1)S(1)} %collective-permute-done.opposite, bf16[64,768]{1,0:T(8,128)(2,1)S(1)} %collective-permute-done.1.neighbour, ...), custom_call_target="tpu_custom_call" | custom-call | tf_op jit(solution)/shard_map/pallas_call | solution.py:293
  90.1 1.7 %collective-permute-start.10 = (bf16[128,768]{1,0:T(8,128)(2,1)S(1)}, bf16[128,768]{1,0:T(8,128)(2,1)S(1)}, u32[]{:S(2)}, u32[]{:S(2)}) collective-permute-start(bf16[128,768]{1,0:T(8,128)(2,1)S(1)} %get-tuple-element.32), channel_id=1, source_target_pairs={{0,1},{1,0},{2,3},{3,2},{4,5},{5,4},{6,7},{7,6},{8,9},{9,8},{10,11... | collective-permute-start | bytes 589832 | tf_op jit(solution)/shard_map/ppermute | solution.py:24
  91.8 0.0 collective-permute-done.15.others
  91.8 0.7 shard_map.127
  92.5 4.1 %collective-permute-done.10 = bf16[128,768]{1,0:T(8,128)(2,1)S(1)} collective-permute-done((bf16[128,768]{1,0:T(8,128)(2,1)S(1)}, bf16[128,768]{1,0:T(8,128)(2,1)S(1)}, u32[]{:S(2)}, u32[]{:S(2)}) %collective-permute-start.10) | collective-permute-done | bytes 196640 | tf_op jit(solution)/shard_map/ppermute | solution.py:24
  96.6 0.1 fusion.3
  96.7 0.2 multiply_reduce_fusion
  96.9 0.1 multiply_convert_fusion.normed
  97.1 1.8 %collective-permute-start.17 = (bf16[128,768]{1,0:T(8,128)(2,1)S(1)}, bf16[128,768]{1,0:T(8,128)(2,1)S(1)}, u32[]{:S(2)}, u32[]{:S(2)}) collective-permute-start(bf16[128,768]{1,0:T(8,128)(2,1)S(1)} %multiply_convert_fusion.normed), channel_id=1, source_target_pairs={{0,1},{1,0},{2,3},{3,2},{4,5},{5,4},{6,7},{7,6},{8,9},{9,8},{10,11... | collective-permute-start | bytes 589832 | tf_op jit(solution)/shard_map/ppermute | solution.py:24
  98.9 2.5 %shard_map.128 = (f32[128,768]{1,0:T(8,128)S(1)}, bf16[768,768]{1,0:T(8,128)(2,1)S(1)}, bf16[768,768]{1,0:T(8,128)(2,1)S(1)}) custom-call(bf16[128,768]{1,0:T(8,128)(2,1)S(1)} %multiply_convert_fusion.normed, bf16[768,768]{1,0:T(8,128)(2,1)S(1)} %get-tuple-element.34.up_far, bf16[768,768]{1,0:T(8,128)(2,1)S(1)} %get-tuple-element.35.down_far, ...), custom_call_target="tpu_custom_call" | custom-call | tf_op jit(solution)/shard_map/pallas_call | solution.py:325
  101.4 0.7 collective-permute-start.16
  102.1 1.0 collective-permute-done.17.normed
  103.2 1.0 shard_map.129
  104.2 2.6 %collective-permute-start.18 = (bf16[64,768]{1,0:T(8,128)(2,1)S(1)}, bf16[64,768]{1,0:T(8,128)(2,1)S(1)}, u32[]{:S(2)}, u32[]{:S(2)}) collective-permute-start(bf16[64,768]{1,0:T(8,128)(2,1)S(1)} %get-tuple-element.39), channel_id=1, source_target_pairs={{0,3},{1,2},{2,1},{3,0},{4,7},{5,6},{6,5},{7,4},{8,11},{9,10},{10,... | collective-permute-start | bytes 294920 | tf_op jit(solution)/shard_map/ppermute | solution.py:24
  106.8 0.9 collective-permute-start.19
  107.7 3.2 %collective-permute-done.16 = bf16[64,768]{1,0:T(8,128)(2,1)S(1)} collective-permute-done((bf16[64,768]{1,0:T(8,128)(2,1)S(1)}, bf16[64,768]{1,0:T(8,128)(2,1)S(1)}, u32[]{:S(2)}, u32[]{:S(2)}) %collective-permute-start.16) | collective-permute-done | bytes 98336 | tf_op jit(solution)/shard_map/ppermute | solution.py:24
  110.9 1.0 collective-permute-done.19
  111.9 0.1 select_bitcast_fusion.1
  112.0 0.7 pad_maximum_fusion.2
  (16 shorter events, 0.1 us)
Async XLA Ops:
  4.1 21.5 %collective-permute-start.4 = (bf16[768,128]{1,0:T(8,128)(2,1)S(1)}, bf16[768,128]{1,0:T(8,128)(2,1)S(1)}, u32[]{:S(2)}, u32[]{:S(2)}) collective-permute-start(bf16[768,128]{1,0:T(8,128)(2,1)S(1)} %get-tuple-element.28), channel_id=1, source_target_pairs={{0,2},{1,3},{2,0},{3,1},{4,6},{5,7},{6,4},{7,5},{8,10},{9,11},{10,... | collective-permute-start | bytes 589832 | tf_op jit(solution)/shard_map/ppermute | solution.py:24
  8.2 6.4 %collective-permute-start.3 = (bf16[192,128]{1,0:T(8,128)(2,1)S(1)}, bf16[192,128]{1,0:T(8,128)(2,1)S(1)}, u32[]{:S(2)}, u32[]{:S(2)}) collective-permute-start(bf16[192,128]{1,0:T(8,128)(2,1)S(1)} %get-tuple-element.27), channel_id=1, source_target_pairs={{0,1},{1,0},{2,3},{3,2},{4,5},{5,4},{6,7},{7,6},{8,9},{9,8},{10,11... | collective-permute-start | bytes 147464 | tf_op jit(solution)/shard_map/ppermute | solution.py:24
  9.8 7.6 %collective-permute-start.5 = (bf16[192,128]{1,0:T(8,128)(2,1)S(1)}, bf16[192,128]{1,0:T(8,128)(2,1)S(1)}, u32[]{:S(2)}, u32[]{:S(2)}) collective-permute-start(bf16[192,128]{1,0:T(8,128)(2,1)S(1)} %get-tuple-element.27), channel_id=1, source_target_pairs={{0,3},{1,2},{2,1},{3,0},{4,7},{5,6},{6,5},{7,4},{8,11},{9,10},{10,... | collective-permute-start | bytes 147464 | tf_op jit(solution)/shard_map/ppermute | solution.py:24
  9.8 22.3 %collective-permute-start.11 = (bf16[192,768]{1,0:T(8,128)(2,1)S(1)}, bf16[192,768]{1,0:T(8,128)(2,1)S(1)}, u32[]{:S(2)}, u32[]{:S(2)}) collective-permute-start(bf16[192,768]{1,0:T(8,128)(2,1)S(1)} %get-tuple-element.33), channel_id=1, source_target_pairs={{0,2},{1,3},{2,0},{3,1},{4,6},{5,7},{6,4},{7,5},{8,10},{9,11},{10,... | collective-permute-start | bytes 884744 | tf_op jit(solution)/shard_map/ppermute | solution.py:24
  26.1 9.9 %collective-permute-start.6 = (bf16[1152,128]{1,0:T(8,128)(2,1)S(1)}, bf16[1152,128]{1,0:T(8,128)(2,1)S(1)}, u32[]{:S(2)}, u32[]{:S(2)}) collective-permute-start(bf16[1152,128]{1,0:T(8,128)(2,1)S(1)} %shard_map.121.refs_0_), channel_id=1, source_target_pairs={{0,8},{4,12},{8,0},{12,4},{16,24},{20,28},{24,16},{28,20},{1,9},{5... | collective-permute-start | bytes 884744 | tf_op jit(solution)/shard_map/ppermute | solution.py:24
  28.0 13.0 %collective-permute-start.7 = (bf16[1152,128]{1,0:T(8,128)(2,1)S(1)}, bf16[1152,128]{1,0:T(8,128)(2,1)S(1)}, u32[]{:S(2)}, u32[]{:S(2)}) collective-permute-start(bf16[1152,128]{1,0:T(8,128)(2,1)S(1)} %shard_map.121.refs_0_), channel_id=1, source_target_pairs={{0,16},{4,20},{8,24},{12,28},{16,0},{20,4},{24,8},{28,12},{1,17},{... | collective-permute-start | bytes 884744 | tf_op jit(solution)/shard_map/ppermute | solution.py:24
  29.5 14.1 %collective-permute-start.8 = (bf16[1152,128]{1,0:T(8,128)(2,1)S(1)}, bf16[1152,128]{1,0:T(8,128)(2,1)S(1)}, u32[]{:S(2)}, u32[]{:S(2)}) collective-permute-start(bf16[1152,128]{1,0:T(8,128)(2,1)S(1)} %shard_map.121.refs_0_), channel_id=1, source_target_pairs={{0,24},{4,28},{8,16},{12,20},{16,8},{20,12},{24,0},{28,4},{1,25},{... | collective-permute-start | bytes 884744 | tf_op jit(solution)/shard_map/ppermute | solution.py:24
  32.0 16.7 %collective-permute-start.12 = (bf16[192,768]{1,0:T(8,128)(2,1)S(1)}, bf16[192,768]{1,0:T(8,128)(2,1)S(1)}, u32[]{:S(2)}, u32[]{:S(2)}) collective-permute-start(bf16[192,768]{1,0:T(8,128)(2,1)S(1)} %collective-permute-done.11.refs_0_), channel_id=1, source_target_pairs={{0,8},{4,12},{8,0},{12,4},{16,24},{20,28},{24,16},{28,20},{1,9},{5... | collective-permute-start | bytes 884744 | tf_op jit(solution)/shard_map/ppermute | solution.py:24
  33.6 19.9 %collective-permute-start.13 = (bf16[192,768]{1,0:T(8,128)(2,1)S(1)}, bf16[192,768]{1,0:T(8,128)(2,1)S(1)}, u32[]{:S(2)}, u32[]{:S(2)}) collective-permute-start(bf16[192,768]{1,0:T(8,128)(2,1)S(1)} %collective-permute-done.11.refs_0_), channel_id=1, source_target_pairs={{0,16},{4,20},{8,24},{12,28},{16,0},{20,4},{24,8},{28,12},{1,17},{... | collective-permute-start | bytes 884744 | tf_op jit(solution)/shard_map/ppermute | solution.py:24
  36.0 17.4 %collective-permute-start.14 = (bf16[192,768]{1,0:T(8,128)(2,1)S(1)}, bf16[192,768]{1,0:T(8,128)(2,1)S(1)}, u32[]{:S(2)}, u32[]{:S(2)}) collective-permute-start(bf16[192,768]{1,0:T(8,128)(2,1)S(1)} %collective-permute-done.11.refs_0_), channel_id=1, source_target_pairs={{0,24},{4,28},{8,16},{12,20},{16,8},{20,12},{24,0},{28,4},{1,25},{... | collective-permute-start | bytes 884744 | tf_op jit(solution)/shard_map/ppermute | solution.py:24
  44.2 9.9 %copy-start = (bf16[8,64,768]{2,1,0:T(8,128)(2,1)S(1)}, bf16[8,64,768]{2,1,0:T(8,128)(2,1)}, u32[]{:S(2)}) copy-start(bf16[8,64,768]{2,1,0:T(8,128)(2,1)} %candidates.1) | copy-start | bytes 2359300
  44.3 9.9 %copy-start.1 = (s32[64]{0:T(128)S(1)}, s32[64]{0:T(128)}, u32[]{:S(2)}) copy-start(s32[64]{0:T(128)} %owner_row.1) | copy-start | bytes 772
  44.3 9.9 %copy-start.2 = (s32[16]{0:T(128)S(1)}, s32[16]{0:T(128)}, u32[]{:S(2)}) copy-start(s32[16]{0:T(128)} %selected.1) | copy-start | bytes 196
  44.3 9.9 %copy-start.3 = (s32[16]{0:T(128)S(1)}, s32[16]{0:T(128)}, u32[]{:S(2)}) copy-start(s32[16]{0:T(128)} %dest_slot.1) | copy-start | bytes 196
  44.3 35.1 %collective-permute-start.9 = (bf16[4608,128]{1,0:T(8,128)(2,1)S(1)}, bf16[4608,128]{1,0:T(8,128)(2,1)S(1)}, u32[]{:S(2)}, u32[]{:S(2)}) collective-permute-start(bf16[4608,128]{1,0:T(8,128)(2,1)S(1)} %shard_map.122.mine), channel_id=1, source_target_pairs={{0,4},{4,0},{8,12},{12,8},{16,20},{20,16},{24,28},{28,24},{1,5},{5... | collective-permute-start | bytes 3538952 | tf_op jit(solution)/shard_map/ppermute | solution.py:24
  54.1 37.7 %collective-permute-start.15 = (bf16[768,768]{1,0:T(8,128)(2,1)S(1)}, bf16[768,768]{1,0:T(8,128)(2,1)S(1)}, u32[]{:S(2)}, u32[]{:S(2)}) collective-permute-start(bf16[768,768]{1,0:T(8,128)(2,1)S(1)} %shard_map.126.mine), channel_id=1, source_target_pairs={{0,4},{4,0},{8,12},{12,8},{16,20},{20,16},{24,28},{28,24},{1,5},{5... | collective-permute-start | bytes 3538952 | tf_op jit(solution)/shard_map/ppermute | solution.py:24
  55.8 23.6 %copy-start.4 = (bf16[768]{0:T(1024)(128)(2,1)S(1)}, bf16[768]{0:T(1024)(128)(2,1)}, u32[]{:S(2)}) copy-start(bf16[768]{0:T(1024)(128)(2,1)} %param.20) | copy-start | bytes 4612
  73.1 10.5 %collective-permute-start = (bf16[64,768]{1,0:T(8,128)(2,1)S(1)}, bf16[64,768]{1,0:T(8,128)(2,1)S(1)}, u32[]{:S(2)}, u32[]{:S(2)}) collective-permute-start(bf16[64,768]{1,0:T(8,128)(2,1)S(1)} %get-tuple-element.26), channel_id=1, source_target_pairs={{0,2},{1,3},{2,0},{3,1},{4,6},{5,7},{6,4},{7,5},{8,10},{9,11},{10,... | collective-permute-start | bytes 294920 | tf_op jit(solution)/shard_map/ppermute | solution.py:24
  77.8 7.5 %collective-permute-start.1 = (bf16[64,768]{1,0:T(8,128)(2,1)S(1)}, bf16[64,768]{1,0:T(8,128)(2,1)S(1)}, u32[]{:S(2)}, u32[]{:S(2)}) collective-permute-start(bf16[64,768]{1,0:T(8,128)(2,1)S(1)} %get-tuple-element.25.kept), channel_id=1, source_target_pairs={{0,1},{1,0},{2,3},{3,2},{4,5},{5,4},{6,7},{7,6},{8,9},{9,8},{10,11... | collective-permute-start | bytes 294920 | tf_op jit(solution)/shard_map/ppermute | solution.py:24
  78.2 7.1 %collective-permute-start.2 = (bf16[64,768]{1,0:T(8,128)(2,1)S(1)}, bf16[64,768]{1,0:T(8,128)(2,1)S(1)}, u32[]{:S(2)}, u32[]{:S(2)}) collective-permute-start(bf16[64,768]{1,0:T(8,128)(2,1)S(1)} %get-tuple-element.26), channel_id=1, source_target_pairs={{0,3},{1,2},{2,1},{3,0},{4,7},{5,6},{6,5},{7,4},{8,11},{9,10},{10,... | collective-permute-start | bytes 294920 | tf_op jit(solution)/shard_map/ppermute | solution.py:24
  85.3 6.5 %copy-start.5 = (bf16[768]{0:T(1024)(128)(2,1)S(1)}, bf16[768]{0:T(1024)(128)(2,1)}, u32[]{:S(2)}) copy-start(bf16[768]{0:T(1024)(128)(2,1)} %param.21) | copy-start | bytes 4612
  90.1 6.5 %collective-permute-start.10 = (bf16[128,768]{1,0:T(8,128)(2,1)S(1)}, bf16[128,768]{1,0:T(8,128)(2,1)S(1)}, u32[]{:S(2)}, u32[]{:S(2)}) collective-permute-start(bf16[128,768]{1,0:T(8,128)(2,1)S(1)} %get-tuple-element.32), channel_id=1, source_target_pairs={{0,1},{1,0},{2,3},{3,2},{4,5},{5,4},{6,7},{7,6},{8,9},{9,8},{10,11... | collective-permute-start | bytes 589832 | tf_op jit(solution)/shard_map/ppermute | solution.py:24
  97.1 6.1 %collective-permute-start.17 = (bf16[128,768]{1,0:T(8,128)(2,1)S(1)}, bf16[128,768]{1,0:T(8,128)(2,1)S(1)}, u32[]{:S(2)}, u32[]{:S(2)}) collective-permute-start(bf16[128,768]{1,0:T(8,128)(2,1)S(1)} %multiply_convert_fusion.normed), channel_id=1, source_target_pairs={{0,1},{1,0},{2,3},{3,2},{4,5},{5,4},{6,7},{7,6},{8,9},{9,8},{10,11... | collective-permute-start | bytes 589832 | tf_op jit(solution)/shard_map/ppermute | solution.py:24
  101.4 9.5 %collective-permute-start.16 = (bf16[64,768]{1,0:T(8,128)(2,1)S(1)}, bf16[64,768]{1,0:T(8,128)(2,1)S(1)}, u32[]{:S(2)}, u32[]{:S(2)}) collective-permute-start(bf16[64,768]{1,0:T(8,128)(2,1)S(1)} %fusion.1), channel_id=1, source_target_pairs={{0,2},{1,3},{2,0},{3,1},{4,6},{5,7},{6,4},{7,5},{8,10},{9,11},{10,... | collective-permute-start | bytes 294920 | tf_op jit(solution)/shard_map/ppermute | solution.py:24
  104.2 6.7 %collective-permute-start.18 = (bf16[64,768]{1,0:T(8,128)(2,1)S(1)}, bf16[64,768]{1,0:T(8,128)(2,1)S(1)}, u32[]{:S(2)}, u32[]{:S(2)}) collective-permute-start(bf16[64,768]{1,0:T(8,128)(2,1)S(1)} %get-tuple-element.39), channel_id=1, source_target_pairs={{0,3},{1,2},{2,1},{3,0},{4,7},{5,6},{6,5},{7,4},{8,11},{9,10},{10,... | collective-permute-start | bytes 294920 | tf_op jit(solution)/shard_map/ppermute | solution.py:24
  106.8 5.1 %collective-permute-start.19 = (bf16[64,768]{1,0:T(8,128)(2,1)S(1)}, bf16[64,768]{1,0:T(8,128)(2,1)S(1)}, u32[]{:S(2)}, u32[]{:S(2)}) collective-permute-start(bf16[64,768]{1,0:T(8,128)(2,1)S(1)} %get-tuple-element.40), channel_id=1, source_target_pairs={{0,1},{1,0},{2,3},{3,2},{4,5},{5,4},{6,7},{7,6},{8,9},{9,8},{10,11... | collective-permute-start | bytes 294920 | tf_op jit(solution)/shard_map/ppermute | solution.py:24

commit v6 on v5

--- a/solution.py
+++ b/solution.py
@@ -78,12 +78,14 @@
 def route(owner_row, selected, dest_slot, candidates):
     learners = lax.axis_size("dp")
     own = jnp.full((1,), lax.axis_index("dp"), jnp.int32)
+    shape = (learners,) + candidates.shape[1:]
+    small = learners <= 2 * SPREAD
     return pl.pallas_call(
         route_kernel,
         in_specs=[SCALARS] * 4 + [ANY],
         out_specs=(FAST, SCALARS),
         out_shape=(
-            jax.ShapeDtypeStruct((learners,) + candidates.shape[1:], BF16),
+            pltpu.VMEM(shape, BF16) if small else jax.ShapeDtypeStruct(shape, BF16),
             jax.ShapeDtypeStruct((SEL_DEV,), jnp.int32),
         ),
         scratch_shapes=[pltpu.SemaphoreType.DMA((1,))],
@@ -205,19 +207,18 @@
         target[n * rows : (n + 1) * rows] = part[...]
 
 
-def place_attn_kernel(where, embed, mine, others, embed_whole, attn_far):
+def place_attn_kernel(where, embed, *refs):
+    *pieces, embed_whole, attn_far = refs
     piece, group = where[0], where[1]
     rows = embed.shape[0]
-    size = 6 * rows
     embed_whole[block(group, rows)] = embed[...]
-    for source, core in ((mine, 0), (others, 1)):
-        for n in range(SPREAD // 2):
-            p = piece ^ (2 * n + core)
-            for k in range(3):
-                at = n * size + k * rows
-                embed_whole[block(group ^ (k + 1), rows), lanes(p)] = source[at : at + rows]
-                at += 3 * rows
-                attn_far[attn_unit(attn_far, 3 * p + k)] = source[at : at + rows]
+    for n, source in enumerate(pieces):
+        p = piece ^ (2 * (n % (SPREAD // 2)) + n // (SPREAD // 2))
+        for k in range(3):
+            at = k * rows
+            embed_whole[block(group ^ (k + 1), rows), lanes(p)] = source[at : at + rows]
+            at += 3 * rows
+            attn_far[attn_unit(attn_far, 3 * p + k)] = source[at : at + rows]
 
 
 def place_mlp_kernel(where, mine, others, up_far, down_far):
@@ -231,13 +232,15 @@
             down_far[block(p, size)] = source[at + size : at + 2 * size]
 
 
-def neighbours_of(where, piece):
+def neighbours_of(piece):
     parts = [piece]
     for bits in range(2, SPREAD, 2):
         parts.append(swap(piece, "dp", bits))
-    rows = len(parts) * piece.shape[0]
-    mine = copier(stack_kernel, ((rows,) + piece.shape[1:],), where, *parts)[0]
-    return mine, swap(mine, "dp", 1)
+    return parts
+
+
+def other_core(value):
+    return swap(value, "dp", 1)
 
 
 def turned_dot(left, right):
@@ -248,25 +251,29 @@
     return lax.dot_general(left, right, (((0,), (0,)), ((), ())), preferred_element_type=F32)
 
 
-def context_of(normed, shard):
-    width = shard.shape[0] // 4
-    projected = turned_dot(shard[: 3 * width], normed).astype(BF16)
+def attended_of(projected, shards, start, stop):
     results = []
-    for at in range(0, width, HEAD_DIM):
-        queries, attn_keys, attn_values = (
-            projected[c * width + at : c * width + at + HEAD_DIM] for c in range(3)
-        )
-        scores = columns_dot(attn_keys, queries) * HEAD_DIM ** (-0.5)
-        raised = jnp.exp(scores - jnp.max(scores, axis=0, keepdims=True))
-        probs = (raised / jnp.sum(raised, axis=0, keepdims=True)).astype(BF16)
-        results.append(dot(attn_values, probs).astype(BF16))
-    return results
-
-
-def attend_kernel(where, kept, opposite, neighbour, third, embed, own, far, gain, mine, other):
+    for values, shard in zip(projected, shards):
+        width = shard.shape[0] // 4
+        for at in range(0, width, HEAD_DIM):
+            queries, attn_keys, attn_values = (
+                values[c * width + at : c * width + at + HEAD_DIM] for c in range(3)
+            )
+            scores = columns_dot(attn_keys, queries[:, start:stop]) * HEAD_DIM ** (-0.5)
+            raised = jnp.exp(scores - jnp.max(scores, axis=0, keepdims=True))
+            probs = (raised / jnp.sum(raised, axis=0, keepdims=True)).astype(BF16)
+            results.append(dot(attn_values, probs).astype(BF16))
+    out = jnp.concatenate([shard[3 * (shard.shape[0] // 4) :] for shard in shards], axis=0)
+    return columns_dot(jnp.concatenate(results, axis=0), out)
+
+
+def attend_kernel(
+    where, kept, opposite, neighbour, third, embed, own, far, gain, own_qkv, far_qkv, embedded, other
+):
     group = where[1]
     quarter, pixel_width = kept.shape
     count = embed.shape[1] - pixel_width
+    half = 2 * quarter
     pixels = jnp.concatenate([kept[...], opposite[...], neighbour[...], third[...]], axis=0)
     row = lax.broadcasted_iota(jnp.int32, (count, count), 0)
     column = lax.broadcasted_iota(jnp.int32, (count, count), 1)
@@ -275,65 +282,107 @@
     spot = (turned ^ group) * quarter + row % quarter
     picks = jnp.where(spot == column, 1.0, 0.0).astype(BF16)
     product = turned_dot(pixels, embed[:, :pixel_width]) + turned_dot(picks, embed[:, pixel_width:])
-    activations = product.astype(BF16).astype(F32)
-    normed = norm_rows(activations, gain[...]).astype(BF16)
+    rounded = product.astype(BF16)
+    embedded[...] = rounded[:half]
+    normed = norm_rows(rounded.astype(F32), gain[...]).astype(BF16)
     width = own.shape[0] // 4
-    context = jnp.concatenate(context_of(normed, own) + context_of(normed, far), axis=0)
-    out = jnp.concatenate([own[3 * width :], far[3 * width :]], axis=0)
-    attended = columns_dot(context, out)
-    half = 2 * quarter
-    mine[...] = activations[:half] + attended[:half]
-    other[...] = attended[half:].astype(BF16)
-
-
-def attend(where, parts, embed, own, far, gain):
-    half = 2 * parts[0].shape[0]
-    model = own.shape[1]
-    held = [pltpu.with_memory_space_constraint(x, pltpu.VMEM) for x in (*parts, embed, own, far)]
-    return pl.pallas_call(
-        attend_kernel,
-        in_specs=[SCALARS] + [FAST] * 8,
-        out_specs=(FAST, FAST),
-        out_shape=(pltpu.VMEM((half, model), F32), pltpu.VMEM((half, model), BF16)),
-        compiler_params=pltpu.CompilerParams(vmem_limit_bytes=20 * 1024 * 1024),
-    )(where, *held, gain.reshape(1, -1))
-
-
-def gelu(values):
-    return 0.5 * values * (1.0 + lax.erf(values * 0.5 ** 0.5))
-
-
-def feed_through(normed, up, down):
-    return dot(gelu(dot(normed, up)).astype(BF16), down)
-
-
-def first_kernel(normed, up_far, down_far, up, down, feed, up_own, down_own, sem):
+    projected = [turned_dot(shard[: 3 * width], normed).astype(BF16) for shard in (own, far)]
+    own_qkv[...] = projected[0]
+    far_qkv[...] = projected[1]
+    other[...] = attended_of(projected, (own, far), half, count).astype(BF16)
+
+
+def attend_mine_kernel(own_qkv, far_qkv, embedded, own, far, up, down, mine, up_own, down_own, sem):
     copies = [
         pltpu.make_async_copy(up, up_own, sem.at[0]),
         pltpu.make_async_copy(down, down_own, sem.at[1]),
     ]
     for copy in copies:
         copy.start()
-    part = feed_through(normed[...], up_far[...], down_far[...])
+    projected = (own_qkv[...], far_qkv[...])
+    half = embedded.shape[0]
+    mine[...] = embedded[...].astype(F32) + attended_of(projected, (own, far), 0, half)
     for copy in copies:
         copy.wait()
-    feed[...] = part + feed_through(normed[...], up_own[...], down_own[...])
-
-
-def feed_first(normed, up_far, down_far, up, down):
-    held = [pltpu.with_memory_space_constraint(x, pltpu.VMEM) for x in (normed, up_far, down_far)]
-    return pl.pallas_call(
-        first_kernel,
-        in_specs=[FAST, FAST, FAST, SLOW, SLOW],
-        out_specs=(FAST, FAST, FAST),
+
+
+def held(operands):
+    return [pltpu.with_memory_space_constraint(x, pltpu.VMEM) for x in operands]
+
+
+def attend(where, parts, embed, own, far, gain):
+    half = 2 * parts[0].shape[0]
+    rows, model = own.shape
+    qkv = (rows // 4 * 3, 2 * half)
+    return pl.pallas_call(
+        attend_kernel,
+        in_specs=[SCALARS] + [FAST] * 8,
+        out_specs=(FAST,) * 4,
+        out_shape=tuple(
+            pltpu.VMEM(shape, BF16) for shape in (qkv, qkv, (half, model), (half, model))
+        ),
+        compiler_params=pltpu.CompilerParams(vmem_limit_bytes=20 * 1024 * 1024),
+    )(where, *held((*parts, embed, own, far)), gain.reshape(1, -1))
+
+
+def attend_mine(embedded, own_qkv, far_qkv, own, far, up, down):
+    return pl.pallas_call(
+        attend_mine_kernel,
+        in_specs=[FAST] * 5 + [SLOW] * 2,
+        out_specs=(FAST,) * 3,
         out_shape=(
-            pltpu.VMEM((normed.shape[0], down.shape[1]), F32),
+            pltpu.VMEM(embedded.shape, F32),
             pltpu.VMEM(up.shape, BF16),
             pltpu.VMEM(down.shape, BF16),
         ),
         scratch_shapes=[pltpu.SemaphoreType.DMA((2,))],
+        compiler_params=pltpu.CompilerParams(vmem_limit_bytes=12 * 1024 * 1024),
+    )(
+        *held((own_qkv, far_qkv, embedded, own, far)),
+        *(pltpu.with_memory_space_constraint(x, pltpu.HBM) for x in (up, down)),
+    )
+
+
+def join_kernel(mine, other, gain, after_attn, normed2):
+    after = mine[...] + other[...].astype(F32)
+    after_attn[...] = after
+    normed2[...] = norm_rows(after, gain[...]).astype(BF16)
+
+
+def join(mine, other, gain):
+    return pl.pallas_call(
+        join_kernel,
+        in_specs=[FAST] * 3,
+        out_specs=(FAST, FAST),
+        out_shape=(pltpu.VMEM(mine.shape, F32), pltpu.VMEM(mine.shape, BF16)),
+        compiler_params=SMALL,
+    )(*held((mine, other)), gain)
+
+
+def gelu(values):
+    return 0.5 * values * (1.0 + lax.erf(values * 0.5 ** 0.5))
+
+
+def feed_through(normed, up, down):
+    return dot(gelu(dot(normed, up)).astype(BF16), down)
+
+
+def own_kernel(normed, up, down, feed):
+    feed[...] = feed_through(normed[...], up[...], down[...])
+
+
+def first_kernel(normed, up, down, part, feed):
+    feed[...] = part[...] + feed_through(normed[...], up[...], down[...])
+
+
+def feed_first(body, *operands):
+    return pl.pallas_call(
+        body,
+        in_specs=[FAST] * len(operands),
+        out_specs=FAST,
+        out_shape=pltpu.VMEM(operands[0].shape, F32),
         compiler_params=pltpu.CompilerParams(vmem_limit_bytes=16 * 1024 * 1024),
-    )(*held, *(pltpu.with_memory_space_constraint(x, pltpu.HBM) for x in (up, down)))
+    )(*held(operands))
 
 
 def second_kernel(normed, up_far, down_far, up_own, down_own, near, third):
@@ -346,14 +395,13 @@
 
 def feed_second(*operands):
     half, model = operands[0].shape
-    held = [pltpu.with_memory_space_constraint(x, pltpu.VMEM) for x in operands]
     return pl.pallas_call(
         second_kernel,
         in_specs=[FAST] * 5,
         out_specs=(FAST, FAST),
         out_shape=(pltpu.VMEM((half // 2, model), BF16), pltpu.VMEM((half // 2, model), BF16)),
         compiler_params=pltpu.CompilerParams(vmem_limit_bytes=16 * 1024 * 1024),
-    )(*held)
+    )(*held(operands))
 
 
 def layer(
@@ -388,34 +436,41 @@
     opposite = swap(both_piece, "mp", 2)
     neighbour = swap(embed_piece, "mp", 1)
     units = copier(units_kernel, ((6 * width, UNIT),), where, neighbour, opposite, third)[0]
+    near = neighbours_of(units)
+    far = [other_core(part) for part in near]
     embed_whole, attn_far = copier(
         place_attn_kernel,
         ((groups * width, pixel_width + positions.shape[0]), attn_own.shape),
         where,
         embed_own,
-        *neighbours_of(where, units),
+        *near,
+        *far,
     )
     mlp_piece = swap(mlp_piece, "mp", 2)
+    near2 = neighbours_of(mlp_piece)
+    rows2 = len(near2) * mlp_piece.shape[0]
+    mine2 = copier(stack_kernel, ((rows2, model),), where, *near2)[0]
+    far2 = other_core(mine2)
     up_far, down_far = copier(
-        place_mlp_kernel,
-        (up_weight.shape, down_weight.shape),
-        where,
-        *neighbours_of(where, mlp_piece),
+        place_mlp_kernel, (up_weight.shape, down_weight.shape), where, mine2, far2
     )
 
     kept, given = choose(where, senders, incoming)
     third = swap(given, "mp", 3)
     opposite = swap(given, "mp", 2)
     neighbour = swap(kept, "mp", 1)
-    mine, other = attend(
+    own_qkv, far_qkv, embedded, other = attend(
         where, (kept, opposite, neighbour, third), embed_whole, attn_own, attn_far, attn_gain
     )
     other = swap(other, "mp", 1)
-    after_attn = mine + other.astype(F32)
+    mine, up_own, down_own = attend_mine(
+        embedded, own_qkv, far_qkv, attn_own, attn_far, up_weight, down_weight
+    )
     gain2 = widen(mlp_gain)
-    normed2 = norm_rows(after_attn, gain2).astype(BF16)
+    after_attn, normed2 = join(mine, other, gain2)
     neighbour2 = swap(normed2, "mp", 1)
-    feed, up_own, down_own = feed_first(normed2, up_far, down_far, up_weight, down_weight)
+    feed = feed_first(own_kernel, normed2, up_own, down_own)
+    feed = feed_first(first_kernel, normed2, up_far, down_far, feed)
     from_opposite = swap((after_attn + feed)[quarter:].astype(BF16), "mp", 2)
     for_near, for_third = feed_second(neighbour2, up_far, down_far, up_own, down_own)
     from_third = swap(for_third, "mp", 3)

time: 113 us -> 112 us (level)
  blocking collectives: 15.8 us -> 0 us
  waiting for transfers between devices: 45.1 us -> 51.1 us
  local copies, waits for them, and re-layouts: 0.04 us -> 3.49 us
  starting transfers between devices: 31.1 us -> 34.5 us
  Pallas kernels: 16.6 us -> 18.8 us
    all_to_all x1 -> x0, blocking collectives: 15.8 us -> none  [layer(): lax.all_to_all(outgoing, 'dp', split_axis=0, concat_axis=0, tiled=True)]
    ppermute x20 -> x23, waiting for transfers between devices: 45.1 us -> 51.1 us  [swap(): lax.ppermute(value, axis, [(i, i ^ bits) for i in range(lax.axis_size(axi...]
    all_to_all x0 -> x1, starting transfers between devices: none -> 4.23 us  [layer(): lax.all_to_all(outgoing, 'dp', split_axis=0, concat_axis=0, tiled=True)]
    unnamed x12 -> x24, local copies, waits for them, and re-layouts: 0.04 us -> 3.48 us
    pallas_call x5 -> x4, Pallas kernels: 3.72 us -> 4.73 us  [copier(): pl.pallas_call(body, in_specs=[SCALARS] + [FAST] * len(operands), out_spe...]
    pallas_call x1 -> x4, Pallas kernels: 2.5 us -> 3.43 us  [the longest x1 1.97 us: attend_mine(): pl.pallas_call(attend_mine_kernel, in_specs=[FAST] * 5 + [SLOW] * 2, out_...]
    ppermute x20 -> x23, starting transfers between devices: 31.1 us -> 30.3 us  [swap(): lax.ppermute(value, axis, [(i, i ^ bits) for i in range(lax.axis_size(axi...]
  transfers between devices with their start and end apart: 20 -> 24, of which waited for: 15 -> 13; matrix products, arithmetic and copies ran while one was open for 0% -> 0% of each run, Pallas kernels for 13% -> 14%
where the time goes in v6:
time: 112 us; the launch traced here: 111 us
  waiting for transfers between devices  51.1 us (46%)
  starting transfers between devices  34.5 us (31%)
  Pallas kernels  18.8 us (17%)
  local copies, waits for them, and re-layouts  3.49 us (3%)
  other arithmetic  3.29 us (3%)
    ppermute x23, waiting for transfers between devices, swap(): lax.ppermute(value, axis, [(i, i ^ bits) for i in range(lax.axis_size(axi...  51.1 us
    ppermute x23, starting transfers between devices, swap(): lax.ppermute(value, axis, [(i, i ^ bits) for i in range(lax.axis_size(axi...  30.3 us
    pallas_call x4, Pallas kernels, copier(): pl.pallas_call(body, in_specs=[SCALARS] + [FAST] * len(operands), out_spe...  4.73 us
    all_to_all x1, starting transfers between devices, layer(): lax.all_to_all(outgoing, 'dp', split_axis=0, concat_axis=0, tiled=True)  4.23 us
    pallas_call x1, Pallas kernels, attend(): pl.pallas_call(attend_kernel, in_specs=[SCALARS] + [FAST] * 8, out_specs=...  3.96 us
    unnamed x24, local copies, waits for them, and re-layouts  3.48 us
  transfers between devices with their start and end apart: 24, of which 13 were waited for; matrix products, arithmetic and copies ran while one was open for 0% of the time, Pallas kernels for 14%

profile of v6, /device:TPU:0, one launch (start us, length us, event | category | flops | bytes accessed | tf_op | source)
XLA Modules:
  0.0 111.4 jit_solution(12940912480069360551)
XLA Ops:
  0.0 0.1 pad_add_fusion.where
  0.1 1.1 pad_maximum_fusion.1.embed
  1.1 1.3 %pad_maximum_fusion.attn.own = bf16[768,768]{1,0:T(8,128)(2,1)S(1)} fusion(bf16[192,768]{1,0:T(8,128)(2,1)} %param.19, bf16[576,768]{1,0:T(8,128)(2,1)} %bitcast.12), kind=kLoop, calls=%fused_computation | loop fusion | flops 2359296 | bytes 2359296 | tf_op jit(solution)/shard_map/concatenate | solution.py:433
  2.5 0.0 copy-start
  2.5 0.0 copy-start.5
  2.5 0.0 copy-start.6
  2.5 0.0 copy-start.7
  2.5 2.2 %shard_map.120 = (bf16[192,128]{1,0:T(8,128)(2,1)S(1)}, bf16[768,128]{1,0:T(8,128)(2,1)}, bf16[192,768]{1,0:T(8,128)(2,1)S(1)}) custom-call(s32[2]{0:T(128)S(1)} %pad_add_fusion.where, bf16[192,1024]{1,0:T(8,128)(2,1)S(1)} %pad_maximum_fusion.1.embed, bf16[768,768]{1,0:T(8,128)(2,1)S(1)} %pad_maximum_fusion.attn.own, bf16[768,768]{1,0:T(8,128)(2,1)} %up.3, ...), custom_call_target="tpu_custom_call" | custom-call | tf_op jit(solution)/shard_map/pallas_call | solution.py:175
  4.8 4.1 %collective-permute-start.14 = (bf16[192,768]{1,0:T(8,128)(2,1)S(1)}, bf16[192,768]{1,0:T(8,128)(2,1)S(1)}, u32[]{:S(2)}, u32[]{:S(2)}) collective-permute-start(bf16[192,768]{1,0:T(8,128)(2,1)S(1)} %get-tuple-element.42), channel_id=1, source_target_pairs={{0,2},{1,3},{2,0},{3,1},{4,6},{5,7},{6,4},{7,5},{8,10},{9,11},{10,... | collective-permute-start | bytes 884744 | tf_op jit(solution)/shard_map/ppermute | solution.py:24
  8.9 13.3 %collective-permute-done.14.refs_0_ = bf16[192,768]{1,0:T(8,128)(2,1)S(1)} collective-permute-done((bf16[192,768]{1,0:T(8,128)(2,1)S(1)}, bf16[192,768]{1,0:T(8,128)(2,1)S(1)}, u32[]{:S(2)}, u32[]{:S(2)}) %collective-permute-start.14) | collective-permute-done | bytes 294944 | tf_op jit(solution)/shard_map/ppermute | solution.py:24
  22.2 1.5 %collective-permute-start.15 = (bf16[192,768]{1,0:T(8,128)(2,1)S(1)}, bf16[192,768]{1,0:T(8,128)(2,1)S(1)}, u32[]{:S(2)}, u32[]{:S(2)}) collective-permute-start(bf16[192,768]{1,0:T(8,128)(2,1)S(1)} %collective-permute-done.14.refs_0_), channel_id=1, source_target_pairs={{0,8},{4,12},{8,0},{12,4},{16,24},{20,28},{24,16},{28,20},{1,9},{5... | collective-permute-start | bytes 884744 | tf_op jit(solution)/shard_map/ppermute | solution.py:24
  23.8 1.5 %collective-permute-start.16 = (bf16[192,768]{1,0:T(8,128)(2,1)S(1)}, bf16[192,768]{1,0:T(8,128)(2,1)S(1)}, u32[]{:S(2)}, u32[]{:S(2)}) collective-permute-start(bf16[192,768]{1,0:T(8,128)(2,1)S(1)} %collective-permute-done.14.refs_0_), channel_id=1, source_target_pairs={{0,16},{4,20},{8,24},{12,28},{16,0},{20,4},{24,8},{28,12},{1,17},{... | collective-permute-start | bytes 884744 | tf_op jit(solution)/shard_map/ppermute | solution.py:24
  25.3 0.4 collective-permute-start.17
  25.7 0.0 collective-permute-start.4
  25.8 1.9 %shard_map.118 = (bf16[8,64,768]{2,1,0:T(8,128)(2,1)}, s32[2]{0:T(128)S(1)}) custom-call(s32[1]{0:T(128)} %bitcast.2.own, s32[64]{0:T(128)S(1)} %copy-done.5, s32[16]{0:T(128)S(1)} %copy-done.6, s32[16]{0:T(128)S(1)} %copy-done.7, bf16[8,64,768]{2,1,0:T(8,128)(2,1)S(1)} %copy-done), custom_call_target="tpu_custom_call" | custom-call | tf_op jit(solution)/shard_map/pallas_call | solution.py:83
  27.6 4.2 %all-to-all-start = ((bf16[8,64,768]{2,1,0:T(8,128)(2,1)}), bf16[8,64,768]{2,1,0:T(8,128)(2,1)}, u32[]{:S(2)}, u32[]{:S(2)}) async-start(bf16[8,64,768]{2,1,0:T(8,128)(2,1)} %get-tuple-element.28), calls=%async_computation | async-start | bytes 1572864 | tf_op jit(solution)/shard_map/all_to_all | solution.py:428
  31.9 0.2 collective-permute-done.15.refs_1_
  32.1 6.5 %collective-permute-done.16.refs_2_ = bf16[192,768]{1,0:T(8,128)(2,1)S(1)} collective-permute-done((bf16[192,768]{1,0:T(8,128)(2,1)S(1)}, bf16[192,768]{1,0:T(8,128)(2,1)S(1)}, u32[]{:S(2)}, u32[]{:S(2)}) %collective-permute-start.16) | collective-permute-done | bytes 294944 | tf_op jit(solution)/shard_map/ppermute | solution.py:24
  38.7 0.7 copy-done.1
  39.4 0.7 copy-done.3
  40.1 1.0 copy-done.2
  41.1 1.0 copy-done.4
  42.0 0.6 shard_map.127.mine
  42.6 0.0 copy-start.10
  42.7 0.1 collective-permute-start.18
  42.7 0.1 copy-done.9
  42.8 1.0 collective-permute-start.3
  43.8 3.6 %collective-permute-start.5 = (bf16[192,128]{1,0:T(8,128)(2,1)S(1)}, bf16[192,128]{1,0:T(8,128)(2,1)S(1)}, u32[]{:S(2)}, u32[]{:S(2)}) collective-permute-start(bf16[192,128]{1,0:T(8,128)(2,1)S(1)} %copy-done.9), channel_id=1, source_target_pairs={{0,3},{1,2},{2,1},{3,0},{4,7},{5,6},{6,5},{7,4},{8,11},{9,10},{10,... | collective-permute-start | bytes 147464 | tf_op jit(solution)/shard_map/ppermute | solution.py:24
  47.4 0.0 collective-permute-done.3.neighbour
  47.4 3.4 %collective-permute-done.5.third = bf16[192,128]{1,0:T(8,128)(2,1)S(1)} collective-permute-done((bf16[192,128]{1,0:T(8,128)(2,1)S(1)}, bf16[192,128]{1,0:T(8,128)(2,1)S(1)}, u32[]{:S(2)}, u32[]{:S(2)}) %collective-permute-start.5) | collective-permute-done | bytes 49184 | tf_op jit(solution)/shard_map/ppermute | solution.py:24
  50.8 0.6 shard_map.121.refs_0_
  51.4 0.7 collective-permute-start.6
  52.1 2.6 %collective-permute-start.7 = (bf16[1152,128]{1,0:T(8,128)(2,1)S(1)}, bf16[1152,128]{1,0:T(8,128)(2,1)}, u32[]{:S(2)}, u32[]{:S(2)}) collective-permute-start(bf16[1152,128]{1,0:T(8,128)(2,1)S(1)} %shard_map.121.refs_0_), channel_id=1, source_target_pairs={{0,16},{4,20},{8,24},{12,28},{16,0},{20,4},{24,8},{28,12},{1,17},{... | collective-permute-start | bytes 884744 | tf_op jit(solution)/shard_map/ppermute | solution.py:24
  54.7 1.4 %collective-permute-start.8 = (bf16[1152,128]{1,0:T(8,128)(2,1)S(1)}, bf16[1152,128]{1,0:T(8,128)(2,1)}, u32[]{:S(2)}, u32[]{:S(2)}) collective-permute-start(bf16[1152,128]{1,0:T(8,128)(2,1)S(1)} %shard_map.121.refs_0_), channel_id=1, source_target_pairs={{0,24},{4,28},{8,16},{12,20},{16,8},{20,12},{24,0},{28,4},{1,25},{... | collective-permute-start | bytes 884744 | tf_op jit(solution)/shard_map/ppermute | solution.py:24
  56.1 5.2 %collective-permute-done.6.refs_1_ = bf16[1152,128]{1,0:T(8,128)(2,1)S(1)} collective-permute-done((bf16[1152,128]{1,0:T(8,128)(2,1)S(1)}, bf16[1152,128]{1,0:T(8,128)(2,1)S(1)}, u32[]{:S(2)}, u32[]{:S(2)}) %collective-permute-start.6) | collective-permute-done | bytes 294944 | tf_op jit(solution)/shard_map/ppermute | solution.py:24
  61.4 0.0 collective-permute-start.10
  61.4 5.9 %collective-permute-done.7.refs_2_ = bf16[1152,128]{1,0:T(8,128)(2,1)} collective-permute-done((bf16[1152,128]{1,0:T(8,128)(2,1)S(1)}, bf16[1152,128]{1,0:T(8,128)(2,1)}, u32[]{:S(2)}, u32[]{:S(2)}) %collective-permute-start.7) | collective-permute-done | bytes 294944 | tf_op jit(solution)/shard_map/ppermute | solution.py:24
  67.2 1.9 %collective-permute-done.8.refs_3_ = bf16[1152,128]{1,0:T(8,128)(2,1)} collective-permute-done((bf16[1152,128]{1,0:T(8,128)(2,1)S(1)}, bf16[1152,128]{1,0:T(8,128)(2,1)}, u32[]{:S(2)}, u32[]{:S(2)}) %collective-permute-start.8) | collective-permute-done | bytes 294944 | tf_op jit(solution)/shard_map/ppermute | solution.py:24
  69.2 0.0 collective-permute-start.12
  69.2 1.5 %shard_map.119 = (bf16[64,768]{1,0:T(8,128)(2,1)S(1)}, bf16[64,768]{1,0:T(8,128)(2,1)S(1)}) custom-call(s32[2]{0:T(128)S(1)} %pad_add_fusion.where, s32[2]{0:T(128)S(1)} %get-tuple-element.27.senders, bf16[8,64,768]{2,1,0:T(8,128)(2,1)} %all-to-all-done.incoming), custom_call_target="tpu_custom_call" | custom-call | tf_op jit(solution)/shard_map/pallas_call | solution.py:110
  70.7 0.5 collective-permute-start
  71.2 2.1 %collective-permute-start.1 = (bf16[64,768]{1,0:T(8,128)(2,1)S(1)}, bf16[64,768]{1,0:T(8,128)(2,1)S(1)}, u32[]{:S(2)}, u32[]{:S(2)}) collective-permute-start(bf16[64,768]{1,0:T(8,128)(2,1)S(1)} %get-tuple-element.29.kept), channel_id=1, source_target_pairs={{0,1},{1,0},{2,3},{3,2},{4,5},{5,4},{6,7},{7,6},{8,9},{9,8},{10,11... | collective-permute-start | bytes 294920 | tf_op jit(solution)/shard_map/ppermute | solution.py:24
  73.3 1.8 %collective-permute-start.2 = (bf16[64,768]{1,0:T(8,128)(2,1)S(1)}, bf16[64,768]{1,0:T(8,128)(2,1)S(1)}, u32[]{:S(2)}, u32[]{:S(2)}) collective-permute-start(bf16[64,768]{1,0:T(8,128)(2,1)S(1)} %get-tuple-element.30), channel_id=1, source_target_pairs={{0,3},{1,2},{2,1},{3,0},{4,7},{5,6},{6,5},{7,4},{8,11},{9,10},{10,... | collective-permute-start | bytes 294920 | tf_op jit(solution)/shard_map/ppermute | solution.py:24
  75.2 2.1 %shard_map.122 = (bf16[768,1024]{1,0:T(8,128)(2,1)S(1)}, bf16[768,768]{1,0:T(8,128)(2,1)S(1)}) custom-call(s32[2]{0:T(128)S(1)} %pad_add_fusion.where, bf16[192,1024]{1,0:T(8,128)(2,1)S(1)} %pad_maximum_fusion.1.embed, bf16[1152,128]{1,0:T(8,128)(2,1)S(1)} %shard_map.121.refs_0_, bf16[1152,128]{1,0:T(8,128)(2,1)S(1)} %collective-permute-done.6.refs_1_, ...), custom_call_target="tpu_custom_call" | custom-call | tf_op jit(solution)/shard_map/pallas_call | solution.py:40
  77.3 1.6 %collective-permute-done.opposite = bf16[64,768]{1,0:T(8,128)(2,1)S(1)} collective-permute-done((bf16[64,768]{1,0:T(8,128)(2,1)S(1)}, bf16[64,768]{1,0:T(8,128)(2,1)S(1)}, u32[]{:S(2)}, u32[]{:S(2)}) %collective-permute-start) | collective-permute-done | bytes 98336 | tf_op jit(solution)/shard_map/ppermute | solution.py:24
  78.9 1.8 %collective-permute-done.1.neighbour = bf16[64,768]{1,0:T(8,128)(2,1)S(1)} collective-permute-done((bf16[64,768]{1,0:T(8,128)(2,1)S(1)}, bf16[64,768]{1,0:T(8,128)(2,1)S(1)}, u32[]{:S(2)}, u32[]{:S(2)}) %collective-permute-start.1) | collective-permute-done | bytes 98336 | tf_op jit(solution)/shard_map/ppermute | solution.py:24
  80.7 4.0 %shard_map.123 = (bf16[576,256]{1,0:T(8,128)(2,1)S(1)}, bf16[576,256]{1,0:T(8,128)(2,1)S(1)}, bf16[128,768]{1,0:T(8,128)(2,1)S(1)}, bf16[128,768]{1,0:T(8,128)(2,1)S(1)}) custom-call(s32[2]{0:T(128)S(1)} %pad_add_fusion.where, bf16[64,768]{1,0:T(8,128)(2,1)S(1)} %get-tuple-element.29.kept, bf16[64,768]{1,0:T(8,128)(2,1)S(1)} %collective-permute-done.opposite, ...), custom_call_target="tpu_custom_call" | custom-call | tf_op jit(solution)/shard_map/pallas_call | solution.py:317
  84.7 2.5 %collective-permute-start.13 = (bf16[128,768]{1,0:T(8,128)(2,1)S(1)}, bf16[128,768]{1,0:T(8,128)(2,1)S(1)}, u32[]{:S(2)}, u32[]{:S(2)}) collective-permute-start(bf16[128,768]{1,0:T(8,128)(2,1)S(1)} %get-tuple-element.39), channel_id=1, source_target_pairs={{0,1},{1,0},{2,3},{3,2},{4,5},{5,4},{6,7},{7,6},{8,9},{9,8},{10,11... | collective-permute-start | bytes 589832 | tf_op jit(solution)/shard_map/ppermute | solution.py:24
  87.2 2.0 %shard_map.124 = (f32[128,768]{1,0:T(8,128)S(1)}, bf16[768,768]{1,0:T(8,128)(2,1)S(1)}, bf16[768,768]{1,0:T(8,128)(2,1)S(1)}) custom-call(bf16[576,256]{1,0:T(8,128)(2,1)S(1)} %get-tuple-element.35.own_qkv, bf16[576,256]{1,0:T(8,128)(2,1)S(1)} %get-tuple-element.36.far_qkv, bf16[128,768]{1,0:T(8,128)(2,1)S(1)} %get-tuple-element.37.embedded, ...), custom_call_target="tpu_custom_call" | custom-call | tf_op jit(solution)/shard_map/pallas_call | solution.py:329
  89.2 3.1 %collective-permute-done.13.other = bf16[128,768]{1,0:T(8,128)(2,1)S(1)} collective-permute-done((bf16[128,768]{1,0:T(8,128)(2,1)S(1)}, bf16[128,768]{1,0:T(8,128)(2,1)S(1)}, u32[]{:S(2)}, u32[]{:S(2)}) %collective-permute-start.13) | collective-permute-done | bytes 196640 | tf_op jit(solution)/shard_map/ppermute | solution.py:24
  92.3 0.2 shard_map.126
  92.5 1.8 %collective-permute-start.20 = (bf16[128,768]{1,0:T(8,128)(2,1)S(1)}, bf16[128,768]{1,0:T(8,128)(2,1)S(1)}, u32[]{:S(2)}, u32[]{:S(2)}) collective-permute-start(bf16[128,768]{1,0:T(8,128)(2,1)S(1)} %get-tuple-element.41.normed), channel_id=1, source_target_pairs={{0,1},{1,0},{2,3},{3,2},{4,5},{5,4},{6,7},{7,6},{8,9},{9,8},{10,11... | collective-permute-start | bytes 589832 | tf_op jit(solution)/shard_map/ppermute | solution.py:24
  94.3 0.6 shard_map.129.part
  95.0 1.4 %shard_map.128 = (bf16[768,768]{1,0:T(8,128)(2,1)S(1)}, bf16[768,768]{1,0:T(8,128)(2,1)S(1)}) custom-call(s32[2]{0:T(128)S(1)} %pad_add_fusion.where, bf16[768,768]{1,0:T(8,128)(2,1)S(1)} %shard_map.127.mine, bf16[768,768]{1,0:T(8,128)(2,1)} %collective-permute-done.18.others), custom_call_target="tpu_custom_call" | custom-call | tf_op jit(solution)/shard_map/pallas_call | solution.py:40
  96.4 2.5 %collective-permute-done.20.normed = bf16[128,768]{1,0:T(8,128)(2,1)S(1)} collective-permute-done((bf16[128,768]{1,0:T(8,128)(2,1)S(1)}, bf16[128,768]{1,0:T(8,128)(2,1)S(1)}, u32[]{:S(2)}, u32[]{:S(2)}) %collective-permute-start.20) | collective-permute-done | bytes 196640 | tf_op jit(solution)/shard_map/ppermute | solution.py:24
  98.9 1.0 shard_map.131
  99.9 2.0 %collective-permute-start.21 = (bf16[64,768]{1,0:T(8,128)(2,1)S(1)}, bf16[64,768]{1,0:T(8,128)(2,1)S(1)}, u32[]{:S(2)}, u32[]{:S(2)}) collective-permute-start(bf16[64,768]{1,0:T(8,128)(2,1)S(1)} %get-tuple-element.47), channel_id=1, source_target_pairs={{0,3},{1,2},{2,1},{3,0},{4,7},{5,6},{6,5},{7,4},{8,11},{9,10},{10,... | collective-permute-start | bytes 294920 | tf_op jit(solution)/shard_map/ppermute | solution.py:24
  102.0 0.6 shard_map.130
  102.6 1.0 collective-permute-start.19
  103.7 1.5 %collective-permute-start.22 = (bf16[64,768]{1,0:T(8,128)(2,1)S(1)}, bf16[64,768]{1,0:T(8,128)(2,1)S(1)}, u32[]{:S(2)}, u32[]{:S(2)}) collective-permute-start(bf16[64,768]{1,0:T(8,128)(2,1)S(1)} %get-tuple-element.48), channel_id=1, source_target_pairs={{0,1},{1,0},{2,3},{3,2},{4,5},{5,4},{6,7},{7,6},{8,9},{9,8},{10,11... | collective-permute-start | bytes 294920 | tf_op jit(solution)/shard_map/ppermute | solution.py:24
  105.1 2.0 %collective-permute-done.21 = bf16[64,768]{1,0:T(8,128)(2,1)S(1)} collective-permute-done((bf16[64,768]{1,0:T(8,128)(2,1)S(1)}, bf16[64,768]{1,0:T(8,128)(2,1)S(1)}, u32[]{:S(2)}, u32[]{:S(2)}) %collective-permute-start.21) | collective-permute-done | bytes 98336 | tf_op jit(solution)/shard_map/ppermute | solution.py:24
  107.1 3.5 %collective-permute-done.19 = bf16[64,768]{1,0:T(8,128)(2,1)S(1)} collective-permute-done((bf16[64,768]{1,0:T(8,128)(2,1)S(1)}, bf16[64,768]{1,0:T(8,128)(2,1)S(1)}, u32[]{:S(2)}, u32[]{:S(2)}) %collective-permute-start.19) | collective-permute-done | bytes 98336 | tf_op jit(solution)/shard_map/ppermute | solution.py:24
  110.6 0.1 select_bitcast_fusion.1
  110.7 0.7 pad_maximum_fusion.2
  (31 shorter events, 0.1 us)
Async XLA Ops:
  2.5 23.2 %copy-start = (bf16[8,64,768]{2,1,0:T(8,128)(2,1)S(1)}, bf16[8,64,768]{2,1,0:T(8,128)(2,1)}, u32[]{:S(2)}) copy-start(bf16[8,64,768]{2,1,0:T(8,128)(2,1)} %candidates.1) | copy-start | bytes 2359300
  2.5 23.2 %copy-start.5 = (s32[64]{0:T(128)S(1)}, s32[64]{0:T(128)}, u32[]{:S(2)}) copy-start(s32[64]{0:T(128)} %owner_row.1) | copy-start | bytes 772
  2.5 23.2 %copy-start.6 = (s32[16]{0:T(128)S(1)}, s32[16]{0:T(128)}, u32[]{:S(2)}) copy-start(s32[16]{0:T(128)} %selected.1) | copy-start | bytes 196
  2.5 23.2 %copy-start.7 = (s32[16]{0:T(128)S(1)}, s32[16]{0:T(128)}, u32[]{:S(2)}) copy-start(s32[16]{0:T(128)} %dest_slot.1) | copy-start | bytes 196
  4.8 22.9 %copy-start.8 = (bf16[192,128]{1,0:T(8,128)(2,1)}, bf16[192,128]{1,0:T(8,128)(2,1)S(1)}, u32[]{:S(2)}) copy-start(bf16[192,128]{1,0:T(8,128)(2,1)S(1)} %get-tuple-element.31) | copy-start | bytes 147460
  4.8 17.5 %collective-permute-start.14 = (bf16[192,768]{1,0:T(8,128)(2,1)S(1)}, bf16[192,768]{1,0:T(8,128)(2,1)S(1)}, u32[]{:S(2)}, u32[]{:S(2)}) collective-permute-start(bf16[192,768]{1,0:T(8,128)(2,1)S(1)} %get-tuple-element.42), channel_id=1, source_target_pairs={{0,2},{1,3},{2,0},{3,1},{4,6},{5,7},{6,4},{7,5},{8,10},{9,11},{10,... | collective-permute-start | bytes 884744 | tf_op jit(solution)/shard_map/ppermute | solution.py:24
  22.2 9.9 %collective-permute-start.15 = (bf16[192,768]{1,0:T(8,128)(2,1)S(1)}, bf16[192,768]{1,0:T(8,128)(2,1)S(1)}, u32[]{:S(2)}, u32[]{:S(2)}) collective-permute-start(bf16[192,768]{1,0:T(8,128)(2,1)S(1)} %collective-permute-done.14.refs_0_), channel_id=1, source_target_pairs={{0,8},{4,12},{8,0},{12,4},{16,24},{20,28},{24,16},{28,20},{1,9},{5... | collective-permute-start | bytes 884744 | tf_op jit(solution)/shard_map/ppermute | solution.py:24
  23.8 14.9 %collective-permute-start.16 = (bf16[192,768]{1,0:T(8,128)(2,1)S(1)}, bf16[192,768]{1,0:T(8,128)(2,1)S(1)}, u32[]{:S(2)}, u32[]{:S(2)}) collective-permute-start(bf16[192,768]{1,0:T(8,128)(2,1)S(1)} %collective-permute-done.14.refs_0_), channel_id=1, source_target_pairs={{0,16},{4,20},{8,24},{12,28},{16,0},{20,4},{24,8},{28,12},{1,17},{... | collective-permute-start | bytes 884744 | tf_op jit(solution)/shard_map/ppermute | solution.py:24
  25.3 14.1 %collective-permute-start.17 = (bf16[192,768]{1,0:T(8,128)(2,1)S(1)}, bf16[192,768]{1,0:T(8,128)(2,1)S(1)}, u32[]{:S(2)}, u32[]{:S(2)}) collective-permute-start(bf16[192,768]{1,0:T(8,128)(2,1)S(1)} %collective-permute-done.14.refs_0_), channel_id=1, source_target_pairs={{0,24},{4,28},{8,16},{12,20},{16,8},{20,12},{24,0},{28,4},{1,25},{... | collective-permute-start | bytes 884744 | tf_op jit(solution)/shard_map/ppermute | solution.py:24
  25.7 25.1 %collective-permute-start.4 = (bf16[768,128]{1,0:T(8,128)(2,1)}, bf16[768,128]{1,0:T(8,128)(2,1)S(1)}, u32[]{:S(2)}, u32[]{:S(2)}) collective-permute-start(bf16[768,128]{1,0:T(8,128)(2,1)} %get-tuple-element.32), channel_id=1, source_target_pairs={{0,2},{1,3},{2,0},{3,1},{4,6},{5,7},{6,4},{7,5},{8,10},{9,11},{10,... | collective-permute-start | bytes 589832 | tf_op jit(solution)/shard_map/ppermute | solution.py:24
  27.6 41.5 %all-to-all-start = ((bf16[8,64,768]{2,1,0:T(8,128)(2,1)}), bf16[8,64,768]{2,1,0:T(8,128)(2,1)}, u32[]{:S(2)}, u32[]{:S(2)}) async-start(bf16[8,64,768]{2,1,0:T(8,128)(2,1)} %get-tuple-element.28), calls=%async_computation | async-start | bytes 1572864 | tf_op jit(solution)/shard_map/all_to_all | solution.py:428
  38.6 0.7 copy-start.1
  39.4 0.7 copy-start.3
  40.1 1.0 copy-start.2
  41.1 1.0 copy-start.4
  42.0 0.8 copy-start.9
  42.6 32.5 %copy-start.10 = (bf16[768]{0:T(1024)(128)(2,1)S(1)}, bf16[768]{0:T(1024)(128)(2,1)}, u32[]{:S(2)}) copy-start(bf16[768]{0:T(1024)(128)(2,1)} %param.20) | copy-start | bytes 4612
  42.7 52.3 %collective-permute-start.18 = (bf16[768,768]{1,0:T(8,128)(2,1)S(1)}, bf16[768,768]{1,0:T(8,128)(2,1)}, u32[]{:S(2)}, u32[]{:S(2)}) collective-permute-start(bf16[768,768]{1,0:T(8,128)(2,1)S(1)} %shard_map.127.mine), channel_id=1, source_target_pairs={{0,4},{4,0},{8,12},{12,8},{16,20},{20,16},{24,28},{28,24},{1,5},{5... | collective-permute-start | bytes 3538952 | tf_op jit(solution)/shard_map/ppermute | solution.py:24
  42.8 4.6 %collective-permute-start.3 = (bf16[192,128]{1,0:T(8,128)(2,1)S(1)}, bf16[192,128]{1,0:T(8,128)(2,1)S(1)}, u32[]{:S(2)}, u32[]{:S(2)}) collective-permute-start(bf16[192,128]{1,0:T(8,128)(2,1)S(1)} %copy-done.9), channel_id=1, source_target_pairs={{0,1},{1,0},{2,3},{3,2},{4,5},{5,4},{6,7},{7,6},{8,9},{9,8},{10,11... | collective-permute-start | bytes 147464 | tf_op jit(solution)/shard_map/ppermute | solution.py:24
  43.8 7.0 %collective-permute-start.5 = (bf16[192,128]{1,0:T(8,128)(2,1)S(1)}, bf16[192,128]{1,0:T(8,128)(2,1)S(1)}, u32[]{:S(2)}, u32[]{:S(2)}) collective-permute-start(bf16[192,128]{1,0:T(8,128)(2,1)S(1)} %copy-done.9), channel_id=1, source_target_pairs={{0,3},{1,2},{2,1},{3,0},{4,7},{5,6},{6,5},{7,4},{8,11},{9,10},{10,... | collective-permute-start | bytes 147464 | tf_op jit(solution)/shard_map/ppermute | solution.py:24
  51.4 9.9 %collective-permute-start.6 = (bf16[1152,128]{1,0:T(8,128)(2,1)S(1)}, bf16[1152,128]{1,0:T(8,128)(2,1)S(1)}, u32[]{:S(2)}, u32[]{:S(2)}) collective-permute-start(bf16[1152,128]{1,0:T(8,128)(2,1)S(1)} %shard_map.121.refs_0_), channel_id=1, source_target_pairs={{0,8},{4,12},{8,0},{12,4},{16,24},{20,28},{24,16},{28,20},{1,9},{5... | collective-permute-start | bytes 884744 | tf_op jit(solution)/shard_map/ppermute | solution.py:24
  52.1 15.1 %collective-permute-start.7 = (bf16[1152,128]{1,0:T(8,128)(2,1)S(1)}, bf16[1152,128]{1,0:T(8,128)(2,1)}, u32[]{:S(2)}, u32[]{:S(2)}) collective-permute-start(bf16[1152,128]{1,0:T(8,128)(2,1)S(1)} %shard_map.121.refs_0_), channel_id=1, source_target_pairs={{0,16},{4,20},{8,24},{12,28},{16,0},{20,4},{24,8},{28,12},{1,17},{... | collective-permute-start | bytes 884744 | tf_op jit(solution)/shard_map/ppermute | solution.py:24
  54.7 14.4 %collective-permute-start.8 = (bf16[1152,128]{1,0:T(8,128)(2,1)S(1)}, bf16[1152,128]{1,0:T(8,128)(2,1)}, u32[]{:S(2)}, u32[]{:S(2)}) collective-permute-start(bf16[1152,128]{1,0:T(8,128)(2,1)S(1)} %shard_map.121.refs_0_), channel_id=1, source_target_pairs={{0,24},{4,28},{8,16},{12,20},{16,8},{20,12},{24,0},{28,4},{1,25},{... | collective-permute-start | bytes 884744 | tf_op jit(solution)/shard_map/ppermute | solution.py:24
  56.1 14.6 %collective-permute-start.9 = (bf16[1152,128]{1,0:T(8,128)(2,1)S(1)}, bf16[1152,128]{1,0:T(8,128)(2,1)}, u32[]{:S(2)}, u32[]{:S(2)}) collective-permute-start(bf16[1152,128]{1,0:T(8,128)(2,1)S(1)} %shard_map.121.refs_0_), channel_id=1, source_target_pairs={{0,4},{4,0},{8,12},{12,8},{16,20},{20,16},{24,28},{28,24},{1,5},{5... | collective-permute-start | bytes 884744 | tf_op jit(solution)/shard_map/ppermute | solution.py:24
  61.4 9.8 %collective-permute-start.10 = (bf16[1152,128]{1,0:T(8,128)(2,1)S(1)}, bf16[1152,128]{1,0:T(8,128)(2,1)}, u32[]{:S(2)}, u32[]{:S(2)}) collective-permute-start(bf16[1152,128]{1,0:T(8,128)(2,1)S(1)} %collective-permute-done.6.refs_1_), channel_id=1, source_target_pairs={{0,4},{4,0},{8,12},{12,8},{16,20},{20,16},{24,28},{28,24},{1,5},{5... | collective-permute-start | bytes 884744 | tf_op jit(solution)/shard_map/ppermute | solution.py:24
  67.2 6.1 %collective-permute-start.11 = (bf16[1152,128]{1,0:T(8,128)(2,1)}, bf16[1152,128]{1,0:T(8,128)(2,1)}, u32[]{:S(2)}, u32[]{:S(2)}) collective-permute-start(bf16[1152,128]{1,0:T(8,128)(2,1)} %collective-permute-done.7.refs_2_), channel_id=1, source_target_pairs={{0,4},{4,0},{8,12},{12,8},{16,20},{20,16},{24,28},{28,24},{1,5},{5... | collective-permute-start | bytes 884744 | tf_op jit(solution)/shard_map/ppermute | solution.py:24
  69.2 6.0 %collective-permute-start.12 = (bf16[1152,128]{1,0:T(8,128)(2,1)}, bf16[1152,128]{1,0:T(8,128)(2,1)}, u32[]{:S(2)}, u32[]{:S(2)}) collective-permute-start(bf16[1152,128]{1,0:T(8,128)(2,1)} %collective-permute-done.8.refs_3_), channel_id=1, source_target_pairs={{0,4},{4,0},{8,12},{12,8},{16,20},{20,16},{24,28},{28,24},{1,5},{5... | collective-permute-start | bytes 884744 | tf_op jit(solution)/shard_map/ppermute | solution.py:24
  70.7 8.2 %collective-permute-start = (bf16[64,768]{1,0:T(8,128)(2,1)S(1)}, bf16[64,768]{1,0:T(8,128)(2,1)S(1)}, u32[]{:S(2)}, u32[]{:S(2)}) collective-permute-start(bf16[64,768]{1,0:T(8,128)(2,1)S(1)} %get-tuple-element.30), channel_id=1, source_target_pairs={{0,2},{1,3},{2,0},{3,1},{4,6},{5,7},{6,4},{7,5},{8,10},{9,11},{10,... | collective-permute-start | bytes 294920 | tf_op jit(solution)/shard_map/ppermute | solution.py:24
  71.2 9.5 %collective-permute-start.1 = (bf16[64,768]{1,0:T(8,128)(2,1)S(1)}, bf16[64,768]{1,0:T(8,128)(2,1)S(1)}, u32[]{:S(2)}, u32[]{:S(2)}) collective-permute-start(bf16[64,768]{1,0:T(8,128)(2,1)S(1)} %get-tuple-element.29.kept), channel_id=1, source_target_pairs={{0,1},{1,0},{2,3},{3,2},{4,5},{5,4},{6,7},{7,6},{8,9},{9,8},{10,11... | collective-permute-start | bytes 294920 | tf_op jit(solution)/shard_map/ppermute | solution.py:24
  73.3 7.4 %collective-permute-start.2 = (bf16[64,768]{1,0:T(8,128)(2,1)S(1)}, bf16[64,768]{1,0:T(8,128)(2,1)S(1)}, u32[]{:S(2)}, u32[]{:S(2)}) collective-permute-start(bf16[64,768]{1,0:T(8,128)(2,1)S(1)} %get-tuple-element.30), channel_id=1, source_target_pairs={{0,3},{1,2},{2,1},{3,0},{4,7},{5,6},{6,5},{7,4},{8,11},{9,10},{10,... | collective-permute-start | bytes 294920 | tf_op jit(solution)/shard_map/ppermute | solution.py:24
  80.7 6.5 %copy-start.11 = (bf16[768]{0:T(1024)(128)(2,1)S(1)}, bf16[768]{0:T(1024)(128)(2,1)}, u32[]{:S(2)}) copy-start(bf16[768]{0:T(1024)(128)(2,1)} %param.21) | copy-start | bytes 4612
  84.7 7.6 %collective-permute-start.13 = (bf16[128,768]{1,0:T(8,128)(2,1)S(1)}, bf16[128,768]{1,0:T(8,128)(2,1)S(1)}, u32[]{:S(2)}, u32[]{:S(2)}) collective-permute-start(bf16[128,768]{1,0:T(8,128)(2,1)S(1)} %get-tuple-element.39), channel_id=1, source_target_pairs={{0,1},{1,0},{2,3},{3,2},{4,5},{5,4},{6,7},{7,6},{8,9},{9,8},{10,11... | collective-permute-start | bytes 589832 | tf_op jit(solution)/shard_map/ppermute | solution.py:24
  92.5 6.4 %collective-permute-start.20 = (bf16[128,768]{1,0:T(8,128)(2,1)S(1)}, bf16[128,768]{1,0:T(8,128)(2,1)S(1)}, u32[]{:S(2)}, u32[]{:S(2)}) collective-permute-start(bf16[128,768]{1,0:T(8,128)(2,1)S(1)} %get-tuple-element.41.normed), channel_id=1, source_target_pairs={{0,1},{1,0},{2,3},{3,2},{4,5},{5,4},{6,7},{7,6},{8,9},{9,8},{10,11... | collective-permute-start | bytes 589832 | tf_op jit(solution)/shard_map/ppermute | solution.py:24
  99.9 7.2 %collective-permute-start.21 = (bf16[64,768]{1,0:T(8,128)(2,1)S(1)}, bf16[64,768]{1,0:T(8,128)(2,1)S(1)}, u32[]{:S(2)}, u32[]{:S(2)}) collective-permute-start(bf16[64,768]{1,0:T(8,128)(2,1)S(1)} %get-tuple-element.47), channel_id=1, source_target_pairs={{0,3},{1,2},{2,1},{3,0},{4,7},{5,6},{6,5},{7,4},{8,11},{9,10},{10,... | collective-permute-start | bytes 294920 | tf_op jit(solution)/shard_map/ppermute | solution.py:24
  102.6 8.0 %collective-permute-start.19 = (bf16[64,768]{1,0:T(8,128)(2,1)S(1)}, bf16[64,768]{1,0:T(8,128)(2,1)S(1)}, u32[]{:S(2)}, u32[]{:S(2)}) collective-permute-start(bf16[64,768]{1,0:T(8,128)(2,1)S(1)} %fusion.2), channel_id=1, source_target_pairs={{0,2},{1,3},{2,0},{3,1},{4,6},{5,7},{6,4},{7,5},{8,10},{9,11},{10,... | collective-permute-start | bytes 294920 | tf_op jit(solution)/shard_map/ppermute | solution.py:24
  103.7 6.9 %collective-permute-start.22 = (bf16[64,768]{1,0:T(8,128)(2,1)S(1)}, bf16[64,768]{1,0:T(8,128)(2,1)S(1)}, u32[]{:S(2)}, u32[]{:S(2)}) collective-permute-start(bf16[64,768]{1,0:T(8,128)(2,1)S(1)} %get-tuple-element.48), channel_id=1, source_target_pairs={{0,1},{1,0},{2,3},{3,2},{4,5},{5,4},{6,7},{7,6},{8,9},{9,8},{10,11... | collective-permute-start | bytes 294920 | tf_op jit(solution)/shard_map/ppermute | solution.py:24

commit v7 on v6

--- a/solution.py
+++ b/solution.py
@@ -9,6 +9,7 @@
 SEL_DEV = 2
 HEAD_DIM = 64
 SPREAD = 8
+CHIPS = (0, 6, 2, 4)
 BF16 = jnp.bfloat16
 F32 = jnp.float32
 
@@ -36,18 +37,30 @@
 SMALL = pltpu.CompilerParams(vmem_limit_bytes=4 * 1024 * 1024)
 
 
-def copier(body, outs, where, *operands):
+def copier(body, outs, where, *operands, aliases={}):
     return pl.pallas_call(
         body,
         in_specs=[SCALARS] + [FAST] * len(operands),
         out_specs=tuple(FAST for _ in outs),
         out_shape=tuple(pltpu.VMEM(shape, BF16) for shape in outs),
         compiler_params=SMALL,
+        input_output_aliases=aliases,
     )(where, *(pltpu.with_memory_space_constraint(x, pltpu.VMEM) for x in operands))
 
 
-def route_kernel(own, owner_row, selected, dest_slot, candidates, outgoing, senders, sem):
+def route_kernel(
+    own, owner_row, selected, dest_slot, candidates, up, down, outgoing, senders, mlp_piece, sem
+):
     me = own[0]
+    size = up.shape[0] // SPREAD
+    copies = [
+        pltpu.make_async_copy(
+            source.at[block(me % SPREAD, size)], mlp_piece.at[pl.ds(n * size, size)], sem.at[1 + n]
+        )
+        for n, source in enumerate((up, down))
+    ]
+    for copy in copies:
+        copy.start()
 
     def visit(i, sent):
         row = owner_row[selected[i]]
@@ -73,24 +86,34 @@
         return carry
 
     lax.fori_loop(0, sent, finish, 0)
-
-
-def route(owner_row, selected, dest_slot, candidates):
+    for copy in copies:
+        copy.wait()
+
+
+def route(owner_row, selected, dest_slot, candidates, up, down):
     learners = lax.axis_size("dp")
     own = jnp.full((1,), lax.axis_index("dp"), jnp.int32)
     shape = (learners,) + candidates.shape[1:]
     small = learners <= 2 * SPREAD
     return pl.pallas_call(
         route_kernel,
-        in_specs=[SCALARS] * 4 + [ANY],
-        out_specs=(FAST, SCALARS),
+        in_specs=[SCALARS] * 4 + [ANY, SLOW, SLOW],
+        out_specs=(FAST, SCALARS, FAST),
         out_shape=(
             pltpu.VMEM(shape, BF16) if small else jax.ShapeDtypeStruct(shape, BF16),
             jax.ShapeDtypeStruct((SEL_DEV,), jnp.int32),
+            pltpu.VMEM((2 * up.shape[0] // SPREAD, up.shape[1]), BF16),
         ),
-        scratch_shapes=[pltpu.SemaphoreType.DMA((1,))],
+        scratch_shapes=[pltpu.SemaphoreType.DMA((3,))],
         compiler_params=pltpu.CompilerParams(vmem_limit_bytes=24 * 1024 * 1024),
-    )(own, owner_row, selected, dest_slot, candidates)
+    )(
+        own,
+        owner_row,
+        selected,
+        dest_slot,
+        candidates,
+        *(pltpu.with_memory_space_constraint(x, pltpu.HBM) for x in (up, down)),
+    )
 
 
 def choose_kernel(where, senders, incoming, kept, given, sem):
@@ -149,47 +172,14 @@
     return pl.ds(pl.multiple_of(index * size, size), size)
 
 
-def extract_kernel(where, embed, attn, up, down, embed_piece, both_piece, mlp_piece, sem):
+def extract_kernel(where, embed, attn, embed_piece, both_piece):
     piece = where[0]
     rows = embed.shape[0]
-    size = up.shape[0] // SPREAD
-    copies = [
-        pltpu.make_async_copy(up.at[block(piece, size)], mlp_piece.at[pl.ds(0, size)], sem.at[0]),
-        pltpu.make_async_copy(
-            down.at[block(piece, size)], mlp_piece.at[pl.ds(size, size)], sem.at[1]
-        ),
-    ]
-    for copy in copies:
-        copy.start()
     unit = embed[:, lanes(piece)]
     embed_piece[...] = unit
     both_piece[:rows] = unit
     for i in range(3):
         both_piece[(1 + i) * rows : (2 + i) * rows] = attn[attn_unit(attn, 3 * piece + i)]
-    for copy in copies:
-        copy.wait()
-
-
-def extract(where, embed, attn, up, down):
-    rows = embed.shape[0]
-    return pl.pallas_call(
-        extract_kernel,
-        in_specs=[SCALARS, FAST, FAST, SLOW, SLOW],
-        out_specs=(FAST, FAST, FAST),
-        out_shape=(
-            pltpu.VMEM((rows, UNIT), BF16),
-            pltpu.VMEM((4 * rows, UNIT), BF16),
-            pltpu.VMEM((2 * up.shape[0] // SPREAD, up.shape[1]), BF16),
-        ),
-        scratch_shapes=[pltpu.SemaphoreType.DMA((2,))],
-        compiler_params=SMALL,
-    )(
-        where,
-        pltpu.with_memory_space_constraint(embed, pltpu.VMEM),
-        pltpu.with_memory_space_constraint(attn, pltpu.VMEM),
-        pltpu.with_memory_space_constraint(up, pltpu.HBM),
-        pltpu.with_memory_space_constraint(down, pltpu.HBM),
-    )
 
 
 def units_kernel(where, neighbour, opposite, third, target):
@@ -207,13 +197,11 @@
         target[n * rows : (n + 1) * rows] = part[...]
 
 
-def place_attn_kernel(where, embed, *refs):
-    *pieces, embed_whole, attn_far = refs
+def place_pieces(where, pieces, first, embed_whole, attn_far):
     piece, group = where[0], where[1]
-    rows = embed.shape[0]
-    embed_whole[block(group, rows)] = embed[...]
-    for n, source in enumerate(pieces):
-        p = piece ^ (2 * (n % (SPREAD // 2)) + n // (SPREAD // 2))
+    rows = pieces[0].shape[0] // 6
+    for n, source in enumerate(pieces, first):
+        p = piece ^ (CHIPS[n % len(CHIPS)] + n // len(CHIPS))
         for k in range(3):
             at = k * rows
             embed_whole[block(group ^ (k + 1), rows), lanes(p)] = source[at : at + rows]
@@ -221,12 +209,23 @@
             attn_far[attn_unit(attn_far, 3 * p + k)] = source[at : at + rows]
 
 
+def place_attn_kernel(where, embed, *refs):
+    *pieces, embed_whole, attn_far = refs
+    embed_whole[block(where[1], embed.shape[0])] = embed[...]
+    place_pieces(where, pieces, 0, embed_whole, attn_far)
+
+
+def place_rest_kernel(where, embed_in, attn_in, *refs):
+    *pieces, embed_whole, attn_far = refs
+    place_pieces(where, pieces, 2 * len(CHIPS) - len(pieces), embed_whole, attn_far)
+
+
 def place_mlp_kernel(where, mine, others, up_far, down_far):
     piece = where[0]
     size = up_far.shape[0] // SPREAD
     for source, core in ((mine, 0), (others, 1)):
-        for n in range(SPREAD // 2):
-            p = piece ^ (2 * n + core)
+        for n, bits in enumerate(CHIPS):
+            p = piece ^ (bits + core)
             at = n * 2 * size
             up_far[block(p, size)] = source[at : at + size]
             down_far[block(p, size)] = source[at + size : at + 2 * size]
@@ -234,7 +233,7 @@
 
 def neighbours_of(piece):
     parts = [piece]
-    for bits in range(2, SPREAD, 2):
+    for bits in CHIPS[1:]:
         parts.append(swap(piece, "dp", bits))
     return parts
 
@@ -274,11 +273,11 @@
     quarter, pixel_width = kept.shape
     count = embed.shape[1] - pixel_width
     half = 2 * quarter
-    pixels = jnp.concatenate([kept[...], opposite[...], neighbour[...], third[...]], axis=0)
+    pixels = jnp.concatenate([kept[...], third[...], neighbour[...], opposite[...]], axis=0)
     row = lax.broadcasted_iota(jnp.int32, (count, count), 0)
     column = lax.broadcasted_iota(jnp.int32, (count, count), 1)
     block_of = row // quarter
-    turned = (block_of >> 1) + 2 * (block_of & 1)
+    turned = (block_of >> 1) ^ (3 * (block_of & 1))
     spot = (turned ^ group) * quarter + row % quarter
     picks = jnp.where(spot == column, 1.0, 0.0).astype(BF16)
     product = turned_dot(pixels, embed[:, :pixel_width]) + turned_dot(picks, embed[:, pixel_width:])
@@ -385,12 +384,12 @@
     )(*held(operands))
 
 
-def second_kernel(normed, up_far, down_far, up_own, down_own, near, third):
+def second_kernel(normed, up_far, down_far, up_own, down_own, near, opposite):
     part = feed_through(normed[...], up_far[...], down_far[...])
     part = part + feed_through(normed[...], up_own[...], down_own[...])
     quarter = near.shape[0]
     near[...] = part[:quarter].astype(BF16)
-    third[...] = part[quarter:].astype(BF16)
+    opposite[...] = part[quarter:].astype(BF16)
 
 
 def feed_second(*operands):
@@ -424,27 +423,28 @@
     quarter = candidates.shape[1]
     where = jnp.stack([lax.axis_index("dp") % SPREAD, group]).astype(jnp.int32)
 
-    outgoing, senders = route(owner_row, selected, dest_slot, candidates)
+    outgoing, senders, mlp_piece = route(
+        owner_row, selected, dest_slot, candidates, up_weight, down_weight
+    )
     incoming = lax.all_to_all(outgoing, "dp", split_axis=0, concat_axis=0, tiled=True)
 
     pixel_width, width = patch_weight.shape
     model = out_weight.shape[1]
     embed_own = jnp.concatenate([patch_weight.T, positions.T], axis=1)
     attn_own = jnp.concatenate([qkv_weight.transpose(1, 2, 0).reshape(-1, model), out_weight])
-    embed_piece, both_piece, mlp_piece = extract(where, embed_own, attn_own, up_weight, down_weight)
+    embed_piece, both_piece = copier(
+        extract_kernel, ((width, UNIT), (4 * width, UNIT)), where, embed_own, attn_own
+    )
     third = swap(embed_piece, "mp", 3)
     opposite = swap(both_piece, "mp", 2)
     neighbour = swap(embed_piece, "mp", 1)
     units = copier(units_kernel, ((6 * width, UNIT),), where, neighbour, opposite, third)[0]
     near = neighbours_of(units)
     far = [other_core(part) for part in near]
+    shapes = ((groups * width, pixel_width + positions.shape[0]), attn_own.shape)
+    placed = copier(place_attn_kernel, shapes, where, embed_own, *near, *far[:2])
     embed_whole, attn_far = copier(
-        place_attn_kernel,
-        ((groups * width, pixel_width + positions.shape[0]), attn_own.shape),
-        where,
-        embed_own,
-        *near,
-        *far,
+        place_rest_kernel, shapes, where, *placed, *far[2:], aliases={1: 0, 2: 1}
     )
     mlp_piece = swap(mlp_piece, "mp", 2)
     near2 = neighbours_of(mlp_piece)
@@ -471,9 +471,9 @@
     neighbour2 = swap(normed2, "mp", 1)
     feed = feed_first(own_kernel, normed2, up_own, down_own)
     feed = feed_first(first_kernel, normed2, up_far, down_far, feed)
-    from_opposite = swap((after_attn + feed)[quarter:].astype(BF16), "mp", 2)
-    for_near, for_third = feed_second(neighbour2, up_far, down_far, up_own, down_own)
-    from_third = swap(for_third, "mp", 3)
+    from_third = swap((after_attn + feed)[quarter:].astype(BF16), "mp", 3)
+    for_near, for_opposite = feed_second(neighbour2, up_far, down_far, up_own, down_own)
+    from_opposite = swap(for_opposite, "mp", 2)
     from_neighbour = swap(for_near, "mp", 1)
     kept_out = (after_attn[:quarter] + (feed[:quarter] + from_neighbour.astype(F32))).astype(BF16)
     given_out = (from_opposite.astype(F32) + from_third.astype(F32)).astype(BF16)

time: 112 us -> 112 us (level)
  waiting for transfers between devices: 51.1 us -> 56.1 us
  other arithmetic: 3.29 us -> 1 us
  starting transfers between devices: 34.5 us -> 32.7 us
    ppermute x23, waiting for transfers between devices: 51.1 us -> 56.1 us  [swap(): lax.ppermute(value, axis, [(i, i ^ bits) for i in range(lax.axis_size(axi...]
    ppermute x23, starting transfers between devices: 30.3 us -> 28.5 us  [swap(): lax.ppermute(value, axis, [(i, i ^ bits) for i in range(lax.axis_size(axi...]
    pallas_call x2 -> x1, Pallas kernels: 4.09 us -> 2.45 us  [route(): pl.pallas_call(route_kernel, in_specs=[SCALARS] * 4 + [ANY, SLOW, SLOW],...]
    pallas_call x4 -> x6, Pallas kernels: 4.73 us -> 6.17 us  [copier(): pl.pallas_call(body, in_specs=[SCALARS] + [FAST] * len(operands), out_spe...]
    concatenate x1, other arithmetic: 1.34 us -> 0.08 us  [layer(): jnp.concatenate([qkv_weight.transpose(1, 2, 0).reshape(-1, model), out_we...]
    unnamed x24 -> x20, local copies, waits for them, and re-layouts: 3.48 us -> 3.13 us
where the time goes in v7:
time: 112 us
  waiting for transfers between devices  56.1 us (50%)
  starting transfers between devices  32.7 us (29%)
  Pallas kernels  18.6 us (17%)
  local copies, waits for them, and re-layouts  3.14 us (3%)
    ppermute x23, waiting for transfers between devices, swap(): lax.ppermute(value, axis, [(i, i ^ bits) for i in range(lax.axis_size(axi...  56.1 us
    ppermute x23, starting transfers between devices, swap(): lax.ppermute(value, axis, [(i, i ^ bits) for i in range(lax.axis_size(axi...  28.5 us
    pallas_call x6, Pallas kernels, copier(): pl.pallas_call(body, in_specs=[SCALARS] + [FAST] * len(operands), out_spe...  6.17 us
    all_to_all x1, starting transfers between devices, layer(): lax.all_to_all(outgoing, 'dp', split_axis=0, concat_axis=0, tiled=True)  4.22 us
    pallas_call x1, Pallas kernels, attend(): pl.pallas_call(attend_kernel, in_specs=[SCALARS] + [FAST] * 8, out_specs=...  3.96 us
    unnamed x20, local copies, waits for them, and re-layouts  3.13 us
    pallas_call x1, Pallas kernels, route(): pl.pallas_call(route_kernel, in_specs=[SCALARS] * 4 + [ANY, SLOW, SLOW],...  2.45 us
  transfers between devices with their start and end apart: 24, of which 13 were waited for; matrix products, arithmetic and copies ran while one was open for 0% of the time, Pallas kernels for 14%

profile of v7, /device:TPU:0, one launch (start us, length us, event | category | flops | bytes accessed | tf_op | source)
XLA Modules:
  0.0 111.8 jit_solution(18389417708165581920)
XLA Ops:
  0.0 1.1 %copy-done = bf16[8,64,768]{2,1,0:T(8,128)(2,1)S(1)} copy-done((bf16[8,64,768]{2,1,0:T(8,128)(2,1)S(1)}, bf16[8,64,768]{2,1,0:T(8,128)(2,1)}, u32[]{:S(2)}) %copy-start) | copy-done | bytes 786456
  1.1 0.7 copy-done.1
  1.8 0.7 copy-done.2
  2.4 0.7 copy-done.3
  3.1 2.4 %shard_map.118 = (bf16[8,64,768]{2,1,0:T(8,128)(2,1)}, s32[2]{0:T(128)S(1)}, bf16[192,768]{1,0:T(8,128)(2,1)S(1)}) custom-call(s32[1]{0:T(128)} %bitcast.2.own, s32[64]{0:T(128)S(1)} %copy-done.1, s32[16]{0:T(128)S(1)} %copy-done.2, s32[16]{0:T(128)S(1)} %copy-done.3, bf16[8,64,768]{2,1,0:T(8,128)(2,1)S(1)} %copy-done, bf16[768,768]{1,0:T(8,128)(2,1)} %up.3, ...), custom_call_target="tpu_custom_call" | custom-call | tf_op jit(solution)/shard_map/pallas_call | solution.py:98
  5.6 4.1 %collective-permute-start.15 = (bf16[192,768]{1,0:T(8,128)(2,1)S(1)}, bf16[192,768]{1,0:T(8,128)(2,1)S(1)}, u32[]{:S(2)}, u32[]{:S(2)}) collective-permute-start(bf16[192,768]{1,0:T(8,128)(2,1)S(1)} %get-tuple-element.45), channel_id=1, source_target_pairs={{0,2},{1,3},{2,0},{3,1},{4,6},{5,7},{6,4},{7,5},{8,10},{9,11},{10,... | collective-permute-start | bytes 884744 | tf_op jit(solution)/shard_map/ppermute | solution.py:25
  9.7 13.3 %collective-permute-done.15.refs_0_ = bf16[192,768]{1,0:T(8,128)(2,1)S(1)} collective-permute-done((bf16[192,768]{1,0:T(8,128)(2,1)S(1)}, bf16[192,768]{1,0:T(8,128)(2,1)S(1)}, u32[]{:S(2)}, u32[]{:S(2)}) %collective-permute-start.15) | collective-permute-done | bytes 294944 | tf_op jit(solution)/shard_map/ppermute | solution.py:25
  23.0 2.5 %collective-permute-start.16 = (bf16[192,768]{1,0:T(8,128)(2,1)S(1)}, bf16[192,768]{1,0:T(8,128)(2,1)S(1)}, u32[]{:S(2)}, u32[]{:S(2)}) collective-permute-start(bf16[192,768]{1,0:T(8,128)(2,1)S(1)} %collective-permute-done.15.refs_0_), channel_id=1, source_target_pairs={{0,24},{4,28},{8,16},{12,20},{16,8},{20,12},{24,0},{28,4},{1,25},{... | collective-permute-start | bytes 884744 | tf_op jit(solution)/shard_map/ppermute | solution.py:25
  25.5 0.5 collective-permute-start.17
  26.1 0.5 collective-permute-start.18
  26.5 0.1 pad_add_fusion.where
  26.6 0.1 pad_maximum_fusion.attn.own
  26.7 0.0 copy-start.6
  26.7 0.0 copy-start.7
  26.7 7.1 %collective-permute-done.16.refs_1_ = bf16[192,768]{1,0:T(8,128)(2,1)S(1)} collective-permute-done((bf16[192,768]{1,0:T(8,128)(2,1)S(1)}, bf16[192,768]{1,0:T(8,128)(2,1)S(1)}, u32[]{:S(2)}, u32[]{:S(2)}) %collective-permute-start.16) | collective-permute-done | bytes 294944 | tf_op jit(solution)/shard_map/ppermute | solution.py:25
  33.8 4.5 %collective-permute-done.17.refs_2_ = bf16[192,768]{1,0:T(8,128)(2,1)S(1)} collective-permute-done((bf16[192,768]{1,0:T(8,128)(2,1)S(1)}, bf16[192,768]{1,0:T(8,128)(2,1)S(1)}, u32[]{:S(2)}, u32[]{:S(2)}) %collective-permute-start.17) | collective-permute-done | bytes 294944 | tf_op jit(solution)/shard_map/ppermute | solution.py:25
  38.3 0.1 collective-permute-done.18.refs_3_
  38.4 0.6 shard_map.128.mine
  39.0 0.1 collective-permute-start.19
  39.2 0.6 shard_map.120
  39.8 0.1 collective-permute-start.4
  39.9 0.0 copy-start.8
  39.9 4.2 %all-to-all-start = ((bf16[8,64,768]{2,1,0:T(8,128)(2,1)}), bf16[8,64,768]{2,1,0:T(8,128)(2,1)}, u32[]{:S(2)}, u32[]{:S(2)}) async-start(bf16[8,64,768]{2,1,0:T(8,128)(2,1)} %get-tuple-element.30), calls=%async_computation | async-start | bytes 1572864 | tf_op jit(solution)/shard_map/all_to_all | solution.py:429
  44.1 5.1 %collective-permute-start.3 = (bf16[192,128]{1,0:T(8,128)(2,1)S(1)}, bf16[192,128]{1,0:T(8,128)(2,1)S(1)}, u32[]{:S(2)}, u32[]{:S(2)}) collective-permute-start(bf16[192,128]{1,0:T(8,128)(2,1)S(1)} %get-tuple-element.33), channel_id=1, source_target_pairs={{0,1},{1,0},{2,3},{3,2},{4,5},{5,4},{6,7},{7,6},{8,9},{9,8},{10,11... | collective-permute-start | bytes 147464 | tf_op jit(solution)/shard_map/ppermute | solution.py:25
  49.2 0.0 collective-permute-start.5
  49.2 4.1 %collective-permute-done.3.neighbour = bf16[192,128]{1,0:T(8,128)(2,1)S(1)} collective-permute-done((bf16[192,128]{1,0:T(8,128)(2,1)S(1)}, bf16[192,128]{1,0:T(8,128)(2,1)S(1)}, u32[]{:S(2)}, u32[]{:S(2)}) %collective-permute-start.3) | collective-permute-done | bytes 49184 | tf_op jit(solution)/shard_map/ppermute | solution.py:25
  53.3 1.8 %collective-permute-done.5.third = bf16[192,128]{1,0:T(8,128)(2,1)S(1)} collective-permute-done((bf16[192,128]{1,0:T(8,128)(2,1)S(1)}, bf16[192,128]{1,0:T(8,128)(2,1)S(1)}, u32[]{:S(2)}, u32[]{:S(2)}) %collective-permute-start.5) | collective-permute-done | bytes 49184 | tf_op jit(solution)/shard_map/ppermute | solution.py:25
  55.1 0.0 collective-permute-done.4.opposite
  55.1 0.6 shard_map.121.refs_0_
  55.7 2.8 %collective-permute-start.6 = (bf16[1152,128]{1,0:T(8,128)(2,1)S(1)}, bf16[1152,128]{1,0:T(8,128)(2,1)S(1)}, u32[]{:S(2)}, u32[]{:S(2)}) collective-permute-start(bf16[1152,128]{1,0:T(8,128)(2,1)S(1)} %shard_map.121.refs_0_), channel_id=1, source_target_pairs={{0,24},{4,28},{8,16},{12,20},{16,8},{20,12},{24,0},{28,4},{1,25},{... | collective-permute-start | bytes 884744 | tf_op jit(solution)/shard_map/ppermute | solution.py:25
  58.5 0.6 collective-permute-start.7
  59.1 0.2 collective-permute-start.8
  59.3 0.0 collective-permute-start.9
  59.3 7.3 %collective-permute-done.6.refs_1_ = bf16[1152,128]{1,0:T(8,128)(2,1)S(1)} collective-permute-done((bf16[1152,128]{1,0:T(8,128)(2,1)S(1)}, bf16[1152,128]{1,0:T(8,128)(2,1)S(1)}, u32[]{:S(2)}, u32[]{:S(2)}) %collective-permute-start.6) | collective-permute-done | bytes 294944 | tf_op jit(solution)/shard_map/ppermute | solution.py:25
  66.6 4.5 %collective-permute-done.7.refs_2_ = bf16[1152,128]{1,0:T(8,128)(2,1)} collective-permute-done((bf16[1152,128]{1,0:T(8,128)(2,1)S(1)}, bf16[1152,128]{1,0:T(8,128)(2,1)}, u32[]{:S(2)}, u32[]{:S(2)}) %collective-permute-start.7) | collective-permute-done | bytes 294944 | tf_op jit(solution)/shard_map/ppermute | solution.py:25
  71.1 0.0 collective-permute-start.11
  71.1 0.0 collective-permute-done.8.refs_3_
  71.1 0.5 collective-permute-start.12
  71.7 1.5 %shard_map.119 = (bf16[64,768]{1,0:T(8,128)(2,1)S(1)}, bf16[64,768]{1,0:T(8,128)(2,1)S(1)}) custom-call(s32[2]{0:T(128)S(1)} %pad_add_fusion.where, s32[2]{0:T(128)S(1)} %get-tuple-element.29.senders, bf16[8,64,768]{2,1,0:T(8,128)(2,1)} %all-to-all-done.incoming), custom_call_target="tpu_custom_call" | custom-call | tf_op jit(solution)/shard_map/pallas_call | solution.py:133
  73.2 0.0 collective-permute-done.9.refs_4_
  73.2 0.8 collective-permute-start
  74.0 1.9 %collective-permute-start.1 = (bf16[64,768]{1,0:T(8,128)(2,1)S(1)}, bf16[64,768]{1,0:T(8,128)(2,1)S(1)}, u32[]{:S(2)}, u32[]{:S(2)}) collective-permute-start(bf16[64,768]{1,0:T(8,128)(2,1)S(1)} %get-tuple-element.31.kept), channel_id=1, source_target_pairs={{0,1},{1,0},{2,3},{3,2},{4,5},{5,4},{6,7},{7,6},{8,9},{9,8},{10,11... | collective-permute-start | bytes 294920 | tf_op jit(solution)/shard_map/ppermute | solution.py:25
  75.9 2.1 %collective-permute-start.2 = (bf16[64,768]{1,0:T(8,128)(2,1)S(1)}, bf16[64,768]{1,0:T(8,128)(2,1)S(1)}, u32[]{:S(2)}, u32[]{:S(2)}) collective-permute-start(bf16[64,768]{1,0:T(8,128)(2,1)S(1)} %get-tuple-element.32), channel_id=1, source_target_pairs={{0,3},{1,2},{2,1},{3,0},{4,7},{5,6},{6,5},{7,4},{8,11},{9,10},{10,... | collective-permute-start | bytes 294920 | tf_op jit(solution)/shard_map/ppermute | solution.py:25
  78.1 1.7 %shard_map.122 = (bf16[768,1024]{1,0:T(8,128)(2,1)S(1)}, bf16[768,768]{1,0:T(8,128)(2,1)S(1)}) custom-call(s32[2]{0:T(128)S(1)} %pad_add_fusion.where, bf16[192,1024]{1,0:T(8,128)(2,1)S(1)} %pad_maximum_fusion.1.embed, bf16[1152,128]{1,0:T(8,128)(2,1)S(1)} %shard_map.121.refs_0_, bf16[1152,128]{1,0:T(8,128)(2,1)S(1)} %collective-permute-done.6.refs_1_, ...), custom_call_target="tpu_custom_call" | custom-call | tf_op jit(solution)/shard_map/pallas_call | solution.py:41
  79.8 0.0 collective-permute-done.12.refs_1_
  79.8 1.2 %shard_map.123 = (bf16[768,1024]{1,0:T(8,128)(2,1)S(1)}, bf16[768,768]{1,0:T(8,128)(2,1)S(1)}) custom-call(s32[2]{0:T(128)S(1)} %pad_add_fusion.where, bf16[768,1024]{1,0:T(8,128)(2,1)S(1)} %get-tuple-element.35.embed_in, bf16[768,768]{1,0:T(8,128)(2,1)S(1)} %get-tuple-element.36.attn_in, ...), custom_call_target="tpu_custom_call", output_to_operand_aliasing={{0}: (1, {}), {1}: (2, {})} | custom-call | tf_op jit(solution)/shard_map/pallas_call | solution.py:41
  81.1 4.1 %collective-permute-done.2.third = bf16[64,768]{1,0:T(8,128)(2,1)S(1)} collective-permute-done((bf16[64,768]{1,0:T(8,128)(2,1)S(1)}, bf16[64,768]{1,0:T(8,128)(2,1)S(1)}, u32[]{:S(2)}, u32[]{:S(2)}) %collective-permute-start.2) | collective-permute-done | bytes 98336 | tf_op jit(solution)/shard_map/ppermute | solution.py:25
  85.2 4.0 %shard_map.124 = (bf16[576,256]{1,0:T(8,128)(2,1)S(1)}, bf16[576,256]{1,0:T(8,128)(2,1)S(1)}, bf16[128,768]{1,0:T(8,128)(2,1)S(1)}, bf16[128,768]{1,0:T(8,128)(2,1)S(1)}) custom-call(s32[2]{0:T(128)S(1)} %pad_add_fusion.where, bf16[64,768]{1,0:T(8,128)(2,1)S(1)} %get-tuple-element.31.kept, bf16[64,768]{1,0:T(8,128)(2,1)S(1)} %collective-permute-done.opposite, ...), custom_call_target="tpu_custom_call" | custom-call | tf_op jit(solution)/shard_map/pallas_call | solution.py:316
  89.2 0.1 collective-permute-start.13
  89.3 2.0 %shard_map.125 = (f32[128,768]{1,0:T(8,128)S(1)}, bf16[768,768]{1,0:T(8,128)(2,1)S(1)}, bf16[768,768]{1,0:T(8,128)(2,1)S(1)}) custom-call(bf16[576,256]{1,0:T(8,128)(2,1)S(1)} %get-tuple-element.39.own_qkv, bf16[576,256]{1,0:T(8,128)(2,1)S(1)} %get-tuple-element.40.far_qkv, bf16[128,768]{1,0:T(8,128)(2,1)S(1)} %get-tuple-element.41.embedded, ...), custom_call_target="tpu_custom_call" | custom-call | tf_op jit(solution)/shard_map/pallas_call | solution.py:328
  91.3 4.1 %collective-permute-done.13.other = bf16[128,768]{1,0:T(8,128)(2,1)S(1)} collective-permute-done((bf16[128,768]{1,0:T(8,128)(2,1)S(1)}, bf16[128,768]{1,0:T(8,128)(2,1)S(1)}, u32[]{:S(2)}, u32[]{:S(2)}) %collective-permute-start.13) | collective-permute-done | bytes 196640 | tf_op jit(solution)/shard_map/ppermute | solution.py:25
  95.4 0.2 shard_map.127
  95.6 0.4 collective-permute-start.14
  96.0 0.6 shard_map.131.part
  96.6 1.4 %shard_map.129 = (bf16[768,768]{1,0:T(8,128)(2,1)S(1)}, bf16[768,768]{1,0:T(8,128)(2,1)S(1)}) custom-call(s32[2]{0:T(128)S(1)} %pad_add_fusion.where, bf16[768,768]{1,0:T(8,128)(2,1)S(1)} %shard_map.128.mine, bf16[768,768]{1,0:T(8,128)(2,1)} %collective-permute-done.19.others), custom_call_target="tpu_custom_call" | custom-call | tf_op jit(solution)/shard_map/pallas_call | solution.py:41
  98.1 0.6 shard_map.132
  98.7 3.2 %collective-permute-start.21 = (bf16[64,768]{1,0:T(8,128)(2,1)S(1)}, bf16[64,768]{1,0:T(8,128)(2,1)S(1)}, u32[]{:S(2)}, u32[]{:S(2)}) collective-permute-start(bf16[64,768]{1,0:T(8,128)(2,1)S(1)} %fusion.2), channel_id=1, source_target_pairs={{0,3},{1,2},{2,1},{3,0},{4,7},{5,6},{6,5},{7,4},{8,11},{9,10},{10,... | collective-permute-start | bytes 294920 | tf_op jit(solution)/shard_map/ppermute | solution.py:25
  101.9 1.0 shard_map.130
  102.9 3.0 %collective-permute-start.20 = (bf16[64,768]{1,0:T(8,128)(2,1)S(1)}, bf16[64,768]{1,0:T(8,128)(2,1)S(1)}, u32[]{:S(2)}, u32[]{:S(2)}) collective-permute-start(bf16[64,768]{1,0:T(8,128)(2,1)S(1)} %get-tuple-element.50), channel_id=1, source_target_pairs={{0,2},{1,3},{2,0},{3,1},{4,6},{5,7},{6,4},{7,5},{8,10},{9,11},{10,... | collective-permute-start | bytes 294920 | tf_op jit(solution)/shard_map/ppermute | solution.py:25
  106.0 0.5 collective-permute-done.21
  106.5 3.5 %collective-permute-done.20 = bf16[64,768]{1,0:T(8,128)(2,1)S(1)} collective-permute-done((bf16[64,768]{1,0:T(8,128)(2,1)S(1)}, bf16[64,768]{1,0:T(8,128)(2,1)S(1)}, u32[]{:S(2)}, u32[]{:S(2)}) %collective-permute-start.20) | collective-permute-done | bytes 98336 | tf_op jit(solution)/shard_map/ppermute | solution.py:25
  110.0 1.1 collective-permute-done.22
  111.0 0.1 select_bitcast_fusion.1
  111.1 0.7 pad_maximum_fusion.2
  (28 shorter events, 0.2 us)
Async XLA Ops:
  0.0 1.1 %copy-start = (bf16[8,64,768]{2,1,0:T(8,128)(2,1)S(1)}, bf16[8,64,768]{2,1,0:T(8,128)(2,1)}, u32[]{:S(2)}) copy-start(bf16[8,64,768]{2,1,0:T(8,128)(2,1)} %candidates.1) | copy-start | bytes 2359300
  1.1 0.7 copy-start.1
  1.8 0.7 copy-start.2
  2.4 0.7 copy-start.3
  3.1 23.5 %copy-start.4 = (bf16[768,3,192]{0,2,1:T(8,128)(2,1)S(1)}, bf16[768,3,192]{0,2,1:T(8,128)(2,1)}, u32[]{:S(2)}) copy-start(bf16[768,3,192]{0,2,1:T(8,128)(2,1)} %param.18) | copy-start | bytes 2654212
  3.1 23.5 %copy-start.5 = (bf16[192,768]{1,0:T(8,128)(2,1)S(1)}, bf16[192,768]{1,0:T(8,128)(2,1)}, u32[]{:S(2)}) copy-start(bf16[192,768]{1,0:T(8,128)(2,1)} %param.19) | copy-start | bytes 884740
  5.6 17.5 %collective-permute-start.15 = (bf16[192,768]{1,0:T(8,128)(2,1)S(1)}, bf16[192,768]{1,0:T(8,128)(2,1)S(1)}, u32[]{:S(2)}, u32[]{:S(2)}) collective-permute-start(bf16[192,768]{1,0:T(8,128)(2,1)S(1)} %get-tuple-element.45), channel_id=1, source_target_pairs={{0,2},{1,3},{2,0},{3,1},{4,6},{5,7},{6,4},{7,5},{8,10},{9,11},{10,... | collective-permute-start | bytes 884744 | tf_op jit(solution)/shard_map/ppermute | solution.py:25
  23.0 10.8 %collective-permute-start.16 = (bf16[192,768]{1,0:T(8,128)(2,1)S(1)}, bf16[192,768]{1,0:T(8,128)(2,1)S(1)}, u32[]{:S(2)}, u32[]{:S(2)}) collective-permute-start(bf16[192,768]{1,0:T(8,128)(2,1)S(1)} %collective-permute-done.15.refs_0_), channel_id=1, source_target_pairs={{0,24},{4,28},{8,16},{12,20},{16,8},{20,12},{24,0},{28,4},{1,25},{... | collective-permute-start | bytes 884744 | tf_op jit(solution)/shard_map/ppermute | solution.py:25
  25.5 12.8 %collective-permute-start.17 = (bf16[192,768]{1,0:T(8,128)(2,1)S(1)}, bf16[192,768]{1,0:T(8,128)(2,1)S(1)}, u32[]{:S(2)}, u32[]{:S(2)}) collective-permute-start(bf16[192,768]{1,0:T(8,128)(2,1)S(1)} %collective-permute-done.15.refs_0_), channel_id=1, source_target_pairs={{0,8},{4,12},{8,0},{12,4},{16,24},{20,28},{24,16},{28,20},{1,9},{5... | collective-permute-start | bytes 884744 | tf_op jit(solution)/shard_map/ppermute | solution.py:25
  26.1 12.4 %collective-permute-start.18 = (bf16[192,768]{1,0:T(8,128)(2,1)S(1)}, bf16[192,768]{1,0:T(8,128)(2,1)S(1)}, u32[]{:S(2)}, u32[]{:S(2)}) collective-permute-start(bf16[192,768]{1,0:T(8,128)(2,1)S(1)} %collective-permute-done.15.refs_0_), channel_id=1, source_target_pairs={{0,16},{4,20},{8,24},{12,28},{16,0},{20,4},{24,8},{28,12},{1,17},{... | collective-permute-start | bytes 884744 | tf_op jit(solution)/shard_map/ppermute | solution.py:25
  26.7 12.4 %copy-start.6 = (bf16[768,192]{0,1:T(8,128)(2,1)S(1)}, bf16[768,192]{0,1:T(8,128)(2,1)}, u32[]{:S(2)}) copy-start(bf16[768,192]{0,1:T(8,128)(2,1)} %param.16) | copy-start | bytes 884740
  26.7 12.4 %copy-start.7 = (bf16[256,192]{0,1:T(8,128)(2,1)S(1)}, bf16[256,192]{0,1:T(8,128)(2,1)}, u32[]{:S(2)}) copy-start(bf16[256,192]{0,1:T(8,128)(2,1)} %param.17) | copy-start | bytes 294916
  39.0 57.6 %collective-permute-start.19 = (bf16[768,768]{1,0:T(8,128)(2,1)S(1)}, bf16[768,768]{1,0:T(8,128)(2,1)}, u32[]{:S(2)}, u32[]{:S(2)}) collective-permute-start(bf16[768,768]{1,0:T(8,128)(2,1)S(1)} %shard_map.128.mine), channel_id=1, source_target_pairs={{0,4},{4,0},{8,12},{12,8},{16,20},{20,16},{24,28},{28,24},{1,5},{5... | collective-permute-start | bytes 3538952 | tf_op jit(solution)/shard_map/ppermute | solution.py:25
  39.8 15.3 %collective-permute-start.4 = (bf16[768,128]{1,0:T(8,128)(2,1)S(1)}, bf16[768,128]{1,0:T(8,128)(2,1)S(1)}, u32[]{:S(2)}, u32[]{:S(2)}) collective-permute-start(bf16[768,128]{1,0:T(8,128)(2,1)S(1)} %get-tuple-element.34), channel_id=1, source_target_pairs={{0,2},{1,3},{2,0},{3,1},{4,6},{5,7},{6,4},{7,5},{8,10},{9,11},{10,... | collective-permute-start | bytes 589832 | tf_op jit(solution)/shard_map/ppermute | solution.py:25
  39.9 38.2 %copy-start.8 = (bf16[768]{0:T(1024)(128)(2,1)S(1)}, bf16[768]{0:T(1024)(128)(2,1)}, u32[]{:S(2)}) copy-start(bf16[768]{0:T(1024)(128)(2,1)} %param.20) | copy-start | bytes 4612
  39.9 31.8 %all-to-all-start = ((bf16[8,64,768]{2,1,0:T(8,128)(2,1)}), bf16[8,64,768]{2,1,0:T(8,128)(2,1)}, u32[]{:S(2)}, u32[]{:S(2)}) async-start(bf16[8,64,768]{2,1,0:T(8,128)(2,1)} %get-tuple-element.30), calls=%async_computation | async-start | bytes 1572864 | tf_op jit(solution)/shard_map/all_to_all | solution.py:429
  44.1 9.2 %collective-permute-start.3 = (bf16[192,128]{1,0:T(8,128)(2,1)S(1)}, bf16[192,128]{1,0:T(8,128)(2,1)S(1)}, u32[]{:S(2)}, u32[]{:S(2)}) collective-permute-start(bf16[192,128]{1,0:T(8,128)(2,1)S(1)} %get-tuple-element.33), channel_id=1, source_target_pairs={{0,1},{1,0},{2,3},{3,2},{4,5},{5,4},{6,7},{7,6},{8,9},{9,8},{10,11... | collective-permute-start | bytes 147464 | tf_op jit(solution)/shard_map/ppermute | solution.py:25
  49.2 5.9 %collective-permute-start.5 = (bf16[192,128]{1,0:T(8,128)(2,1)S(1)}, bf16[192,128]{1,0:T(8,128)(2,1)S(1)}, u32[]{:S(2)}, u32[]{:S(2)}) collective-permute-start(bf16[192,128]{1,0:T(8,128)(2,1)S(1)} %get-tuple-element.33), channel_id=1, source_target_pairs={{0,3},{1,2},{2,1},{3,0},{4,7},{5,6},{6,5},{7,4},{8,11},{9,10},{10,... | collective-permute-start | bytes 147464 | tf_op jit(solution)/shard_map/ppermute | solution.py:25
  55.7 10.9 %collective-permute-start.6 = (bf16[1152,128]{1,0:T(8,128)(2,1)S(1)}, bf16[1152,128]{1,0:T(8,128)(2,1)S(1)}, u32[]{:S(2)}, u32[]{:S(2)}) collective-permute-start(bf16[1152,128]{1,0:T(8,128)(2,1)S(1)} %shard_map.121.refs_0_), channel_id=1, source_target_pairs={{0,24},{4,28},{8,16},{12,20},{16,8},{20,12},{24,0},{28,4},{1,25},{... | collective-permute-start | bytes 884744 | tf_op jit(solution)/shard_map/ppermute | solution.py:25
  58.5 12.6 %collective-permute-start.7 = (bf16[1152,128]{1,0:T(8,128)(2,1)S(1)}, bf16[1152,128]{1,0:T(8,128)(2,1)}, u32[]{:S(2)}, u32[]{:S(2)}) collective-permute-start(bf16[1152,128]{1,0:T(8,128)(2,1)S(1)} %shard_map.121.refs_0_), channel_id=1, source_target_pairs={{0,8},{4,12},{8,0},{12,4},{16,24},{20,28},{24,16},{28,20},{1,9},{5... | collective-permute-start | bytes 884744 | tf_op jit(solution)/shard_map/ppermute | solution.py:25
  59.1 12.1 %collective-permute-start.8 = (bf16[1152,128]{1,0:T(8,128)(2,1)S(1)}, bf16[1152,128]{1,0:T(8,128)(2,1)}, u32[]{:S(2)}, u32[]{:S(2)}) collective-permute-start(bf16[1152,128]{1,0:T(8,128)(2,1)S(1)} %shard_map.121.refs_0_), channel_id=1, source_target_pairs={{0,16},{4,20},{8,24},{12,28},{16,0},{20,4},{24,8},{28,12},{1,17},{... | collective-permute-start | bytes 884744 | tf_op jit(solution)/shard_map/ppermute | solution.py:25
  59.3 13.9 %collective-permute-start.9 = (bf16[1152,128]{1,0:T(8,128)(2,1)S(1)}, bf16[1152,128]{1,0:T(8,128)(2,1)}, u32[]{:S(2)}, u32[]{:S(2)}) collective-permute-start(bf16[1152,128]{1,0:T(8,128)(2,1)S(1)} %shard_map.121.refs_0_), channel_id=1, source_target_pairs={{0,4},{4,0},{8,12},{12,8},{16,20},{20,16},{24,28},{28,24},{1,5},{5... | collective-permute-start | bytes 884744 | tf_op jit(solution)/shard_map/ppermute | solution.py:25
  66.6 7.4 %collective-permute-start.10 = (bf16[1152,128]{1,0:T(8,128)(2,1)S(1)}, bf16[1152,128]{1,0:T(8,128)(2,1)}, u32[]{:S(2)}, u32[]{:S(2)}) collective-permute-start(bf16[1152,128]{1,0:T(8,128)(2,1)S(1)} %collective-permute-done.6.refs_1_), channel_id=1, source_target_pairs={{0,4},{4,0},{8,12},{12,8},{16,20},{20,16},{24,28},{28,24},{1,5},{5... | collective-permute-start | bytes 884744 | tf_op jit(solution)/shard_map/ppermute | solution.py:25
  71.1 4.8 %collective-permute-start.11 = (bf16[1152,128]{1,0:T(8,128)(2,1)}, bf16[1152,128]{1,0:T(8,128)(2,1)}, u32[]{:S(2)}, u32[]{:S(2)}) collective-permute-start(bf16[1152,128]{1,0:T(8,128)(2,1)} %collective-permute-done.7.refs_2_), channel_id=1, source_target_pairs={{0,4},{4,0},{8,12},{12,8},{16,20},{20,16},{24,28},{28,24},{1,5},{5... | collective-permute-start | bytes 884744 | tf_op jit(solution)/shard_map/ppermute | solution.py:25
  71.1 8.7 %collective-permute-start.12 = (bf16[1152,128]{1,0:T(8,128)(2,1)}, bf16[1152,128]{1,0:T(8,128)(2,1)}, u32[]{:S(2)}, u32[]{:S(2)}) collective-permute-start(bf16[1152,128]{1,0:T(8,128)(2,1)} %collective-permute-done.8.refs_3_), channel_id=1, source_target_pairs={{0,4},{4,0},{8,12},{12,8},{16,20},{20,16},{24,28},{28,24},{1,5},{5... | collective-permute-start | bytes 884744 | tf_op jit(solution)/shard_map/ppermute | solution.py:25
  73.2 7.9 %collective-permute-start = (bf16[64,768]{1,0:T(8,128)(2,1)S(1)}, bf16[64,768]{1,0:T(8,128)(2,1)S(1)}, u32[]{:S(2)}, u32[]{:S(2)}) collective-permute-start(bf16[64,768]{1,0:T(8,128)(2,1)S(1)} %get-tuple-element.32), channel_id=1, source_target_pairs={{0,2},{1,3},{2,0},{3,1},{4,6},{5,7},{6,4},{7,5},{8,10},{9,11},{10,... | collective-permute-start | bytes 294920 | tf_op jit(solution)/shard_map/ppermute | solution.py:25
  74.0 7.1 %collective-permute-start.1 = (bf16[64,768]{1,0:T(8,128)(2,1)S(1)}, bf16[64,768]{1,0:T(8,128)(2,1)S(1)}, u32[]{:S(2)}, u32[]{:S(2)}) collective-permute-start(bf16[64,768]{1,0:T(8,128)(2,1)S(1)} %get-tuple-element.31.kept), channel_id=1, source_target_pairs={{0,1},{1,0},{2,3},{3,2},{4,5},{5,4},{6,7},{7,6},{8,9},{9,8},{10,11... | collective-permute-start | bytes 294920 | tf_op jit(solution)/shard_map/ppermute | solution.py:25
  75.9 9.3 %collective-permute-start.2 = (bf16[64,768]{1,0:T(8,128)(2,1)S(1)}, bf16[64,768]{1,0:T(8,128)(2,1)S(1)}, u32[]{:S(2)}, u32[]{:S(2)}) collective-permute-start(bf16[64,768]{1,0:T(8,128)(2,1)S(1)} %get-tuple-element.32), channel_id=1, source_target_pairs={{0,3},{1,2},{2,1},{3,0},{4,7},{5,6},{6,5},{7,4},{8,11},{9,10},{10,... | collective-permute-start | bytes 294920 | tf_op jit(solution)/shard_map/ppermute | solution.py:25
  85.2 4.0 %copy-start.9 = (bf16[768]{0:T(1024)(128)(2,1)S(1)}, bf16[768]{0:T(1024)(128)(2,1)}, u32[]{:S(2)}) copy-start(bf16[768]{0:T(1024)(128)(2,1)} %param.21) | copy-start | bytes 4612
  89.2 6.2 %collective-permute-start.13 = (bf16[128,768]{1,0:T(8,128)(2,1)S(1)}, bf16[128,768]{1,0:T(8,128)(2,1)S(1)}, u32[]{:S(2)}, u32[]{:S(2)}) collective-permute-start(bf16[128,768]{1,0:T(8,128)(2,1)S(1)} %get-tuple-element.43), channel_id=1, source_target_pairs={{0,1},{1,0},{2,3},{3,2},{4,5},{5,4},{6,7},{7,6},{8,9},{9,8},{10,11... | collective-permute-start | bytes 589832 | tf_op jit(solution)/shard_map/ppermute | solution.py:25
  95.6 6.3 %collective-permute-start.14 = (bf16[128,768]{1,0:T(8,128)(2,1)S(1)}, bf16[128,768]{1,0:T(8,128)(2,1)S(1)}, u32[]{:S(2)}, u32[]{:S(2)}) collective-permute-start(bf16[128,768]{1,0:T(8,128)(2,1)S(1)} %get-tuple-element.44.normed), channel_id=1, source_target_pairs={{0,1},{1,0},{2,3},{3,2},{4,5},{5,4},{6,7},{7,6},{8,9},{9,8},{10,11... | collective-permute-start | bytes 589832 | tf_op jit(solution)/shard_map/ppermute | solution.py:25
  98.7 7.8 %collective-permute-start.21 = (bf16[64,768]{1,0:T(8,128)(2,1)S(1)}, bf16[64,768]{1,0:T(8,128)(2,1)S(1)}, u32[]{:S(2)}, u32[]{:S(2)}) collective-permute-start(bf16[64,768]{1,0:T(8,128)(2,1)S(1)} %fusion.2), channel_id=1, source_target_pairs={{0,3},{1,2},{2,1},{3,0},{4,7},{5,6},{6,5},{7,4},{8,11},{9,10},{10,... | collective-permute-start | bytes 294920 | tf_op jit(solution)/shard_map/ppermute | solution.py:25
  102.9 7.0 %collective-permute-start.20 = (bf16[64,768]{1,0:T(8,128)(2,1)S(1)}, bf16[64,768]{1,0:T(8,128)(2,1)S(1)}, u32[]{:S(2)}, u32[]{:S(2)}) collective-permute-start(bf16[64,768]{1,0:T(8,128)(2,1)S(1)} %get-tuple-element.50), channel_id=1, source_target_pairs={{0,2},{1,3},{2,0},{3,1},{4,6},{5,7},{6,4},{7,5},{8,10},{9,11},{10,... | collective-permute-start | bytes 294920 | tf_op jit(solution)/shard_map/ppermute | solution.py:25
  106.0 5.1 %collective-permute-start.22 = (bf16[64,768]{1,0:T(8,128)(2,1)S(1)}, bf16[64,768]{1,0:T(8,128)(2,1)S(1)}, u32[]{:S(2)}, u32[]{:S(2)}) collective-permute-start(bf16[64,768]{1,0:T(8,128)(2,1)S(1)} %get-tuple-element.52), channel_id=1, source_target_pairs={{0,1},{1,0},{2,3},{3,2},{4,5},{5,4},{6,7},{7,6},{8,9},{9,8},{10,11... | collective-permute-start | bytes 294920 | tf_op jit(solution)/shard_map/ppermute | solution.py:25

commit v8 on v7

--- a/solution.py
+++ b/solution.py
@@ -258,9 +258,10 @@
             queries, attn_keys, attn_values = (
                 values[c * width + at : c * width + at + HEAD_DIM] for c in range(3)
             )
-            scores = columns_dot(attn_keys, queries[:, start:stop]) * HEAD_DIM ** (-0.5)
-            raised = jnp.exp(scores - jnp.max(scores, axis=0, keepdims=True))
-            probs = (raised / jnp.sum(raised, axis=0, keepdims=True)).astype(BF16)
+            scores = columns_dot(attn_keys, queries[:, start:stop])
+            raised = jnp.exp((scores - jnp.max(scores, axis=0, keepdims=True)) * HEAD_DIM ** (-0.5))
+            share = 1.0 / jnp.sum(raised, axis=0, keepdims=True)
+            probs = (raised * share).astype(BF16)
             results.append(dot(attn_values, probs).astype(BF16))
     out = jnp.concatenate([shard[3 * (shard.shape[0] // 4) :] for shard in shards], axis=0)
     return columns_dot(jnp.concatenate(results, axis=0), out)

time: 112 us -> 112 us (level)
  no operation moved by 1% of the time
where the time goes in v8:
time: 112 us
  waiting for transfers between devices  56.1 us (50%)
  starting transfers between devices  32.7 us (29%)
  Pallas kernels  18.5 us (17%)
  local copies, waits for them, and re-layouts  3.14 us (3%)
    ppermute x23, waiting for transfers between devices, swap(): lax.ppermute(value, axis, [(i, i ^ bits) for i in range(lax.axis_size(axi...  56.1 us
    ppermute x23, starting transfers between devices, swap(): lax.ppermute(value, axis, [(i, i ^ bits) for i in range(lax.axis_size(axi...  28.5 us
    pallas_call x6, Pallas kernels, copier(): pl.pallas_call(body, in_specs=[SCALARS] + [FAST] * len(operands), out_spe...  6.17 us
    all_to_all x1, starting transfers between devices, layer(): lax.all_to_all(outgoing, 'dp', split_axis=0, concat_axis=0, tiled=True)  4.22 us
    pallas_call x1, Pallas kernels, attend(): pl.pallas_call(attend_kernel, in_specs=[SCALARS] + [FAST] * 8, out_specs=...  3.94 us
    unnamed x20, local copies, waits for them, and re-layouts  3.13 us
    pallas_call x1, Pallas kernels, route(): pl.pallas_call(route_kernel, in_specs=[SCALARS] * 4 + [ANY, SLOW, SLOW],...  2.45 us
  transfers between devices with their start and end apart: 24, of which 13 were waited for; matrix products, arithmetic and copies ran while one was open for 0% of the time, Pallas kernels for 14%

profile of v8, /device:TPU:0, one launch (start us, length us, event | category | flops | bytes accessed | tf_op | source)
XLA Modules:
  0.0 111.8 jit_solution(11685513728048914184)
XLA Ops:
  0.0 1.1 %copy-done = bf16[8,64,768]{2,1,0:T(8,128)(2,1)S(1)} copy-done((bf16[8,64,768]{2,1,0:T(8,128)(2,1)S(1)}, bf16[8,64,768]{2,1,0:T(8,128)(2,1)}, u32[]{:S(2)}) %copy-start) | copy-done | bytes 786456
  1.1 0.7 copy-done.1
  1.8 0.7 copy-done.2
  2.4 0.7 copy-done.3
  3.1 2.4 %shard_map.118 = (bf16[8,64,768]{2,1,0:T(8,128)(2,1)}, s32[2]{0:T(128)S(1)}, bf16[192,768]{1,0:T(8,128)(2,1)S(1)}) custom-call(s32[1]{0:T(128)} %bitcast.2.own, s32[64]{0:T(128)S(1)} %copy-done.1, s32[16]{0:T(128)S(1)} %copy-done.2, s32[16]{0:T(128)S(1)} %copy-done.3, bf16[8,64,768]{2,1,0:T(8,128)(2,1)S(1)} %copy-done, bf16[768,768]{1,0:T(8,128)(2,1)} %up.3, ...), custom_call_target="tpu_custom_call" | custom-call | tf_op jit(solution)/shard_map/pallas_call | solution.py:98
  5.6 4.1 %collective-permute-start.15 = (bf16[192,768]{1,0:T(8,128)(2,1)S(1)}, bf16[192,768]{1,0:T(8,128)(2,1)S(1)}, u32[]{:S(2)}, u32[]{:S(2)}) collective-permute-start(bf16[192,768]{1,0:T(8,128)(2,1)S(1)} %get-tuple-element.45), channel_id=1, source_target_pairs={{0,2},{1,3},{2,0},{3,1},{4,6},{5,7},{6,4},{7,5},{8,10},{9,11},{10,... | collective-permute-start | bytes 884744 | tf_op jit(solution)/shard_map/ppermute | solution.py:25
  9.7 13.3 %collective-permute-done.15.refs_0_ = bf16[192,768]{1,0:T(8,128)(2,1)S(1)} collective-permute-done((bf16[192,768]{1,0:T(8,128)(2,1)S(1)}, bf16[192,768]{1,0:T(8,128)(2,1)S(1)}, u32[]{:S(2)}, u32[]{:S(2)}) %collective-permute-start.15) | collective-permute-done | bytes 294944 | tf_op jit(solution)/shard_map/ppermute | solution.py:25
  23.0 2.5 %collective-permute-start.16 = (bf16[192,768]{1,0:T(8,128)(2,1)S(1)}, bf16[192,768]{1,0:T(8,128)(2,1)S(1)}, u32[]{:S(2)}, u32[]{:S(2)}) collective-permute-start(bf16[192,768]{1,0:T(8,128)(2,1)S(1)} %collective-permute-done.15.refs_0_), channel_id=1, source_target_pairs={{0,24},{4,28},{8,16},{12,20},{16,8},{20,12},{24,0},{28,4},{1,25},{... | collective-permute-start | bytes 884744 | tf_op jit(solution)/shard_map/ppermute | solution.py:25
  25.5 0.5 collective-permute-start.17
  26.1 0.5 collective-permute-start.18
  26.5 0.1 pad_add_fusion.where
  26.6 0.1 pad_maximum_fusion.attn.own
  26.7 0.0 copy-start.6
  26.7 0.0 copy-start.7
  26.7 7.1 %collective-permute-done.16.refs_1_ = bf16[192,768]{1,0:T(8,128)(2,1)S(1)} collective-permute-done((bf16[192,768]{1,0:T(8,128)(2,1)S(1)}, bf16[192,768]{1,0:T(8,128)(2,1)S(1)}, u32[]{:S(2)}, u32[]{:S(2)}) %collective-permute-start.16) | collective-permute-done | bytes 294944 | tf_op jit(solution)/shard_map/ppermute | solution.py:25
  33.8 4.5 %collective-permute-done.17.refs_2_ = bf16[192,768]{1,0:T(8,128)(2,1)S(1)} collective-permute-done((bf16[192,768]{1,0:T(8,128)(2,1)S(1)}, bf16[192,768]{1,0:T(8,128)(2,1)S(1)}, u32[]{:S(2)}, u32[]{:S(2)}) %collective-permute-start.17) | collective-permute-done | bytes 294944 | tf_op jit(solution)/shard_map/ppermute | solution.py:25
  38.3 0.1 collective-permute-done.18.refs_3_
  38.4 0.6 shard_map.128.mine
  39.0 0.1 collective-permute-start.19
  39.2 0.6 shard_map.120
  39.8 0.1 collective-permute-start.4
  39.9 0.0 copy-start.8
  39.9 4.2 %all-to-all-start = ((bf16[8,64,768]{2,1,0:T(8,128)(2,1)}), bf16[8,64,768]{2,1,0:T(8,128)(2,1)}, u32[]{:S(2)}, u32[]{:S(2)}) async-start(bf16[8,64,768]{2,1,0:T(8,128)(2,1)} %get-tuple-element.30), calls=%async_computation | async-start | bytes 1572864 | tf_op jit(solution)/shard_map/all_to_all | solution.py:430
  44.1 5.1 %collective-permute-start.3 = (bf16[192,128]{1,0:T(8,128)(2,1)S(1)}, bf16[192,128]{1,0:T(8,128)(2,1)S(1)}, u32[]{:S(2)}, u32[]{:S(2)}) collective-permute-start(bf16[192,128]{1,0:T(8,128)(2,1)S(1)} %get-tuple-element.33), channel_id=1, source_target_pairs={{0,1},{1,0},{2,3},{3,2},{4,5},{5,4},{6,7},{7,6},{8,9},{9,8},{10,11... | collective-permute-start | bytes 147464 | tf_op jit(solution)/shard_map/ppermute | solution.py:25
  49.2 0.0 collective-permute-start.5
  49.2 4.1 %collective-permute-done.3.neighbour = bf16[192,128]{1,0:T(8,128)(2,1)S(1)} collective-permute-done((bf16[192,128]{1,0:T(8,128)(2,1)S(1)}, bf16[192,128]{1,0:T(8,128)(2,1)S(1)}, u32[]{:S(2)}, u32[]{:S(2)}) %collective-permute-start.3) | collective-permute-done | bytes 49184 | tf_op jit(solution)/shard_map/ppermute | solution.py:25
  53.3 1.8 %collective-permute-done.5.third = bf16[192,128]{1,0:T(8,128)(2,1)S(1)} collective-permute-done((bf16[192,128]{1,0:T(8,128)(2,1)S(1)}, bf16[192,128]{1,0:T(8,128)(2,1)S(1)}, u32[]{:S(2)}, u32[]{:S(2)}) %collective-permute-start.5) | collective-permute-done | bytes 49184 | tf_op jit(solution)/shard_map/ppermute | solution.py:25
  55.1 0.0 collective-permute-done.4.opposite
  55.1 0.6 shard_map.121.refs_0_
  55.7 2.8 %collective-permute-start.6 = (bf16[1152,128]{1,0:T(8,128)(2,1)S(1)}, bf16[1152,128]{1,0:T(8,128)(2,1)S(1)}, u32[]{:S(2)}, u32[]{:S(2)}) collective-permute-start(bf16[1152,128]{1,0:T(8,128)(2,1)S(1)} %shard_map.121.refs_0_), channel_id=1, source_target_pairs={{0,24},{4,28},{8,16},{12,20},{16,8},{20,12},{24,0},{28,4},{1,25},{... | collective-permute-start | bytes 884744 | tf_op jit(solution)/shard_map/ppermute | solution.py:25
  58.5 0.6 collective-permute-start.7
  59.1 0.2 collective-permute-start.8
  59.3 0.0 collective-permute-start.9
  59.3 7.3 %collective-permute-done.6.refs_1_ = bf16[1152,128]{1,0:T(8,128)(2,1)S(1)} collective-permute-done((bf16[1152,128]{1,0:T(8,128)(2,1)S(1)}, bf16[1152,128]{1,0:T(8,128)(2,1)S(1)}, u32[]{:S(2)}, u32[]{:S(2)}) %collective-permute-start.6) | collective-permute-done | bytes 294944 | tf_op jit(solution)/shard_map/ppermute | solution.py:25
  66.6 4.5 %collective-permute-done.7.refs_2_ = bf16[1152,128]{1,0:T(8,128)(2,1)} collective-permute-done((bf16[1152,128]{1,0:T(8,128)(2,1)S(1)}, bf16[1152,128]{1,0:T(8,128)(2,1)}, u32[]{:S(2)}, u32[]{:S(2)}) %collective-permute-start.7) | collective-permute-done | bytes 294944 | tf_op jit(solution)/shard_map/ppermute | solution.py:25
  71.1 0.0 collective-permute-start.11
  71.1 0.0 collective-permute-done.8.refs_3_
  71.1 0.5 collective-permute-start.12
  71.7 1.5 %shard_map.119 = (bf16[64,768]{1,0:T(8,128)(2,1)S(1)}, bf16[64,768]{1,0:T(8,128)(2,1)S(1)}) custom-call(s32[2]{0:T(128)S(1)} %pad_add_fusion.where, s32[2]{0:T(128)S(1)} %get-tuple-element.29.senders, bf16[8,64,768]{2,1,0:T(8,128)(2,1)} %all-to-all-done.incoming), custom_call_target="tpu_custom_call" | custom-call | tf_op jit(solution)/shard_map/pallas_call | solution.py:133
  73.2 0.0 collective-permute-done.9.refs_4_
  73.2 0.8 collective-permute-start
  74.0 1.9 %collective-permute-start.1 = (bf16[64,768]{1,0:T(8,128)(2,1)S(1)}, bf16[64,768]{1,0:T(8,128)(2,1)S(1)}, u32[]{:S(2)}, u32[]{:S(2)}) collective-permute-start(bf16[64,768]{1,0:T(8,128)(2,1)S(1)} %get-tuple-element.31.kept), channel_id=1, source_target_pairs={{0,1},{1,0},{2,3},{3,2},{4,5},{5,4},{6,7},{7,6},{8,9},{9,8},{10,11... | collective-permute-start | bytes 294920 | tf_op jit(solution)/shard_map/ppermute | solution.py:25
  75.9 2.1 %collective-permute-start.2 = (bf16[64,768]{1,0:T(8,128)(2,1)S(1)}, bf16[64,768]{1,0:T(8,128)(2,1)S(1)}, u32[]{:S(2)}, u32[]{:S(2)}) collective-permute-start(bf16[64,768]{1,0:T(8,128)(2,1)S(1)} %get-tuple-element.32), channel_id=1, source_target_pairs={{0,3},{1,2},{2,1},{3,0},{4,7},{5,6},{6,5},{7,4},{8,11},{9,10},{10,... | collective-permute-start | bytes 294920 | tf_op jit(solution)/shard_map/ppermute | solution.py:25
  78.1 1.7 %shard_map.122 = (bf16[768,1024]{1,0:T(8,128)(2,1)S(1)}, bf16[768,768]{1,0:T(8,128)(2,1)S(1)}) custom-call(s32[2]{0:T(128)S(1)} %pad_add_fusion.where, bf16[192,1024]{1,0:T(8,128)(2,1)S(1)} %pad_maximum_fusion.1.embed, bf16[1152,128]{1,0:T(8,128)(2,1)S(1)} %shard_map.121.refs_0_, bf16[1152,128]{1,0:T(8,128)(2,1)S(1)} %collective-permute-done.6.refs_1_, ...), custom_call_target="tpu_custom_call" | custom-call | tf_op jit(solution)/shard_map/pallas_call | solution.py:41
  79.8 0.0 collective-permute-done.12.refs_1_
  79.8 1.2 %shard_map.123 = (bf16[768,1024]{1,0:T(8,128)(2,1)S(1)}, bf16[768,768]{1,0:T(8,128)(2,1)S(1)}) custom-call(s32[2]{0:T(128)S(1)} %pad_add_fusion.where, bf16[768,1024]{1,0:T(8,128)(2,1)S(1)} %get-tuple-element.35.embed_in, bf16[768,768]{1,0:T(8,128)(2,1)S(1)} %get-tuple-element.36.attn_in, ...), custom_call_target="tpu_custom_call", output_to_operand_aliasing={{0}: (1, {}), {1}: (2, {})} | custom-call | tf_op jit(solution)/shard_map/pallas_call | solution.py:41
  81.1 4.1 %collective-permute-done.2.third = bf16[64,768]{1,0:T(8,128)(2,1)S(1)} collective-permute-done((bf16[64,768]{1,0:T(8,128)(2,1)S(1)}, bf16[64,768]{1,0:T(8,128)(2,1)S(1)}, u32[]{:S(2)}, u32[]{:S(2)}) %collective-permute-start.2) | collective-permute-done | bytes 98336 | tf_op jit(solution)/shard_map/ppermute | solution.py:25
  85.2 3.9 %shard_map.124 = (bf16[576,256]{1,0:T(8,128)(2,1)S(1)}, bf16[576,256]{1,0:T(8,128)(2,1)S(1)}, bf16[128,768]{1,0:T(8,128)(2,1)S(1)}, bf16[128,768]{1,0:T(8,128)(2,1)S(1)}) custom-call(s32[2]{0:T(128)S(1)} %pad_add_fusion.where, bf16[64,768]{1,0:T(8,128)(2,1)S(1)} %get-tuple-element.31.kept, bf16[64,768]{1,0:T(8,128)(2,1)S(1)} %collective-permute-done.opposite, ...), custom_call_target="tpu_custom_call" | custom-call | tf_op jit(solution)/shard_map/pallas_call | solution.py:317
  89.2 0.1 collective-permute-start.13
  89.3 2.0 %shard_map.125 = (f32[128,768]{1,0:T(8,128)S(1)}, bf16[768,768]{1,0:T(8,128)(2,1)S(1)}, bf16[768,768]{1,0:T(8,128)(2,1)S(1)}) custom-call(bf16[576,256]{1,0:T(8,128)(2,1)S(1)} %get-tuple-element.39.own_qkv, bf16[576,256]{1,0:T(8,128)(2,1)S(1)} %get-tuple-element.40.far_qkv, bf16[128,768]{1,0:T(8,128)(2,1)S(1)} %get-tuple-element.41.embedded, ...), custom_call_target="tpu_custom_call" | custom-call | tf_op jit(solution)/shard_map/pallas_call | solution.py:329
  91.2 4.1 %collective-permute-done.13.other = bf16[128,768]{1,0:T(8,128)(2,1)S(1)} collective-permute-done((bf16[128,768]{1,0:T(8,128)(2,1)S(1)}, bf16[128,768]{1,0:T(8,128)(2,1)S(1)}, u32[]{:S(2)}, u32[]{:S(2)}) %collective-permute-start.13) | collective-permute-done | bytes 196640 | tf_op jit(solution)/shard_map/ppermute | solution.py:25
  95.4 0.2 shard_map.127
  95.6 0.4 collective-permute-start.14
  96.0 0.6 shard_map.131.part
  96.6 1.4 %shard_map.129 = (bf16[768,768]{1,0:T(8,128)(2,1)S(1)}, bf16[768,768]{1,0:T(8,128)(2,1)S(1)}) custom-call(s32[2]{0:T(128)S(1)} %pad_add_fusion.where, bf16[768,768]{1,0:T(8,128)(2,1)S(1)} %shard_map.128.mine, bf16[768,768]{1,0:T(8,128)(2,1)} %collective-permute-done.19.others), custom_call_target="tpu_custom_call" | custom-call | tf_op jit(solution)/shard_map/pallas_call | solution.py:41
  98.0 0.6 shard_map.132
  98.7 3.2 %collective-permute-start.21 = (bf16[64,768]{1,0:T(8,128)(2,1)S(1)}, bf16[64,768]{1,0:T(8,128)(2,1)S(1)}, u32[]{:S(2)}, u32[]{:S(2)}) collective-permute-start(bf16[64,768]{1,0:T(8,128)(2,1)S(1)} %fusion.2), channel_id=1, source_target_pairs={{0,3},{1,2},{2,1},{3,0},{4,7},{5,6},{6,5},{7,4},{8,11},{9,10},{10,... | collective-permute-start | bytes 294920 | tf_op jit(solution)/shard_map/ppermute | solution.py:25
  101.9 1.0 shard_map.130
  102.9 3.0 %collective-permute-start.20 = (bf16[64,768]{1,0:T(8,128)(2,1)S(1)}, bf16[64,768]{1,0:T(8,128)(2,1)S(1)}, u32[]{:S(2)}, u32[]{:S(2)}) collective-permute-start(bf16[64,768]{1,0:T(8,128)(2,1)S(1)} %get-tuple-element.50), channel_id=1, source_target_pairs={{0,2},{1,3},{2,0},{3,1},{4,6},{5,7},{6,4},{7,5},{8,10},{9,11},{10,... | collective-permute-start | bytes 294920 | tf_op jit(solution)/shard_map/ppermute | solution.py:25
  106.0 0.5 collective-permute-done.21
  106.5 3.5 %collective-permute-done.20 = bf16[64,768]{1,0:T(8,128)(2,1)S(1)} collective-permute-done((bf16[64,768]{1,0:T(8,128)(2,1)S(1)}, bf16[64,768]{1,0:T(8,128)(2,1)S(1)}, u32[]{:S(2)}, u32[]{:S(2)}) %collective-permute-start.20) | collective-permute-done | bytes 98336 | tf_op jit(solution)/shard_map/ppermute | solution.py:25
  110.0 1.1 collective-permute-done.22
  111.0 0.1 select_bitcast_fusion.1
  111.1 0.7 pad_maximum_fusion.2
  (28 shorter events, 0.2 us)
Async XLA Ops:
  0.0 1.1 %copy-start = (bf16[8,64,768]{2,1,0:T(8,128)(2,1)S(1)}, bf16[8,64,768]{2,1,0:T(8,128)(2,1)}, u32[]{:S(2)}) copy-start(bf16[8,64,768]{2,1,0:T(8,128)(2,1)} %candidates.1) | copy-start | bytes 2359300
  1.1 0.7 copy-start.1
  1.8 0.7 copy-start.2
  2.4 0.7 copy-start.3
  3.1 23.5 %copy-start.4 = (bf16[768,3,192]{0,2,1:T(8,128)(2,1)S(1)}, bf16[768,3,192]{0,2,1:T(8,128)(2,1)}, u32[]{:S(2)}) copy-start(bf16[768,3,192]{0,2,1:T(8,128)(2,1)} %param.18) | copy-start | bytes 2654212
  3.1 23.5 %copy-start.5 = (bf16[192,768]{1,0:T(8,128)(2,1)S(1)}, bf16[192,768]{1,0:T(8,128)(2,1)}, u32[]{:S(2)}) copy-start(bf16[192,768]{1,0:T(8,128)(2,1)} %param.19) | copy-start | bytes 884740
  5.6 17.5 %collective-permute-start.15 = (bf16[192,768]{1,0:T(8,128)(2,1)S(1)}, bf16[192,768]{1,0:T(8,128)(2,1)S(1)}, u32[]{:S(2)}, u32[]{:S(2)}) collective-permute-start(bf16[192,768]{1,0:T(8,128)(2,1)S(1)} %get-tuple-element.45), channel_id=1, source_target_pairs={{0,2},{1,3},{2,0},{3,1},{4,6},{5,7},{6,4},{7,5},{8,10},{9,11},{10,... | collective-permute-start | bytes 884744 | tf_op jit(solution)/shard_map/ppermute | solution.py:25
  23.0 10.8 %collective-permute-start.16 = (bf16[192,768]{1,0:T(8,128)(2,1)S(1)}, bf16[192,768]{1,0:T(8,128)(2,1)S(1)}, u32[]{:S(2)}, u32[]{:S(2)}) collective-permute-start(bf16[192,768]{1,0:T(8,128)(2,1)S(1)} %collective-permute-done.15.refs_0_), channel_id=1, source_target_pairs={{0,24},{4,28},{8,16},{12,20},{16,8},{20,12},{24,0},{28,4},{1,25},{... | collective-permute-start | bytes 884744 | tf_op jit(solution)/shard_map/ppermute | solution.py:25
  25.5 12.8 %collective-permute-start.17 = (bf16[192,768]{1,0:T(8,128)(2,1)S(1)}, bf16[192,768]{1,0:T(8,128)(2,1)S(1)}, u32[]{:S(2)}, u32[]{:S(2)}) collective-permute-start(bf16[192,768]{1,0:T(8,128)(2,1)S(1)} %collective-permute-done.15.refs_0_), channel_id=1, source_target_pairs={{0,8},{4,12},{8,0},{12,4},{16,24},{20,28},{24,16},{28,20},{1,9},{5... | collective-permute-start | bytes 884744 | tf_op jit(solution)/shard_map/ppermute | solution.py:25
  26.1 12.4 %collective-permute-start.18 = (bf16[192,768]{1,0:T(8,128)(2,1)S(1)}, bf16[192,768]{1,0:T(8,128)(2,1)S(1)}, u32[]{:S(2)}, u32[]{:S(2)}) collective-permute-start(bf16[192,768]{1,0:T(8,128)(2,1)S(1)} %collective-permute-done.15.refs_0_), channel_id=1, source_target_pairs={{0,16},{4,20},{8,24},{12,28},{16,0},{20,4},{24,8},{28,12},{1,17},{... | collective-permute-start | bytes 884744 | tf_op jit(solution)/shard_map/ppermute | solution.py:25
  26.7 12.4 %copy-start.6 = (bf16[768,192]{0,1:T(8,128)(2,1)S(1)}, bf16[768,192]{0,1:T(8,128)(2,1)}, u32[]{:S(2)}) copy-start(bf16[768,192]{0,1:T(8,128)(2,1)} %param.16) | copy-start | bytes 884740
  26.7 12.4 %copy-start.7 = (bf16[256,192]{0,1:T(8,128)(2,1)S(1)}, bf16[256,192]{0,1:T(8,128)(2,1)}, u32[]{:S(2)}) copy-start(bf16[256,192]{0,1:T(8,128)(2,1)} %param.17) | copy-start | bytes 294916
  39.0 57.5 %collective-permute-start.19 = (bf16[768,768]{1,0:T(8,128)(2,1)S(1)}, bf16[768,768]{1,0:T(8,128)(2,1)}, u32[]{:S(2)}, u32[]{:S(2)}) collective-permute-start(bf16[768,768]{1,0:T(8,128)(2,1)S(1)} %shard_map.128.mine), channel_id=1, source_target_pairs={{0,4},{4,0},{8,12},{12,8},{16,20},{20,16},{24,28},{28,24},{1,5},{5... | collective-permute-start | bytes 3538952 | tf_op jit(solution)/shard_map/ppermute | solution.py:25
  39.8 15.3 %collective-permute-start.4 = (bf16[768,128]{1,0:T(8,128)(2,1)S(1)}, bf16[768,128]{1,0:T(8,128)(2,1)S(1)}, u32[]{:S(2)}, u32[]{:S(2)}) collective-permute-start(bf16[768,128]{1,0:T(8,128)(2,1)S(1)} %get-tuple-element.34), channel_id=1, source_target_pairs={{0,2},{1,3},{2,0},{3,1},{4,6},{5,7},{6,4},{7,5},{8,10},{9,11},{10,... | collective-permute-start | bytes 589832 | tf_op jit(solution)/shard_map/ppermute | solution.py:25
  39.9 38.2 %copy-start.8 = (bf16[768]{0:T(1024)(128)(2,1)S(1)}, bf16[768]{0:T(1024)(128)(2,1)}, u32[]{:S(2)}) copy-start(bf16[768]{0:T(1024)(128)(2,1)} %param.20) | copy-start | bytes 4612
  39.9 31.8 %all-to-all-start = ((bf16[8,64,768]{2,1,0:T(8,128)(2,1)}), bf16[8,64,768]{2,1,0:T(8,128)(2,1)}, u32[]{:S(2)}, u32[]{:S(2)}) async-start(bf16[8,64,768]{2,1,0:T(8,128)(2,1)} %get-tuple-element.30), calls=%async_computation | async-start | bytes 1572864 | tf_op jit(solution)/shard_map/all_to_all | solution.py:430
  44.1 9.2 %collective-permute-start.3 = (bf16[192,128]{1,0:T(8,128)(2,1)S(1)}, bf16[192,128]{1,0:T(8,128)(2,1)S(1)}, u32[]{:S(2)}, u32[]{:S(2)}) collective-permute-start(bf16[192,128]{1,0:T(8,128)(2,1)S(1)} %get-tuple-element.33), channel_id=1, source_target_pairs={{0,1},{1,0},{2,3},{3,2},{4,5},{5,4},{6,7},{7,6},{8,9},{9,8},{10,11... | collective-permute-start | bytes 147464 | tf_op jit(solution)/shard_map/ppermute | solution.py:25
  49.2 5.9 %collective-permute-start.5 = (bf16[192,128]{1,0:T(8,128)(2,1)S(1)}, bf16[192,128]{1,0:T(8,128)(2,1)S(1)}, u32[]{:S(2)}, u32[]{:S(2)}) collective-permute-start(bf16[192,128]{1,0:T(8,128)(2,1)S(1)} %get-tuple-element.33), channel_id=1, source_target_pairs={{0,3},{1,2},{2,1},{3,0},{4,7},{5,6},{6,5},{7,4},{8,11},{9,10},{10,... | collective-permute-start | bytes 147464 | tf_op jit(solution)/shard_map/ppermute | solution.py:25
  55.7 10.9 %collective-permute-start.6 = (bf16[1152,128]{1,0:T(8,128)(2,1)S(1)}, bf16[1152,128]{1,0:T(8,128)(2,1)S(1)}, u32[]{:S(2)}, u32[]{:S(2)}) collective-permute-start(bf16[1152,128]{1,0:T(8,128)(2,1)S(1)} %shard_map.121.refs_0_), channel_id=1, source_target_pairs={{0,24},{4,28},{8,16},{12,20},{16,8},{20,12},{24,0},{28,4},{1,25},{... | collective-permute-start | bytes 884744 | tf_op jit(solution)/shard_map/ppermute | solution.py:25
  58.5 12.6 %collective-permute-start.7 = (bf16[1152,128]{1,0:T(8,128)(2,1)S(1)}, bf16[1152,128]{1,0:T(8,128)(2,1)}, u32[]{:S(2)}, u32[]{:S(2)}) collective-permute-start(bf16[1152,128]{1,0:T(8,128)(2,1)S(1)} %shard_map.121.refs_0_), channel_id=1, source_target_pairs={{0,8},{4,12},{8,0},{12,4},{16,24},{20,28},{24,16},{28,20},{1,9},{5... | collective-permute-start | bytes 884744 | tf_op jit(solution)/shard_map/ppermute | solution.py:25
  59.1 12.1 %collective-permute-start.8 = (bf16[1152,128]{1,0:T(8,128)(2,1)S(1)}, bf16[1152,128]{1,0:T(8,128)(2,1)}, u32[]{:S(2)}, u32[]{:S(2)}) collective-permute-start(bf16[1152,128]{1,0:T(8,128)(2,1)S(1)} %shard_map.121.refs_0_), channel_id=1, source_target_pairs={{0,16},{4,20},{8,24},{12,28},{16,0},{20,4},{24,8},{28,12},{1,17},{... | collective-permute-start | bytes 884744 | tf_op jit(solution)/shard_map/ppermute | solution.py:25
  59.3 13.9 %collective-permute-start.9 = (bf16[1152,128]{1,0:T(8,128)(2,1)S(1)}, bf16[1152,128]{1,0:T(8,128)(2,1)}, u32[]{:S(2)}, u32[]{:S(2)}) collective-permute-start(bf16[1152,128]{1,0:T(8,128)(2,1)S(1)} %shard_map.121.refs_0_), channel_id=1, source_target_pairs={{0,4},{4,0},{8,12},{12,8},{16,20},{20,16},{24,28},{28,24},{1,5},{5... | collective-permute-start | bytes 884744 | tf_op jit(solution)/shard_map/ppermute | solution.py:25
  66.6 7.4 %collective-permute-start.10 = (bf16[1152,128]{1,0:T(8,128)(2,1)S(1)}, bf16[1152,128]{1,0:T(8,128)(2,1)}, u32[]{:S(2)}, u32[]{:S(2)}) collective-permute-start(bf16[1152,128]{1,0:T(8,128)(2,1)S(1)} %collective-permute-done.6.refs_1_), channel_id=1, source_target_pairs={{0,4},{4,0},{8,12},{12,8},{16,20},{20,16},{24,28},{28,24},{1,5},{5... | collective-permute-start | bytes 884744 | tf_op jit(solution)/shard_map/ppermute | solution.py:25
  71.1 4.8 %collective-permute-start.11 = (bf16[1152,128]{1,0:T(8,128)(2,1)}, bf16[1152,128]{1,0:T(8,128)(2,1)}, u32[]{:S(2)}, u32[]{:S(2)}) collective-permute-start(bf16[1152,128]{1,0:T(8,128)(2,1)} %collective-permute-done.7.refs_2_), channel_id=1, source_target_pairs={{0,4},{4,0},{8,12},{12,8},{16,20},{20,16},{24,28},{28,24},{1,5},{5... | collective-permute-start | bytes 884744 | tf_op jit(solution)/shard_map/ppermute | solution.py:25
  71.1 8.7 %collective-permute-start.12 = (bf16[1152,128]{1,0:T(8,128)(2,1)}, bf16[1152,128]{1,0:T(8,128)(2,1)}, u32[]{:S(2)}, u32[]{:S(2)}) collective-permute-start(bf16[1152,128]{1,0:T(8,128)(2,1)} %collective-permute-done.8.refs_3_), channel_id=1, source_target_pairs={{0,4},{4,0},{8,12},{12,8},{16,20},{20,16},{24,28},{28,24},{1,5},{5... | collective-permute-start | bytes 884744 | tf_op jit(solution)/shard_map/ppermute | solution.py:25
  73.2 7.9 %collective-permute-start = (bf16[64,768]{1,0:T(8,128)(2,1)S(1)}, bf16[64,768]{1,0:T(8,128)(2,1)S(1)}, u32[]{:S(2)}, u32[]{:S(2)}) collective-permute-start(bf16[64,768]{1,0:T(8,128)(2,1)S(1)} %get-tuple-element.32), channel_id=1, source_target_pairs={{0,2},{1,3},{2,0},{3,1},{4,6},{5,7},{6,4},{7,5},{8,10},{9,11},{10,... | collective-permute-start | bytes 294920 | tf_op jit(solution)/shard_map/ppermute | solution.py:25
  74.0 7.1 %collective-permute-start.1 = (bf16[64,768]{1,0:T(8,128)(2,1)S(1)}, bf16[64,768]{1,0:T(8,128)(2,1)S(1)}, u32[]{:S(2)}, u32[]{:S(2)}) collective-permute-start(bf16[64,768]{1,0:T(8,128)(2,1)S(1)} %get-tuple-element.31.kept), channel_id=1, source_target_pairs={{0,1},{1,0},{2,3},{3,2},{4,5},{5,4},{6,7},{7,6},{8,9},{9,8},{10,11... | collective-permute-start | bytes 294920 | tf_op jit(solution)/shard_map/ppermute | solution.py:25
  75.9 9.3 %collective-permute-start.2 = (bf16[64,768]{1,0:T(8,128)(2,1)S(1)}, bf16[64,768]{1,0:T(8,128)(2,1)S(1)}, u32[]{:S(2)}, u32[]{:S(2)}) collective-permute-start(bf16[64,768]{1,0:T(8,128)(2,1)S(1)} %get-tuple-element.32), channel_id=1, source_target_pairs={{0,3},{1,2},{2,1},{3,0},{4,7},{5,6},{6,5},{7,4},{8,11},{9,10},{10,... | collective-permute-start | bytes 294920 | tf_op jit(solution)/shard_map/ppermute | solution.py:25
  85.2 4.0 %copy-start.9 = (bf16[768]{0:T(1024)(128)(2,1)S(1)}, bf16[768]{0:T(1024)(128)(2,1)}, u32[]{:S(2)}) copy-start(bf16[768]{0:T(1024)(128)(2,1)} %param.21) | copy-start | bytes 4612
  89.2 6.2 %collective-permute-start.13 = (bf16[128,768]{1,0:T(8,128)(2,1)S(1)}, bf16[128,768]{1,0:T(8,128)(2,1)S(1)}, u32[]{:S(2)}, u32[]{:S(2)}) collective-permute-start(bf16[128,768]{1,0:T(8,128)(2,1)S(1)} %get-tuple-element.43), channel_id=1, source_target_pairs={{0,1},{1,0},{2,3},{3,2},{4,5},{5,4},{6,7},{7,6},{8,9},{9,8},{10,11... | collective-permute-start | bytes 589832 | tf_op jit(solution)/shard_map/ppermute | solution.py:25
  95.6 6.3 %collective-permute-start.14 = (bf16[128,768]{1,0:T(8,128)(2,1)S(1)}, bf16[128,768]{1,0:T(8,128)(2,1)S(1)}, u32[]{:S(2)}, u32[]{:S(2)}) collective-permute-start(bf16[128,768]{1,0:T(8,128)(2,1)S(1)} %get-tuple-element.44.normed), channel_id=1, source_target_pairs={{0,1},{1,0},{2,3},{3,2},{4,5},{5,4},{6,7},{7,6},{8,9},{9,8},{10,11... | collective-permute-start | bytes 589832 | tf_op jit(solution)/shard_map/ppermute | solution.py:25
  98.7 7.8 %collective-permute-start.21 = (bf16[64,768]{1,0:T(8,128)(2,1)S(1)}, bf16[64,768]{1,0:T(8,128)(2,1)S(1)}, u32[]{:S(2)}, u32[]{:S(2)}) collective-permute-start(bf16[64,768]{1,0:T(8,128)(2,1)S(1)} %fusion.2), channel_id=1, source_target_pairs={{0,3},{1,2},{2,1},{3,0},{4,7},{5,6},{6,5},{7,4},{8,11},{9,10},{10,... | collective-permute-start | bytes 294920 | tf_op jit(solution)/shard_map/ppermute | solution.py:25
  102.9 7.0 %collective-permute-start.20 = (bf16[64,768]{1,0:T(8,128)(2,1)S(1)}, bf16[64,768]{1,0:T(8,128)(2,1)S(1)}, u32[]{:S(2)}, u32[]{:S(2)}) collective-permute-start(bf16[64,768]{1,0:T(8,128)(2,1)S(1)} %get-tuple-element.50), channel_id=1, source_target_pairs={{0,2},{1,3},{2,0},{3,1},{4,6},{5,7},{6,4},{7,5},{8,10},{9,11},{10,... | collective-permute-start | bytes 294920 | tf_op jit(solution)/shard_map/ppermute | solution.py:25
  106.0 5.1 %collective-permute-start.22 = (bf16[64,768]{1,0:T(8,128)(2,1)S(1)}, bf16[64,768]{1,0:T(8,128)(2,1)S(1)}, u32[]{:S(2)}, u32[]{:S(2)}) collective-permute-start(bf16[64,768]{1,0:T(8,128)(2,1)S(1)} %get-tuple-element.52), channel_id=1, source_target_pairs={{0,1},{1,0},{2,3},{3,2},{4,5},{5,4},{6,7},{7,6},{8,9},{9,8},{10,11... | collective-permute-start | bytes 294920 | tf_op jit(solution)/shard_map/ppermute | solution.py:25
